TPU v7x, 32 devices: a 4x2x2 block of a 4x4x8 slice. The times are simulated.
32 devices in a mesh: dp: 4 (over y, z), tp: 8 (over x, core).
Axes of the slice: x: 4, y: 2, z: 2, core: 2. Of those that a mesh axis runs over, the one named last changes fastest.
The devices are a block of a 4x4x8 slice.
Arguments:
- enc_out: bfloat16 [48, 512, 2048], P('dp', 'tp'), parts along dimension 0
- norm_scale: bfloat16 [2048], replicated
- w_key: bfloat16 [6, 2048, 32, 64], P(None, None, 'tp')
- w_value: bfloat16 [6, 2048, 32, 64], P(None, None, 'tp')
Outputs:
- output 1: bfloat16 [6, 48, 512, 32, 64], P(None, 'dp', None, 'tp'), parts along dimension 1
- output 2: bfloat16 [6, 48, 512, 32, 64], P(None, 'dp', None, 'tp'), parts along dimension 1
There are 4 independent parts. A program takes and returns all parts, laid end to end along the dimension named above; an argument that names none is the same for every part.
All inputs are finite; a program needn't handle non-finite values.
Results may differ from a plain program's by a relative error of at most 0.001.
Values are sent between devices in bfloat16 or wider.
A program may use at most 768 MiB of HBM per device.

v0:
```python
import jax
import jax.numpy as jnp
from jax import lax
from jax.sharding import PartitionSpec as P

NORM_EPS = 1e-6


def rms_norm(enc_out, norm_scale):
    acts = enc_out.astype(jnp.float32)
    mean_sq = jnp.mean(acts * acts, axis=-1, keepdims=True)
    return (acts * lax.rsqrt(mean_sq + NORM_EPS) * norm_scale.astype(jnp.float32)).astype(jnp.bfloat16)


def solution(mesh):
    def per_device(enc_out, norm_scale, w_key, w_value):
        normed = rms_norm(enc_out, norm_scale)
        gathered = lax.all_gather(normed, "tp", axis=1, tiled=True)
        key_cache = jnp.einsum("bsd,ldhk->lbshk", gathered, w_key, preferred_element_type=jnp.float32).astype(jnp.bfloat16)
        value_cache = jnp.einsum("bsd,ldhk->lbshk", gathered, w_value, preferred_element_type=jnp.float32).astype(jnp.bfloat16)
        return key_cache, value_cache

    weight_spec = P(None, None, "tp", None)
    cache_spec = P(None, "dp", None, "tp", None)
    return jax.shard_map(per_device, mesh=mesh, in_specs=(P("dp", "tp", None), P(None), weight_spec, weight_spec), out_specs=(cache_spec, cache_spec), check_vma=False)
```

profile of v0, /device:TPU:81, one launch (start us, length us, event | category | flops | bytes accessed | tf_op | source)
XLA Modules:
  0.0 246.3 jit_solution(16783113904916904372)
XLA Ops:
  7.2 0.1 all-gather.2.cloned.1.call-start
  7.2 0.7 convert_element_type.22
  7.9 2.6 %fusion.8 = f32[12,64]{1,0:T(8,128)S(1)} fusion(bf16[12,64,2048]{2,1,0:T(8,128)(2,1)} %param.4), kind=kLoop, calls=%fused_computation.8 | loop fusion | flops 4717824 | bytes 3148800 | tf_op jit(solution)/shard_map/reduce_sum | solution.py:11
  10.5 4.3 %fusion.10 = bf16[12,64,2048]{2,1,0:T(8,128)(2,1)} fusion(bf16[12,64,2048]{2,1,0:T(8,128)(2,1)} %param.4, f32[2048]{0:T(1024)S(1)} %convert_element_type.22, f32[12,64]{1,0:T(8,128)S(1)} %add_rsqrt_fusion), kind=kLoop, calls=%fused_computation.10 | loop fusion | flops 6291456 | bytes 6302720 | tf_op jit(solution)/shard_map/convert_element_type | solution.py:12
  14.9 0.1 all-gather.2.cloned.1.call-update
  14.9 122.4 %all-gather.2.cloned.1.call-done = bf16[12,512,2048]{2,1,0:T(8,128)(2,1)} async-done(((bf16[12,64,2048]{2,1,0:T(8,128)(2,1)}), bf16[12,512,2048]{2,1,0:T(8,128)(2,1)}) %all-gather.2.cloned.1.call-update) | async-done | bytes 25165840 | tf_op jit(solution)/shard_map/all_gather | solution.py:18
  137.4 44.6 %convert_bitcast_fusion.1 = bf16[6,12,512,4,64]{2,4,3,0,1:T(8,128)(2,1)S(1)} fusion(bf16[12,512,2048]{2,1,0:T(8,128)(2,1)} %all-gather.2.cloned.1.call-done, bf16[6,2048,4,64]{1,3,2,0:T(8,128)(2,1)} %param.6), kind=kOutput, calls=%fused_computation.5 | convolution fusion | flops 38664142848 | bytes 50331648 | tf_op jit(solution)/shard_map/bsd,ldhk->lbshk/dot_general | solution.py:19
  182.0 0.0 copy-start
  182.0 8.0 %copy.6 = bf16[6,12,512,4,64]{2,4,3,1,0:T(8,128)(2,1)} copy(bf16[6,12,512,4,64]{2,4,3,0,1:T(8,128)(2,1)S(1)} %convert_bitcast_fusion.1) | data formatting | bytes 37748736
  189.9 0.0 copy-done
  189.9 42.8 %convert_bitcast_fusion = bf16[6,12,512,4,64]{2,4,3,0,1:T(8,128)(2,1)S(1)} fusion(bf16[12,512,2048]{2,1,0:T(8,128)(2,1)} %all-gather.2.cloned.1.call-done, bf16[6,2048,4,64]{1,3,2,0:T(8,128)(2,1)S(1)} %copy-done), kind=kOutput, calls=%fused_computation.4 | convolution fusion | flops 38664142848 | bytes 50331648 | tf_op jit(solution)/shard_map/bsd,ldhk->lbshk/dot_general | solution.py:20
  232.7 6.7 %copy.7 = bf16[6,12,512,4,64]{2,4,3,1,0:T(8,128)(2,1)} copy(bf16[6,12,512,4,64]{2,4,3,0,1:T(8,128)(2,1)S(1)} %convert_bitcast_fusion) | data formatting | bytes 37748736
  (1 shorter events, 0.0 us)
Async XLA Ops:
  7.2 130.2 %all-gather.2.cloned.1.call-start = ((), (), s32[]{:S(2)}) async-start(), calls=%async_computation | async-start | bytes 28311552 | tf_op jit(solution)/shard_map/all_gather | solution.py:18
  182.0 8.0 %copy-start = (bf16[6,2048,4,64]{1,3,2,0:T(8,128)(2,1)S(1)}, bf16[6,2048,4,64]{1,3,2,0:T(8,128)(2,1)}, u32[]{:S(2)}) copy-start(bf16[6,2048,4,64]{1,3,2,0:T(8,128)(2,1)} %param.7) | copy-start | bytes 18874372
Sparse Core Ops, SparseCore 0:
  15.1 122.2 all-gather.1
where the time goes:
time: 246 us
  waiting for transfers between devices  122 us (50%)
  matrix products  87.4 us (36%)
  local copies, waits for them, and re-layouts  14.7 us (6%)
  between operations  14.1 us (6%)
  other arithmetic  7.62 us (3%)
    all_gather x1, waiting for transfers between devices, per_device(): gathered = lax.all_gather(normed, 'tp', axis=1, tiled=True)  122 us
    dot_general x1, matrix products, per_device(): jnp.einsum('bsd,ldhk->lbshk', gathered, w_key, preferred_element_type=jnp...  44.6 us
    dot_general x1, matrix products, per_device(): jnp.einsum('bsd,ldhk->lbshk', gathered, w_value, preferred_element_type=j...  42.8 us
    unnamed x4, local copies, waits for them, and re-layouts  14.7 us
  transfers between devices with their start and end apart: 1, of which 1 were waited for; matrix products, arithmetic and copies ran while one was open for 0% of the time, Pallas kernels for 0%

commit v1 on v0

v1 whole, which is shorter than its diff:
```python
import functools

import jax
import jax.numpy as jnp
from jax import lax
from jax.experimental import pallas as pl
from jax.experimental.pallas import tpu as pltpu
from jax.sharding import PartitionSpec as P


NORM_EPS = 1e-6
PIECE = 2
ANY = pl.BlockSpec(memory_space=pl.ANY)
VMEM = pl.BlockSpec(memory_space=pltpu.VMEM)
NT = (((1,), (1,)), ((), ()))
MESH = pl.DeviceIdType.MESH


def in_hbm(x):
    return pltpu.with_memory_space_constraint(x, pltpu.HBM)


def rms_norm(x, scale):
    acts = x.astype(jnp.float32)
    mean_sq = jnp.mean(acts * acts, axis=-1, keepdims=True)
    return (acts * lax.rsqrt(mean_sq + NORM_EPS) * scale).astype(jnp.bfloat16)


def prep_kernel(slots, n_slots, n_weights, x_ref, scale_ref, *refs):
    w_in, refs = refs[:n_weights], refs[n_weights:]
    outs, refs = refs[:len(slots)], refs[len(slots):]
    w_out, (xbuf, ybuf, scale_buf, in_sem, w_sem, send_sem, recv_sem) = refs[:n_weights], refs[n_weights:]
    half = x_ref.shape[1]
    me = lax.axis_index("tp")
    core = lax.rem(me, 2)
    other = me + 1 - 2 * core
    rows = pl.ds(pl.multiple_of(core * half, half), half)
    shift = n_slots // 2
    needed = [i for i in range(n_slots) if i in slots or (i + shift) % n_slots in slots]

    barrier = pltpu.get_barrier_semaphore()
    pl.semaphore_signal(barrier, inc=1, device_id={"tp": other}, device_id_type=MESH)

    def load(j):
        first = lax.rem(needed[j] + shift * core, n_slots) * PIECE
        return pltpu.make_async_copy(x_ref.at[pl.ds(first, PIECE)], xbuf.at[j], in_sem.at[j])

    def send(j):
        to = slots.index((needed[j] + shift) % n_slots)
        return pltpu.make_async_remote_copy(
            src_ref=ybuf.at[j],
            dst_ref=outs[to].at[:, rows],
            send_sem=send_sem.at[to],
            recv_sem=recv_sem.at[to],
            device_id={"tp": other},
            device_id_type=MESH,
        )

    get_scale = pltpu.make_async_copy(scale_ref, scale_buf, w_sem.at[n_weights])
    get_scale.start()
    for j in range(len(needed)):
        load(j).start()
    weights = [pltpu.make_async_copy(a, b, w_sem.at[i]) for i, (a, b) in enumerate(zip(w_in, w_out))]
    for copy in weights:
        copy.start()
    get_scale.wait()
    scale = scale_buf[...].astype(jnp.float32).reshape(1, -1)
    sent = []
    order = sorted(range(len(needed)), key=lambda j: (needed[j] + shift) % n_slots not in slots)
    pending = None
    pl.semaphore_wait(barrier, 1)
    for j in order:
        load(j).wait()
        y = rms_norm(xbuf[j], scale)
        sends = (needed[j] + shift) % n_slots in slots
        if sends:
            ybuf[j] = y
        if needed[j] in slots:
            outs[slots.index(needed[j])][:, rows] = y
        if pending is not None:
            send(pending).start()
            sent.append(pending)
        pending = j if sends else None
    if pending is not None:
        send(pending).start()
        sent.append(pending)
    for j in sent:
        send(j).wait()
    for copy in weights:
        copy.wait()


def prepare(x, scale, slots, n_slots, weights, collective_id):
    _, half, d = x.shape
    shift = n_slots // 2
    n_needed = len([i for i in range(n_slots) if i in slots or (i + shift) % n_slots in slots])
    piece = jax.ShapeDtypeStruct((PIECE, 2 * half, d), x.dtype)
    out_shape = (piece,) * len(slots) + tuple(jax.ShapeDtypeStruct(w.shape, w.dtype) for w in weights)
    return pl.pallas_call(
        functools.partial(prep_kernel, slots, n_slots, len(weights)),
        out_shape=out_shape,
        in_specs=[ANY, ANY] + [ANY] * len(weights),
        out_specs=(VMEM,) * len(out_shape),
        scratch_shapes=[
            pltpu.VMEM((n_needed, PIECE, half, d), x.dtype),
            pltpu.VMEM((n_needed, PIECE, half, d), x.dtype),
            pltpu.VMEM(scale.shape, scale.dtype),
            pltpu.SemaphoreType.DMA((n_needed,)),
            pltpu.SemaphoreType.DMA((len(weights) + 1,)),
            pltpu.SemaphoreType.DMA((len(slots),)),
            pltpu.SemaphoreType.DMA((len(slots),)),
        ],
        compiler_params=pltpu.CompilerParams(vmem_limit_bytes=32 * 2**20, collective_id=collective_id, has_side_effects=True),
        cost_estimate=pl.CostEstimate(flops=64 * x.size, bytes_accessed=4 * x.size, transcendentals=0),
    )(in_hbm(x), in_hbm(scale), *map(in_hbm, weights))


def project_kernel(plan, n_pieces, n_alias, *refs):
    wk_ref, wv_ref = refs[:2]
    pieces = refs[2:2 + n_pieces]
    ok_ref, ov_ref, stage, sem = refs[2 + n_pieces + n_alias:]
    chips = lax.axis_size("tp") // 2
    me = lax.axis_index("tp")
    core, chip = lax.rem(me, 2), me // 2
    group, d = pieces[0].shape[1:]
    hk = wk_ref.shape[1]
    chunks, _, per = stage.shape[:3]

    def put(i, c):
        copies = []
        at = 0
        for j, (p, on0, on1) in enumerate(plan[i]):
            n = pieces[p].shape[0]
            off, first = (a if a is b else jnp.where(core == 0, a, b) for a, b in zip(on0, on1))
            lanes = pl.ds(pl.multiple_of(lax.rem(chip + off, chips) * group, group), group)
            for kv, out in enumerate((ok_ref, ov_ref)):
                dst = out.at[pl.ds(c * per, per), pl.ds(first, n), :, lanes]
                copies.append(pltpu.make_async_copy(stage.at[c, kv, :, pl.ds(at, n)], dst, sem.at[c, kv, j]))
            at += n
        return copies

    for i, block in enumerate(plan):

        @pl.loop(0, chunks)
        def _(c):
            if i > 0:
                for copy in put(i - 1, c):
                    copy.wait()
            y = jnp.concatenate([pieces[p][...].reshape(-1, d) for p, _, _ in block])
            for kv, w_ref in enumerate((wk_ref, wv_ref)):
                w = w_ref[pl.ds(c * per, per)].reshape(per * hk, d)
                res = lax.dot_general(w, y, NT, preferred_element_type=jnp.float32).astype(jnp.bfloat16)
                for l in range(per):
                    for s in range(y.shape[0] // group):
                        stage[c, kv, l, s] = res[l * hk:(l + 1) * hk, s * group:(s + 1) * group]
            for copy in put(i, c):
                copy.start()

    for c in range(chunks):
        for copy in put(len(plan) - 1, c):
            copy.wait()


def project(wk, wv, blocks, out, batch, tp):
    layers, hk, d = wk.shape
    pieces, plan = [], []
    for block in blocks:
        plan.append(tuple((len(pieces) + j, *where) for j, (_, *where) in enumerate(block)))
        pieces += [piece for piece, *_ in block]
    group = pieces[0].shape[1]
    shape = jax.ShapeDtypeStruct((layers, batch, hk, group * tp // 2), wk.dtype)
    n_alias = 0 if out is None else 2
    n_in = 2 + len(pieces)
    per = 2
    tok = sum(p.shape[0] for p in pieces) * group
    seqs = sum(p.shape[0] for p, *_ in blocks[0])
    return pl.pallas_call(
        functools.partial(project_kernel, tuple(plan), len(pieces), n_alias),
        out_shape=(shape, shape),
        in_specs=[VMEM] * n_in + [ANY] * n_alias,
        out_specs=(ANY, ANY),
        input_output_aliases={n_in + i: i for i in range(n_alias)},
        scratch_shapes=[
            pltpu.VMEM((layers // per, 2, per, seqs, hk, group), wk.dtype),
            pltpu.SemaphoreType.DMA((layers // per, 2, len(blocks[0]))),
        ],
        compiler_params=pltpu.CompilerParams(vmem_limit_bytes=10 * 2**20),
        cost_estimate=pl.CostEstimate(
            flops=2 * tok * d * hk * 2 * layers,
            bytes_accessed=2 * tok * (d + 2 * layers * hk),
            transcendentals=0,
        ),
    )(wk, wv, *pieces, *(out or ()))


def solution(mesh):
    tp = mesh.shape["tp"]
    chips = tp // 2
    ring = [(i, (i + 2 - 4 * (i % 2)) % tp) for i in range(tp)]
    swap = [(i, i ^ 1) for i in range(tp)]

    def send(v, perm):
        return lax.ppermute(v, "tp", perm)

    def per_device(enc_out, norm_scale, w_key, w_value):
        layers, d, heads, k = w_key.shape
        batch = enc_out.shape[0]
        wk = w_key.reshape(layers, d, heads * k).transpose(0, 2, 1)
        wv = w_value.reshape(layers, d, heads * k).transpose(0, 2, 1)
        n = batch // PIECE
        h = n // 2
        seq = lambda i: (i % n) * PIECE

        def run(blocks, out):
            return project(wk, wv, blocks, out, batch, tp)

        def hold(arrays, out):
            return lax.optimization_barrier((tuple(arrays), out))

        s0, = prepare(enc_out, norm_scale, (0,), n, (), 0)
        near = [None] * n
        near[0] = send(s0, ring)
        *rest, wk, wv = prepare(enc_out, norm_scale, tuple(range(1, n)), n, (wk, wv), 1)
        slots = [s0, *rest]
        near[1] = send(slots[1], ring)
        near[2] = send(slots[2], ring)
        own = [(slots[i], (0, seq(i)), (0, seq(i + h))) for i in range(n)]
        out = run([own[0:2], own[2:4]], None)

        def swapped(v):
            return send(v, swap)

        LEFT, RIGHT = chips - 1, 1

        def near_block(i, p, q):
            mine = ((LEFT, seq(i)), (RIGHT, seq(i + h)))
            return [(p, *mine), (q, *mine[::-1])]

        def far_block(i, p, q):
            mine = ((2, seq(i)), (2, seq(i + h)))
            return [(p, *mine), (q, *mine[::-1])]

        far = [None] * h
        (p0, p1), out = hold(near[:2], out)
        q0, q1 = swapped(p0), swapped(p1)
        near[3] = send(slots[3], ring)
        near[4] = send(slots[4], ring)
        out = run([own[4:6]], out)
        (p2,), out = hold(near[2:3], out)
        q2 = swapped(p2)
        near[5] = send(slots[5], ring)
        out = run([near_block(0, p0, q0), near_block(1, p1, q1)], out)
        (p3,), out = hold(near[3:4], out)
        q3 = swapped(p3)
        far[0] = send(p0, ring)
        out = run([near_block(2, p2, q2)], out)
        (p4,), out = hold(near[4:5], out)
        q4 = swapped(p4)
        far[1] = send(p1, ring)
        out = run([near_block(3, p3, q3)], out)
        (p5,), out = hold(near[5:6], out)
        q5 = swapped(p5)
        far[2] = send(p2, ring)
        out = run([near_block(4, p4, q4)], out)
        (p6,), out = hold(far[0:1], out)
        q6 = swapped(p6)
        out = run([near_block(5, p5, q5)], out)
        out = run([far_block(0, p6, q6)], out)
        (p7,), out = hold(far[1:2], out)
        q7 = swapped(p7)
        out = run([far_block(1, p7, q7)], out)
        (p8,), out = hold(far[2:3], out)
        q8 = swapped(p8)
        out = run([far_block(2, p8, q8)], out)
        to_cache = lambda o: o.reshape(layers, batch, heads, k, -1).transpose(0, 1, 4, 2, 3)
        return to_cache(out[0]), to_cache(out[1])

    weight_spec = P(None, None, "tp", None)
    cache_spec = P(None, "dp", None, "tp", None)
    step = jax.shard_map(per_device, mesh=mesh, in_specs=(P("dp", "tp", None), P(None), weight_spec, weight_spec), out_specs=(cache_spec, cache_spec), check_vma=False)

    def program(*args):
        jax.eval_shape(step, *args)
        return step(*args)

    return program
```

time: 246 us -> 140 us (0.57)
  waiting for transfers between devices: 122 us -> 8.88 us
  Pallas kernels: 0 us -> 110 us
  matrix products: 87.4 us -> 0 us
  starting transfers between devices: 0.06 us -> 19.8 us
  local copies, waits for them, and re-layouts: 14.7 us -> 0 us
  between operations: 14.1 us -> 1 us
  other arithmetic: 7.62 us -> 0 us
    all_gather x1 -> x0, waiting for transfers between devices: 122 us -> none  [per_device(): gathered = lax.all_gather(normed, 'tp', axis=1, tiled=True)]
    pallas_call x0 -> x12, Pallas kernels: none -> 110 us  [the longest x10 96.1 us: project(): pl.pallas_call(functools.partial(project_kernel, tuple(plan), len(pieces)...]
    dot_general x2 -> x0, matrix products: 87.4 us -> none  [the longest x1 44.6 us: per_device(): jnp.einsum('bsd,ldhk->lbshk', gathered, w_key, preferred_element_type=jnp...]
    ppermute x0 -> x18, starting transfers between devices: none -> 19.8 us  [send(): return lax.ppermute(v, 'tp', perm)]
    unnamed x4 -> x0, local copies, waits for them, and re-layouts: 14.7 us -> none
    ppermute x0 -> x18, waiting for transfers between devices: none -> 8.88 us  [send(): return lax.ppermute(v, 'tp', perm)]
    convert_element_type x2 -> x0, other arithmetic: 5.04 us -> none  [the longest x1 4.35 us: rms_norm(): (acts * lax.rsqrt(mean_sq + NORM_EPS) * norm_scale.astype(jnp.float32)).a...]
    reduce_sum x1 -> x0, other arithmetic: 2.57 us -> none  [rms_norm(): mean_sq = jnp.mean(acts * acts, axis=-1, keepdims=True)]
  transfers between devices with their start and end apart: 1 -> 18, of which waited for: 1 -> 4; matrix products, arithmetic and copies ran while one was open for 0% -> 0% of each run, Pallas kernels for 0% -> 65%
where the time goes in v1:
time: 140 us
  Pallas kernels  110 us (79%)
  starting transfers between devices  19.8 us (14%)
  waiting for transfers between devices  8.88 us (6%)
    pallas_call x10, Pallas kernels, project(): pl.pallas_call(functools.partial(project_kernel, tuple(plan), len(pieces)...  96.1 us
    ppermute x18, starting transfers between devices, send(): return lax.ppermute(v, 'tp', perm)  19.8 us
    pallas_call x2, Pallas kernels, prepare(): pl.pallas_call(functools.partial(prep_kernel, slots, n_slots, len(weights...  14.1 us
    ppermute x18, waiting for transfers between devices, send(): return lax.ppermute(v, 'tp', perm)  8.88 us
  transfers between devices with their start and end apart: 18, of which 4 were waited for; matrix products, arithmetic and copies ran while one was open for 0% of the time, Pallas kernels for 65%

profile of v1, /device:TPU:81, one launch (start us, length us, event | category | flops | bytes accessed | tf_op | source)
XLA Modules:
  0.0 139.8 jit_solution(9264832153441095094)
XLA Ops:
  0.6 10.8 %shard_map.59 = (bf16[2,128,2048]{2,1,0:T(8,128)(2,1)S(1)}, bf16[2,128,2048]{2,1,0:T(8,128)(2,1)S(1)}, bf16[2,128,2048]{2,1,0:T(8,128)(2,1)S(1)}, bf16[2,128,204...) custom-call(bf16[12,64,2048]{2,1,0:T(8,128)(2,1)} %x_ref.3, ...), custom_call_target="tpu_custom_call" | custom-call | flops 100663296 | bytes 6291456 | tf_op jit(solution)/shard_map/pallas_call | solution.py:99
  11.4 2.4 %collective-permute-start.2 = (bf16[2,128,2048]{2,1,0:T(8,128)(2,1)S(1)}, bf16[2,128,2048]{2,1,0:T(8,128)(2,1)S(1)}, u32[]{:S(2)}, u32[]{:S(2)}) collective-permute-start(bf16[2,128,2048]{2,1,0:T(8,128)(2,1)S(1)} %get-tuple-element.59.refs_3_), channel_id=1, source_target_pairs={{0,2},{1,7},{2,4},{3,1},{4,6},{5,3},{6,0},{7,5},{8,10},{9,15},{10,... | collective-permute-start | bytes 3145736 | tf_op jit(solution)/shard_map/ppermute | solution.py:203
  13.8 3.3 %shard_map.60.refs_2_ = bf16[2,128,2048]{2,1,0:T(8,128)(2,1)S(1)} custom-call(bf16[12,64,2048]{2,1,0:T(8,128)(2,1)} %x_ref.3, bf16[2048]{0:T(1024)(128)(2,1)} %scale_ref.3), custom_call_target="tpu_custom_call" | custom-call | flops 100663296 | bytes 6291456 | tf_op jit(solution)/shard_map/pallas_call | solution.py:99
  18.9 15.3 %shard_map.61 = (bf16[6,12,256,512]{3,2,1,0:T(8,128)(2,1)}, bf16[6,12,256,512]{3,2,1,0:T(8,128)(2,1)}) custom-call(bf16[6,256,2048]{2,1,0:T(8,128)(2,1)S(1)} %get-tuple-element.54.refs_0_, bf16[6,256,2048]{2,1,0:T(8,128)(2,1)S(1)} %get-tuple-element.55.refs_1_, bf16[2,128,2048]{2,1,0:T(8,128)(2,1)S(1)} %shard_map.60.refs_2_, ...), custom_call_target="tpu_custom_call" | custom-call | flops 12884901888 | bytes 10485760 | tf_op jit(solution)/shard_map/pallas_call | solution.py:177
  34.2 2.6 %collective-permute-done.1.refs_2_ = bf16[2,128,2048]{2,1,0:T(8,128)(2,1)S(1)} collective-permute-done((bf16[2,128,2048]{2,1,0:T(8,128)(2,1)S(1)}, bf16[2,128,2048]{2,1,0:T(8,128)(2,1)S(1)}, u32[]{:S(2)}, u32[]{:S(2)}) %collective-permute-start.1) | collective-permute-done | bytes 1048608 | tf_op jit(solution)/shard_map/ppermute | solution.py:203
  36.8 2.1 %collective-permute-start.10 = (bf16[2,128,2048]{2,1,0:T(8,128)(2,1)S(1)}, bf16[2,128,2048]{2,1,0:T(8,128)(2,1)S(1)}, u32[]{:S(2)}, u32[]{:S(2)}) collective-permute-start(bf16[2,128,2048]{2,1,0:T(8,128)(2,1)S(1)} %collective-permute-done.2.refs_4_), channel_id=1, source_target_pairs={{0,1},{1,0},{2,3},{3,2},{4,5},{5,4},{6,7},{7,6},{8,9},{9,8},{10,11... | collective-permute-start | bytes 3145736 | tf_op jit(solution)/shard_map/ppermute | solution.py:203
  38.9 1.5 %collective-permute-start.8 = (bf16[2,128,2048]{2,1,0:T(8,128)(2,1)S(1)}, bf16[2,128,2048]{2,1,0:T(8,128)(2,1)S(1)}, u32[]{:S(2)}, u32[]{:S(2)}) collective-permute-start(bf16[2,128,2048]{2,1,0:T(8,128)(2,1)S(1)} %get-tuple-element.60.refs_5_), channel_id=1, source_target_pairs={{0,2},{1,7},{2,4},{3,1},{4,6},{5,3},{6,0},{7,5},{8,10},{9,15},{10,... | collective-permute-start | bytes 3145736 | tf_op jit(solution)/shard_map/ppermute | solution.py:203
  40.5 8.2 %shard_map.62 = (bf16[6,12,256,512]{3,2,1,0:T(8,128)(2,1)}, bf16[6,12,256,512]{3,2,1,0:T(8,128)(2,1)}) custom-call(bf16[6,256,2048]{2,1,0:T(8,128)(2,1)S(1)} %get-tuple-element.54.refs_0_, bf16[6,256,2048]{2,1,0:T(8,128)(2,1)S(1)} %get-tuple-element.55.refs_1_, ...), custom_call_target="tpu_custom_call", output_to_operand_aliasing={{0}: (4, {}), {1}: (5, {})} | custom-call | flops 6442450944 | bytes 5242880 | tf_op jit(solution)/shard_map/pallas_call | solution.py:177
  48.6 2.5 %collective-permute-start.12 = (bf16[2,128,2048]{2,1,0:T(8,128)(2,1)S(1)}, bf16[2,128,2048]{2,1,0:T(8,128)(2,1)S(1)}, u32[]{:S(2)}, u32[]{:S(2)}) collective-permute-start(bf16[2,128,2048]{2,1,0:T(8,128)(2,1)S(1)} %get-tuple-element.58.refs_3_), channel_id=1, source_target_pairs={{0,2},{1,7},{2,4},{3,1},{4,6},{5,3},{6,0},{7,5},{8,10},{9,15},{10,... | collective-permute-start | bytes 3145736 | tf_op jit(solution)/shard_map/ppermute | solution.py:203
  51.2 15.3 %shard_map.63 = (bf16[6,12,256,512]{3,2,1,0:T(8,128)(2,1)}, bf16[6,12,256,512]{3,2,1,0:T(8,128)(2,1)}) custom-call(bf16[6,256,2048]{2,1,0:T(8,128)(2,1)S(1)} %get-tuple-element.54.refs_0_, bf16[6,256,2048]{2,1,0:T(8,128)(2,1)S(1)} %get-tuple-element.55.refs_1_, ...), custom_call_target="tpu_custom_call", output_to_operand_aliasing={{0}: (6, {}), {1}: (7, {})} | custom-call | flops 12884901888 | bytes 10485760 | tf_op jit(solution)/shard_map/pallas_call | solution.py:177
  67.1 8.2 %shard_map.64 = (bf16[6,12,256,512]{3,2,1,0:T(8,128)(2,1)}, bf16[6,12,256,512]{3,2,1,0:T(8,128)(2,1)}) custom-call(bf16[6,256,2048]{2,1,0:T(8,128)(2,1)S(1)} %get-tuple-element.54.refs_0_, bf16[6,256,2048]{2,1,0:T(8,128)(2,1)S(1)} %get-tuple-element.55.refs_1_, ...), custom_call_target="tpu_custom_call", output_to_operand_aliasing={{0}: (4, {}), {1}: (5, {})} | custom-call | flops 6442450944 | bytes 5242880 | tf_op jit(solution)/shard_map/pallas_call | solution.py:177
  75.5 1.9 %collective-permute-start.5 = (bf16[2,128,2048]{2,1,0:T(8,128)(2,1)S(1)}, bf16[2,128,2048]{2,1,0:T(8,128)(2,1)S(1)}, u32[]{:S(2)}, u32[]{:S(2)}) collective-permute-start(bf16[2,128,2048]{2,1,0:T(8,128)(2,1)S(1)} %collective-permute-done.1.refs_2_), channel_id=1, source_target_pairs={{0,2},{1,7},{2,4},{3,1},{4,6},{5,3},{6,0},{7,5},{8,10},{9,15},{10,... | collective-permute-start | bytes 3145736 | tf_op jit(solution)/shard_map/ppermute | solution.py:203
  77.4 8.2 %shard_map.65 = (bf16[6,12,256,512]{3,2,1,0:T(8,128)(2,1)}, bf16[6,12,256,512]{3,2,1,0:T(8,128)(2,1)}) custom-call(bf16[6,256,2048]{2,1,0:T(8,128)(2,1)S(1)} %get-tuple-element.54.refs_0_, bf16[6,256,2048]{2,1,0:T(8,128)(2,1)S(1)} %get-tuple-element.55.refs_1_, ...), custom_call_target="tpu_custom_call", output_to_operand_aliasing={{0}: (4, {}), {1}: (5, {})} | custom-call | flops 6442450944 | bytes 5242880 | tf_op jit(solution)/shard_map/pallas_call | solution.py:177
  85.7 8.2 %shard_map.66 = (bf16[6,12,256,512]{3,2,1,0:T(8,128)(2,1)}, bf16[6,12,256,512]{3,2,1,0:T(8,128)(2,1)}) custom-call(bf16[6,256,2048]{2,1,0:T(8,128)(2,1)S(1)} %get-tuple-element.54.refs_0_, bf16[6,256,2048]{2,1,0:T(8,128)(2,1)S(1)} %get-tuple-element.55.refs_1_, ...), custom_call_target="tpu_custom_call", output_to_operand_aliasing={{0}: (4, {}), {1}: (5, {})} | custom-call | flops 6442450944 | bytes 5242880 | tf_op jit(solution)/shard_map/pallas_call | solution.py:177
  93.9 1.2 collective-permute-start.14
  95.1 1.1 collective-permute-start.4
  96.2 8.2 %shard_map.67 = (bf16[6,12,256,512]{3,2,1,0:T(8,128)(2,1)}, bf16[6,12,256,512]{3,2,1,0:T(8,128)(2,1)}) custom-call(bf16[6,256,2048]{2,1,0:T(8,128)(2,1)S(1)} %get-tuple-element.54.refs_0_, bf16[6,256,2048]{2,1,0:T(8,128)(2,1)S(1)} %get-tuple-element.55.refs_1_, ...), custom_call_target="tpu_custom_call", output_to_operand_aliasing={{0}: (4, {}), {1}: (5, {})} | custom-call | flops 6442450944 | bytes 5242880 | tf_op jit(solution)/shard_map/pallas_call | solution.py:177
  104.4 8.2 %shard_map.68 = (bf16[6,12,256,512]{3,2,1,0:T(8,128)(2,1)}, bf16[6,12,256,512]{3,2,1,0:T(8,128)(2,1)}) custom-call(bf16[6,256,2048]{2,1,0:T(8,128)(2,1)S(1)} %get-tuple-element.54.refs_0_, bf16[6,256,2048]{2,1,0:T(8,128)(2,1)S(1)} %get-tuple-element.55.refs_1_, ...), custom_call_target="tpu_custom_call", output_to_operand_aliasing={{0}: (4, {}), {1}: (5, {})} | custom-call | flops 6442450944 | bytes 5242880 | tf_op jit(solution)/shard_map/pallas_call | solution.py:177
  112.7 1.9 %collective-permute-start.3 = (bf16[2,128,2048]{2,1,0:T(8,128)(2,1)S(1)}, bf16[2,128,2048]{2,1,0:T(8,128)(2,1)S(1)}, u32[]{:S(2)}, u32[]{:S(2)}) collective-permute-start(bf16[2,128,2048]{2,1,0:T(8,128)(2,1)S(1)} %collective-permute-done.refs_2_), channel_id=1, source_target_pairs={{0,2},{1,7},{2,4},{3,1},{4,6},{5,3},{6,0},{7,5},{8,10},{9,15},{10,... | collective-permute-start | bytes 3145736 | tf_op jit(solution)/shard_map/ppermute | solution.py:203
  115.3 8.2 %shard_map.69 = (bf16[6,12,256,512]{3,2,1,0:T(8,128)(2,1)}, bf16[6,12,256,512]{3,2,1,0:T(8,128)(2,1)}) custom-call(bf16[6,256,2048]{2,1,0:T(8,128)(2,1)S(1)} %get-tuple-element.54.refs_0_, bf16[6,256,2048]{2,1,0:T(8,128)(2,1)S(1)} %get-tuple-element.55.refs_1_, ...), custom_call_target="tpu_custom_call", output_to_operand_aliasing={{0}: (4, {}), {1}: (5, {})} | custom-call | flops 6442450944 | bytes 5242880 | tf_op jit(solution)/shard_map/pallas_call | solution.py:177
  123.5 3.2 %collective-permute-done.3.refs_2_ = bf16[2,128,2048]{2,1,0:T(8,128)(2,1)S(1)} collective-permute-done((bf16[2,128,2048]{2,1,0:T(8,128)(2,1)S(1)}, bf16[2,128,2048]{2,1,0:T(8,128)(2,1)S(1)}, u32[]{:S(2)}, u32[]{:S(2)}) %collective-permute-start.3) | collective-permute-done | bytes 1048608 | tf_op jit(solution)/shard_map/ppermute | solution.py:203
  126.7 2.5 %collective-permute-start.17 = (bf16[2,128,2048]{2,1,0:T(8,128)(2,1)S(1)}, bf16[2,128,2048]{2,1,0:T(8,128)(2,1)S(1)}, u32[]{:S(2)}, u32[]{:S(2)}) collective-permute-start(bf16[2,128,2048]{2,1,0:T(8,128)(2,1)S(1)} %collective-permute-done.3.refs_2_), channel_id=1, source_target_pairs={{0,1},{1,0},{2,3},{3,2},{4,5},{5,4},{6,7},{7,6},{8,9},{9,8},{10,11... | collective-permute-start | bytes 3145736 | tf_op jit(solution)/shard_map/ppermute | solution.py:203
  129.2 2.3 %collective-permute-done.17.refs_3_ = bf16[2,128,2048]{2,1,0:T(8,128)(2,1)S(1)} collective-permute-done((bf16[2,128,2048]{2,1,0:T(8,128)(2,1)S(1)}, bf16[2,128,2048]{2,1,0:T(8,128)(2,1)S(1)}, u32[]{:S(2)}, u32[]{:S(2)}) %collective-permute-start.17) | collective-permute-done | bytes 1048608 | tf_op jit(solution)/shard_map/ppermute | solution.py:203
  131.5 8.2 %shard_map.70 = (bf16[6,12,256,512]{3,2,1,0:T(8,128)(2,1)}, bf16[6,12,256,512]{3,2,1,0:T(8,128)(2,1)}) custom-call(bf16[6,256,2048]{2,1,0:T(8,128)(2,1)S(1)} %get-tuple-element.54.refs_0_, bf16[6,256,2048]{2,1,0:T(8,128)(2,1)S(1)} %get-tuple-element.55.refs_1_, ...), custom_call_target="tpu_custom_call", output_to_operand_aliasing={{0}: (4, {}), {1}: (5, {})} | custom-call | flops 6442450944 | bytes 5242880 | tf_op jit(solution)/shard_map/pallas_call | solution.py:177
  (24 shorter events, 3.6 us)
Async XLA Ops:
  11.4 22.8 %collective-permute-start.2 = (bf16[2,128,2048]{2,1,0:T(8,128)(2,1)S(1)}, bf16[2,128,2048]{2,1,0:T(8,128)(2,1)S(1)}, u32[]{:S(2)}, u32[]{:S(2)}) collective-permute-start(bf16[2,128,2048]{2,1,0:T(8,128)(2,1)S(1)} %get-tuple-element.59.refs_3_), channel_id=1, source_target_pairs={{0,2},{1,7},{2,4},{3,1},{4,6},{5,3},{6,0},{7,5},{8,10},{9,15},{10,... | collective-permute-start | bytes 3145736 | tf_op jit(solution)/shard_map/ppermute | solution.py:203
  17.1 19.7 %collective-permute-start.1 = (bf16[2,128,2048]{2,1,0:T(8,128)(2,1)S(1)}, bf16[2,128,2048]{2,1,0:T(8,128)(2,1)S(1)}, u32[]{:S(2)}, u32[]{:S(2)}) collective-permute-start(bf16[2,128,2048]{2,1,0:T(8,128)(2,1)S(1)} %shard_map.60.refs_2_), channel_id=1, source_target_pairs={{0,2},{1,7},{2,4},{3,1},{4,6},{5,3},{6,0},{7,5},{8,10},{9,15},{10,... | collective-permute-start | bytes 3145736 | tf_op jit(solution)/shard_map/ppermute | solution.py:203
  17.8 30.8 %collective-permute-start = (bf16[2,128,2048]{2,1,0:T(8,128)(2,1)S(1)}, bf16[2,128,2048]{2,1,0:T(8,128)(2,1)S(1)}, u32[]{:S(2)}, u32[]{:S(2)}) collective-permute-start(bf16[2,128,2048]{2,1,0:T(8,128)(2,1)S(1)} %get-tuple-element.56.refs_4_), channel_id=1, source_target_pairs={{0,2},{1,7},{2,4},{3,1},{4,6},{5,3},{6,0},{7,5},{8,10},{9,15},{10,... | collective-permute-start | bytes 3145736 | tf_op jit(solution)/shard_map/ppermute | solution.py:203
  36.8 14.4 %collective-permute-start.10 = (bf16[2,128,2048]{2,1,0:T(8,128)(2,1)S(1)}, bf16[2,128,2048]{2,1,0:T(8,128)(2,1)S(1)}, u32[]{:S(2)}, u32[]{:S(2)}) collective-permute-start(bf16[2,128,2048]{2,1,0:T(8,128)(2,1)S(1)} %collective-permute-done.2.refs_4_), channel_id=1, source_target_pairs={{0,1},{1,0},{2,3},{3,2},{4,5},{5,4},{6,7},{7,6},{8,9},{9,8},{10,11... | collective-permute-start | bytes 3145736 | tf_op jit(solution)/shard_map/ppermute | solution.py:203
  38.9 12.2 %collective-permute-start.9 = (bf16[2,128,2048]{2,1,0:T(8,128)(2,1)S(1)}, bf16[2,128,2048]{2,1,0:T(8,128)(2,1)S(1)}, u32[]{:S(2)}, u32[]{:S(2)}) collective-permute-start(bf16[2,128,2048]{2,1,0:T(8,128)(2,1)S(1)} %collective-permute-done.1.refs_2_), channel_id=1, source_target_pairs={{0,1},{1,0},{2,3},{3,2},{4,5},{5,4},{6,7},{7,6},{8,9},{9,8},{10,11... | collective-permute-start | bytes 3145736 | tf_op jit(solution)/shard_map/ppermute | solution.py:203
  38.9 27.6 %collective-permute-start.8 = (bf16[2,128,2048]{2,1,0:T(8,128)(2,1)S(1)}, bf16[2,128,2048]{2,1,0:T(8,128)(2,1)S(1)}, u32[]{:S(2)}, u32[]{:S(2)}) collective-permute-start(bf16[2,128,2048]{2,1,0:T(8,128)(2,1)S(1)} %get-tuple-element.60.refs_5_), channel_id=1, source_target_pairs={{0,2},{1,7},{2,4},{3,1},{4,6},{5,3},{6,0},{7,5},{8,10},{9,15},{10,... | collective-permute-start | bytes 3145736 | tf_op jit(solution)/shard_map/ppermute | solution.py:203
  40.4 34.9 %collective-permute-start.6 = (bf16[2,128,2048]{2,1,0:T(8,128)(2,1)S(1)}, bf16[2,128,2048]{2,1,0:T(8,128)(2,1)S(1)}, u32[]{:S(2)}, u32[]{:S(2)}) collective-permute-start(bf16[2,128,2048]{2,1,0:T(8,128)(2,1)S(1)} %get-tuple-element.57.refs_2_), channel_id=1, source_target_pairs={{0,2},{1,7},{2,4},{3,1},{4,6},{5,3},{6,0},{7,5},{8,10},{9,15},{10,... | collective-permute-start | bytes 3145736 | tf_op jit(solution)/shard_map/ppermute | solution.py:203
  48.6 36.9 %collective-permute-start.12 = (bf16[2,128,2048]{2,1,0:T(8,128)(2,1)S(1)}, bf16[2,128,2048]{2,1,0:T(8,128)(2,1)S(1)}, u32[]{:S(2)}, u32[]{:S(2)}) collective-permute-start(bf16[2,128,2048]{2,1,0:T(8,128)(2,1)S(1)} %get-tuple-element.58.refs_3_), channel_id=1, source_target_pairs={{0,2},{1,7},{2,4},{3,1},{4,6},{5,3},{6,0},{7,5},{8,10},{9,15},{10,... | collective-permute-start | bytes 3145736 | tf_op jit(solution)/shard_map/ppermute | solution.py:203
  51.2 16.0 %collective-permute-start.7 = (bf16[2,128,2048]{2,1,0:T(8,128)(2,1)S(1)}, bf16[2,128,2048]{2,1,0:T(8,128)(2,1)S(1)}, u32[]{:S(2)}, u32[]{:S(2)}) collective-permute-start(bf16[2,128,2048]{2,1,0:T(8,128)(2,1)S(1)} %collective-permute-done.refs_2_), channel_id=1, source_target_pairs={{0,1},{1,0},{2,3},{3,2},{4,5},{5,4},{6,7},{7,6},{8,9},{9,8},{10,11... | collective-permute-start | bytes 3145736 | tf_op jit(solution)/shard_map/ppermute | solution.py:203
  66.5 10.8 %collective-permute-start.13 = (bf16[2,128,2048]{2,1,0:T(8,128)(2,1)S(1)}, bf16[2,128,2048]{2,1,0:T(8,128)(2,1)S(1)}, u32[]{:S(2)}, u32[]{:S(2)}) collective-permute-start(bf16[2,128,2048]{2,1,0:T(8,128)(2,1)S(1)} %collective-permute-done.8.refs_2_), channel_id=1, source_target_pairs={{0,1},{1,0},{2,3},{3,2},{4,5},{5,4},{6,7},{7,6},{8,9},{9,8},{10,11... | collective-permute-start | bytes 3145736 | tf_op jit(solution)/shard_map/ppermute | solution.py:203
  75.3 10.4 %collective-permute-start.11 = (bf16[2,128,2048]{2,1,0:T(8,128)(2,1)S(1)}, bf16[2,128,2048]{2,1,0:T(8,128)(2,1)S(1)}, u32[]{:S(2)}, u32[]{:S(2)}) collective-permute-start(bf16[2,128,2048]{2,1,0:T(8,128)(2,1)S(1)} %collective-permute-done.6.refs_2_), channel_id=1, source_target_pairs={{0,1},{1,0},{2,3},{3,2},{4,5},{5,4},{6,7},{7,6},{8,9},{9,8},{10,11... | collective-permute-start | bytes 3145736 | tf_op jit(solution)/shard_map/ppermute | solution.py:203
  75.5 18.4 %collective-permute-start.5 = (bf16[2,128,2048]{2,1,0:T(8,128)(2,1)S(1)}, bf16[2,128,2048]{2,1,0:T(8,128)(2,1)S(1)}, u32[]{:S(2)}, u32[]{:S(2)}) collective-permute-start(bf16[2,128,2048]{2,1,0:T(8,128)(2,1)S(1)} %collective-permute-done.1.refs_2_), channel_id=1, source_target_pairs={{0,2},{1,7},{2,4},{3,1},{4,6},{5,3},{6,0},{7,5},{8,10},{9,15},{10,... | collective-permute-start | bytes 3145736 | tf_op jit(solution)/shard_map/ppermute | solution.py:203
  85.6 10.6 %collective-permute-start.15 = (bf16[2,128,2048]{2,1,0:T(8,128)(2,1)S(1)}, bf16[2,128,2048]{2,1,0:T(8,128)(2,1)S(1)}, u32[]{:S(2)}, u32[]{:S(2)}) collective-permute-start(bf16[2,128,2048]{2,1,0:T(8,128)(2,1)S(1)} %collective-permute-done.12.refs_2_), channel_id=1, source_target_pairs={{0,1},{1,0},{2,3},{3,2},{4,5},{5,4},{6,7},{7,6},{8,9},{9,8},{10,11... | collective-permute-start | bytes 3145736 | tf_op jit(solution)/shard_map/ppermute | solution.py:203
  93.9 10.5 %collective-permute-start.14 = (bf16[2,128,2048]{2,1,0:T(8,128)(2,1)S(1)}, bf16[2,128,2048]{2,1,0:T(8,128)(2,1)S(1)}, u32[]{:S(2)}, u32[]{:S(2)}) collective-permute-start(bf16[2,128,2048]{2,1,0:T(8,128)(2,1)S(1)} %collective-permute-done.5.refs_2_), channel_id=1, source_target_pairs={{0,1},{1,0},{2,3},{3,2},{4,5},{5,4},{6,7},{7,6},{8,9},{9,8},{10,11... | collective-permute-start | bytes 3145736 | tf_op jit(solution)/shard_map/ppermute | solution.py:203
  95.1 17.5 %collective-permute-start.4 = (bf16[2,128,2048]{2,1,0:T(8,128)(2,1)S(1)}, bf16[2,128,2048]{2,1,0:T(8,128)(2,1)S(1)}, u32[]{:S(2)}, u32[]{:S(2)}) collective-permute-start(bf16[2,128,2048]{2,1,0:T(8,128)(2,1)S(1)} %collective-permute-done.2.refs_4_), channel_id=1, source_target_pairs={{0,2},{1,7},{2,4},{3,1},{4,6},{5,3},{6,0},{7,5},{8,10},{9,15},{10,... | collective-permute-start | bytes 3145736 | tf_op jit(solution)/shard_map/ppermute | solution.py:203
  112.6 2.8 %collective-permute-start.16 = (bf16[2,128,2048]{2,1,0:T(8,128)(2,1)S(1)}, bf16[2,128,2048]{2,1,0:T(8,128)(2,1)S(1)}, u32[]{:S(2)}, u32[]{:S(2)}) collective-permute-start(bf16[2,128,2048]{2,1,0:T(8,128)(2,1)S(1)} %collective-permute-done.4.refs_2_), channel_id=1, source_target_pairs={{0,1},{1,0},{2,3},{3,2},{4,5},{5,4},{6,7},{7,6},{8,9},{9,8},{10,11... | collective-permute-start | bytes 3145736 | tf_op jit(solution)/shard_map/ppermute | solution.py:203
  112.7 14.0 %collective-permute-start.3 = (bf16[2,128,2048]{2,1,0:T(8,128)(2,1)S(1)}, bf16[2,128,2048]{2,1,0:T(8,128)(2,1)S(1)}, u32[]{:S(2)}, u32[]{:S(2)}) collective-permute-start(bf16[2,128,2048]{2,1,0:T(8,128)(2,1)S(1)} %collective-permute-done.refs_2_), channel_id=1, source_target_pairs={{0,2},{1,7},{2,4},{3,1},{4,6},{5,3},{6,0},{7,5},{8,10},{9,15},{10,... | collective-permute-start | bytes 3145736 | tf_op jit(solution)/shard_map/ppermute | solution.py:203
  126.7 4.7 %collective-permute-start.17 = (bf16[2,128,2048]{2,1,0:T(8,128)(2,1)S(1)}, bf16[2,128,2048]{2,1,0:T(8,128)(2,1)S(1)}, u32[]{:S(2)}, u32[]{:S(2)}) collective-permute-start(bf16[2,128,2048]{2,1,0:T(8,128)(2,1)S(1)} %collective-permute-done.3.refs_2_), channel_id=1, source_target_pairs={{0,1},{1,0},{2,3},{3,2},{4,5},{5,4},{6,7},{7,6},{8,9},{9,8},{10,11... | collective-permute-start | bytes 3145736 | tf_op jit(solution)/shard_map/ppermute | solution.py:203

commit v2 on v0

v2 whole, which is shorter than its diff:
```python
import functools

import jax
import jax.numpy as jnp
from jax import lax
from jax.experimental import pallas as pl
from jax.experimental.pallas import tpu as pltpu
from jax.sharding import PartitionSpec as P


NORM_EPS = 1e-6
PIECE = 2
LAYERS = 2
ANY = pl.BlockSpec(memory_space=pl.ANY)
VMEM = pl.BlockSpec(memory_space=pltpu.VMEM)
NT = (((1,), (1,)), ((), ()))
MESH = pl.DeviceIdType.MESH


def in_hbm(x):
    return pltpu.with_memory_space_constraint(x, pltpu.HBM)


def rms_norm(x, scale):
    acts = x.astype(jnp.float32)
    mean_sq = jnp.mean(acts * acts, axis=-1, keepdims=True)
    return (acts * lax.rsqrt(mean_sq + NORM_EPS) * scale).astype(jnp.bfloat16)


def output_copies(outs, stage, sem, entry, c, per):
    chips = lax.axis_size("tp") // 2
    me = lax.axis_index("tp")
    core, chip = lax.rem(me, 2), me // 2
    group = stage.shape[-1]
    copies = []
    at = 0
    for j, (n, on0, on1) in enumerate(entry):
        off, first = (a if a is b else jnp.where(core == 0, a, b) for a, b in zip(on0, on1))
        lanes = pl.ds(pl.multiple_of(lax.rem(chip + off, chips) * group, group), group)
        for kv, out in enumerate(outs):
            dst = out.at[pl.ds(c * per, per), pl.ds(first, n), :, lanes]
            copies.append(pltpu.make_async_copy(stage.at[c, kv, :, pl.ds(at, n)], dst, sem.at[c, kv, j]))
        at += n
    return copies


def matmul_block(w_refs, pieces, stage, c):
    per, _, hk, group = stage.shape[2:]
    d = w_refs[0].shape[-1]
    tokens = [p[...].reshape(-1, d) for p in pieces]
    y = jnp.concatenate(tokens) if len(tokens) > 1 else tokens[0]
    for kv, w_ref in enumerate(w_refs):
        w = w_ref[pl.ds(c * per, per)].reshape(per * hk, d)
        res = lax.dot_general(w, y, NT, preferred_element_type=jnp.float32).astype(stage.dtype)
        for l in range(per):
            for s in range(y.shape[0] // group):
                stage[c, kv, l, s] = res[l * hk:(l + 1) * hk, s * group:(s + 1) * group]


def prep_kernel(slots, n_slots, early, n_weights, x_ref, scale_ref, *refs):
    w_in, refs = refs[:n_weights], refs[n_weights:]
    made, refs = refs[:early], refs[early:]
    outs, refs = refs[:len(slots)], refs[len(slots):]
    w_out, refs = refs[:n_weights], refs[n_weights:]
    stage, refs = (refs[0], refs[1:]) if n_weights else (None, refs)
    xbuf, scale_buf, in_sem, scale_sem, w_sem, send_sem, recv_sem = refs
    half = x_ref.shape[1]
    me = lax.axis_index("tp")
    core = lax.rem(me, 2)
    other = me + 1 - 2 * core
    rows = pl.ds(pl.multiple_of(core * half, half), half)
    shift = n_slots // 2
    there = lambda i: (i + shift) % n_slots
    needed = sorted((i for i in range(n_slots) if i in slots or there(i) in slots), key=lambda i: (slots.index(there(i)) if there(i) in slots else n_slots))

    barrier = pltpu.get_barrier_semaphore()
    pl.semaphore_signal(barrier, inc=1, device_id={"tp": other}, device_id_type=MESH)

    def load(j):
        first = lax.rem(needed[j] + shift * core, n_slots) * PIECE
        return pltpu.make_async_copy(x_ref.at[pl.ds(first, PIECE)], xbuf.at[j], in_sem.at[j])

    def send(j):
        to = slots.index(there(needed[j]))
        return pltpu.make_async_remote_copy(
            src_ref=xbuf.at[j],
            dst_ref=outs[to].at[:, rows],
            send_sem=send_sem.at[to],
            recv_sem=recv_sem.at[to],
            device_id={"tp": other},
            device_id_type=MESH,
        )

    def load_weights(kv, c):
        layers = pl.ds(c * stage.shape[2], stage.shape[2])
        return pltpu.make_async_copy(w_in[kv].at[layers], w_out[kv].at[layers], w_sem.at[kv, c])

    get_scale = pltpu.make_async_copy(scale_ref, scale_buf, scale_sem)
    get_scale.start()
    for j in range(len(needed)):
        load(j).start()
    for c in range(stage.shape[0] if n_weights else 0):
        for kv in range(n_weights):
            load_weights(kv, c).start()
    get_scale.wait()
    scale = scale_buf[...].astype(jnp.float32).reshape(1, -1)
    pending = None
    sent = []
    pl.semaphore_wait(barrier, 1)
    for j, i in enumerate(needed):
        load(j).wait()
        y = rms_norm(xbuf[j], scale)
        if there(i) in slots:
            xbuf[j] = y
        if i in slots:
            outs[slots.index(i)][:, rows] = y
        if pending is not None:
            send(pending).start()
            sent.append(pending)
        pending = j if there(i) in slots else None
    if pending is not None:
        send(pending).start()
        sent.append(pending)
    if n_weights:
        first = sent[0]
        send(first).wait_recv()

        @pl.loop(0, stage.shape[0])
        def _(c):
            for kv in range(n_weights):
                load_weights(kv, c).wait()
            matmul_block(w_out, [*made, outs[slots.index(there(needed[first]))]], stage, c)

    for j in sent:
        send(j).wait_send()
        if not n_weights or j != first:
            send(j).wait_recv()


def stage_shape(weights, seqs, group):
    layers, hk, _ = weights[0].shape
    return jax.ShapeDtypeStruct((layers // LAYERS, len(weights), LAYERS, seqs, hk, group), weights[0].dtype)


def prepare(x, scale, slots, n_slots, early, weights, collective_id):
    _, half, d = x.shape
    shift = n_slots // 2
    n_needed = len([i for i in range(n_slots) if i in slots or (i + shift) % n_slots in slots])
    piece = jax.ShapeDtypeStruct((PIECE, 2 * half, d), x.dtype)
    out_shape = (piece,) * len(slots) + tuple(jax.ShapeDtypeStruct(w.shape, w.dtype) for w in weights)
    if weights:
        out_shape += (stage_shape(weights, PIECE * (len(early) + 1), 2 * half),)
    return pl.pallas_call(
        functools.partial(prep_kernel, slots, n_slots, len(early), len(weights)),
        out_shape=out_shape,
        in_specs=[ANY, ANY] + [ANY] * len(weights) + [VMEM] * len(early),
        out_specs=(VMEM,) * len(out_shape),
        scratch_shapes=[
            pltpu.VMEM((n_needed, PIECE, half, d), x.dtype),
            pltpu.VMEM(scale.shape, scale.dtype),
            pltpu.SemaphoreType.DMA((n_needed,)),
            pltpu.SemaphoreType.DMA,
            pltpu.SemaphoreType.DMA((2, weights[0].shape[0] // LAYERS if weights else 1)),
            pltpu.SemaphoreType.DMA((len(slots),)),
            pltpu.SemaphoreType.DMA((len(slots),)),
        ],
        compiler_params=pltpu.CompilerParams(vmem_limit_bytes=8 * 2**20, collective_id=collective_id, has_side_effects=True),
        cost_estimate=pl.CostEstimate(flops=64 * x.size, bytes_accessed=4 * x.size, transcendentals=0),
    )(in_hbm(x), in_hbm(scale), *map(in_hbm, weights), *early)


def project_kernel(plan, n_pieces, carried, n_alias, keep, *refs):
    w_refs, refs = refs[:2], refs[2:]
    pieces, refs = refs[:n_pieces], refs[n_pieces:]
    before, refs = refs[0], refs[1 + n_alias:]
    outs, stage, refs = refs[:2], refs[2], refs[3:]
    sem, before_sem = refs
    chunks, _, per = stage.shape[:3]
    entry, old_chunks = carried
    late = [copy for c in old_chunks for copy in output_copies(outs, before, before_sem, entry, c, per)]
    for copy in late:
        copy.start()
    put = lambda i, c: output_copies(outs, stage, sem, plan[i], c, per)
    used = 0
    for i, block in enumerate(plan):
        mine = pieces[used:used + len(block)]
        used += len(block)
        last = i == len(plan) - 1 and keep

        @pl.loop(0, chunks)
        def _(c):
            if i > 0:
                for copy in put(i - 1, c):
                    copy.wait()
            matmul_block(w_refs, mine, stage, c)
            if last:

                @pl.when(c < chunks - 1)
                def _():
                    for copy in put(i, c):
                        copy.start()
            else:
                for copy in put(i, c):
                    copy.start()

    for copy in late:
        copy.wait()
    for c in range(chunks - 1 if keep else chunks):
        for copy in put(len(plan) - 1, c):
            copy.wait()


def project(weights, blocks, out, carry, batch, tp, keep):
    layers, hk, d = weights[0].shape
    plan = tuple(tuple((p.shape[0], *where) for p, *where in block) for block in blocks)
    pieces = [piece for block in blocks for piece, *_ in block]
    group = pieces[0].shape[1]
    shape = jax.ShapeDtypeStruct((layers, batch, hk, group * tp // 2), weights[0].dtype)
    n_alias = 0 if out is None else 2
    n_in = 3 + len(pieces)
    stage = stage_shape(weights, sum(n for n, *_ in plan[0]), group)
    before, entry, chunks = carry
    tok = sum(p.shape[0] for p in pieces) * group
    *out, stage_out = pl.pallas_call(
        functools.partial(project_kernel, plan, len(pieces), (entry, chunks), n_alias, keep),
        out_shape=(shape, shape, stage),
        in_specs=[VMEM] * n_in + [ANY] * n_alias,
        out_specs=(ANY, ANY, VMEM),
        input_output_aliases={n_in + i: i for i in range(n_alias)},
        scratch_shapes=[
            pltpu.SemaphoreType.DMA((stage.shape[0], 2, len(plan[0]))),
            pltpu.SemaphoreType.DMA((stage.shape[0], 2, len(entry))),
        ],
        compiler_params=pltpu.CompilerParams(vmem_limit_bytes=4 * 2**20),
        cost_estimate=pl.CostEstimate(
            flops=2 * tok * d * hk * 2 * layers,
            bytes_accessed=2 * tok * (d + 2 * layers * hk),
            transcendentals=0,
        ),
    )(*weights, *pieces, before, *(out or ()))
    return out, (stage_out, plan[-1], (stage.shape[0] - 1,))


def solution(mesh):
    tp = mesh.shape["tp"]
    chips = tp // 2
    ring = [(i, (i + 2 - 4 * (i % 2)) % tp) for i in range(tp)]
    swap = [(i, i ^ 1) for i in range(tp)]

    def send(v, perm):
        return lax.ppermute(v, "tp", perm)

    def per_device(enc_out, norm_scale, w_key, w_value):
        layers, d, heads, k = w_key.shape
        batch = enc_out.shape[0]
        wk = w_key.reshape(layers, d, heads * k).transpose(0, 2, 1)
        wv = w_value.reshape(layers, d, heads * k).transpose(0, 2, 1)
        n = batch // PIECE
        h = n // 2
        seq = lambda i: (i % n) * PIECE

        state = {"out": None}

        def run(blocks, keep=True):
            state["out"], state["carry"] = project(weights, blocks, state["out"], state["carry"], batch, tp, keep)

        def hold(*arrays):
            arrays, state["out"] = lax.optimization_barrier((arrays, state["out"]))
            return arrays if len(arrays) > 1 else arrays[0]

        s0, = prepare(enc_out, norm_scale, (0,), n, (), (), 0)
        n0 = send(s0, ring)
        *rest, wk, wv, stage = prepare(enc_out, norm_scale, tuple(range(1, n)), n, (s0,), (wk, wv), 1)
        weights = (wk, wv)
        slots = [s0, *rest]
        own = [(slots[i], (0, seq(i)), (0, seq(i + h))) for i in range(n)]
        entry = tuple((PIECE, *where) for _, *where in own[:2])
        state["carry"] = (stage, entry, tuple(range(stage.shape[0])))
        n1 = send(slots[1], ring)
        n2 = send(slots[2], ring)
        run([own[2:4]])

        LEFT, RIGHT = chips - 1, 1
        near = lambda i: ((LEFT, seq(i)), (RIGHT, seq(i + h)))
        far = lambda i: ((2, seq(i)), (2, seq(i + h)))
        mine = lambda p, where: (p, *where)
        theirs = lambda q, where: (q, *where[::-1])

        p0 = hold(n0)
        q0 = send(p0, swap)
        n3, n4, n5 = (send(slots[i], ring) for i in range(3, 6))
        run([own[4:6]])
        p1 = hold(n1)
        q1 = send(p1, swap)
        run([[mine(p0, near(0)), theirs(q0, near(0))]])
        p2 = hold(n2)
        q2 = send(p2, swap)
        f0, f1, f2 = (send(p, ring) for p in (p0, p1, p2))
        run([[mine(p1, near(1)), theirs(q1, near(1))]])
        p3 = hold(n3)
        q3 = send(p3, swap)
        run([[mine(p2, near(2)), theirs(q2, near(2))]])
        run([[mine(p3, near(3)), theirs(q3, near(3))]])
        for i, v, where in ((4, n4, near(4)), (5, n5, near(5)), (6, f0, far(0)), (7, f1, far(1)), (8, f2, far(2))):
            p = hold(v)
            q = send(p, swap)
            run([[mine(p, where)]])
            q = hold(q)
            run([[theirs(q, where)]], keep=i < 8)
        out = state["out"]
        to_cache = lambda o: o.reshape(layers, batch, heads, k, -1).transpose(0, 1, 4, 2, 3)
        return to_cache(out[0]), to_cache(out[1])

    weight_spec = P(None, None, "tp", None)
    cache_spec = P(None, "dp", None, "tp", None)
    step = jax.shard_map(per_device, mesh=mesh, in_specs=(P("dp", "tp", None), P(None), weight_spec, weight_spec), out_specs=(cache_spec, cache_spec), check_vma=False)

    def program(*args):
        jax.eval_shape(step, *args)
        return step(*args)

    return program
```

time: 246 us -> 151 us (0.61)
  Pallas kernels: 0 us -> 105 us
  waiting for transfers between devices: 122 us -> 21.6 us
  matrix products: 87.4 us -> 0 us
  starting transfers between devices: 0.06 us -> 23.6 us
  local copies, waits for them, and re-layouts: 14.7 us -> 0 us
  between operations: 14.1 us -> 1.04 us
  other arithmetic: 7.62 us -> 0 us
    all_gather x1 -> x0, waiting for transfers between devices: 122 us -> none  [per_device(): gathered = lax.all_gather(normed, 'tp', axis=1, tiled=True)]
    pallas_call x0 -> x18, Pallas kernels: none -> 105 us  [the longest x16 86.5 us: project(): pl.pallas_call(functools.partial(project_kernel, plan, len(pieces), (entr...]
    dot_general x2 -> x0, matrix products: 87.4 us -> none  [the longest x1 44.6 us: per_device(): jnp.einsum('bsd,ldhk->lbshk', gathered, w_key, preferred_element_type=jnp...]
    ppermute x0 -> x18, starting transfers between devices: none -> 23.6 us  [send(): return lax.ppermute(v, 'tp', perm)]
    ppermute x0 -> x18, waiting for transfers between devices: none -> 21.6 us  [send(): return lax.ppermute(v, 'tp', perm)]
    unnamed x4 -> x0, local copies, waits for them, and re-layouts: 14.7 us -> none
    convert_element_type x2 -> x0, other arithmetic: 5.04 us -> none  [the longest x1 4.35 us: rms_norm(): (acts * lax.rsqrt(mean_sq + NORM_EPS) * norm_scale.astype(jnp.float32)).a...]
    reduce_sum x1 -> x0, other arithmetic: 2.57 us -> none  [rms_norm(): mean_sq = jnp.mean(acts * acts, axis=-1, keepdims=True)]
  transfers between devices with their start and end apart: 1 -> 18, of which waited for: 1 -> 5; matrix products, arithmetic and copies ran while one was open for 0% -> 0% of each run, Pallas kernels for 0% -> 62%
where the time goes in v2:
time: 151 us
  Pallas kernels  105 us (70%)
  starting transfers between devices  23.6 us (16%)
  waiting for transfers between devices  21.6 us (14%)
    pallas_call x16, Pallas kernels, project(): pl.pallas_call(functools.partial(project_kernel, plan, len(pieces), (entr...  86.5 us
    ppermute x18, starting transfers between devices, send(): return lax.ppermute(v, 'tp', perm)  23.6 us
    ppermute x18, waiting for transfers between devices, send(): return lax.ppermute(v, 'tp', perm)  21.6 us
    pallas_call x2, Pallas kernels, prepare(): pl.pallas_call(functools.partial(prep_kernel, slots, n_slots, len(early),...  18.4 us
  transfers between devices with their start and end apart: 18, of which 5 were waited for; matrix products, arithmetic and copies ran while one was open for 0% of the time, Pallas kernels for 62%

profile of v2, /device:TPU:81, one launch (start us, length us, event | category | flops | bytes accessed | tf_op | source)
XLA Modules:
  0.0 151.2 jit_solution(13448600696471240259)
XLA Ops:
  0.6 5.0 %shard_map.59.refs_2_ = bf16[2,128,2048]{2,1,0:T(8,128)(2,1)S(1)} custom-call(bf16[12,64,2048]{2,1,0:T(8,128)(2,1)} %x_ref.3, bf16[2048]{0:T(1024)(128)(2,1)} %scale_ref.3), custom_call_target="tpu_custom_call" | custom-call | flops 100663296 | bytes 6291456 | tf_op jit(solution)/shard_map/pallas_call | solution.py:153
  5.7 2.4 %collective-permute-start.1 = (bf16[2,128,2048]{2,1,0:T(8,128)(2,1)S(1)}, bf16[2,128,2048]{2,1,0:T(8,128)(2,1)S(1)}, u32[]{:S(2)}, u32[]{:S(2)}) collective-permute-start(bf16[2,128,2048]{2,1,0:T(8,128)(2,1)S(1)} %shard_map.59.refs_2_), channel_id=1, source_target_pairs={{0,2},{1,7},{2,4},{3,1},{4,6},{5,3},{6,0},{7,5},{8,10},{9,15},{10,... | collective-permute-start | bytes 3145736 | tf_op jit(solution)/shard_map/ppermute | solution.py:251
  8.1 13.4 %shard_map.60 = (bf16[2,128,2048]{2,1,0:T(8,128)(2,1)S(1)}, bf16[2,128,2048]{2,1,0:T(8,128)(2,1)S(1)}, bf16[2,128,2048]{2,1,0:T(8,128)(2,1)S(1)}, bf16[2,128,204...) custom-call(bf16[12,64,2048]{2,1,0:T(8,128)(2,1)} %x_ref.3, ...), custom_call_target="tpu_custom_call" | custom-call | flops 100663296 | bytes 6291456 | tf_op jit(solution)/shard_map/pallas_call | solution.py:153
  23.8 7.4 %shard_map.61 = (bf16[6,12,256,512]{3,2,1,0:T(8,128)(2,1)}, bf16[6,12,256,512]{3,2,1,0:T(8,128)(2,1)}, bf16[3,2,2,4,256,128]{5,4,3,2,1,0:T(8,128)(2,1)S(1)}) custom-call(bf16[6,256,2048]{2,1,0:T(8,128)(2,1)S(1)} %get-tuple-element.99.refs_0_, bf16[6,256,2048]{2,1,0:T(8,128)(2,1)S(1)} %get-tuple-element.100.refs_1_, ...), custom_call_target="tpu_custom_call" | custom-call | flops 6442450944 | bytes 5242880 | tf_op jit(solution)/shard_map/pallas_call | solution.py:224
  31.4 7.4 %shard_map.62 = (bf16[6,12,256,512]{3,2,1,0:T(8,128)(2,1)}, bf16[6,12,256,512]{3,2,1,0:T(8,128)(2,1)}, bf16[3,2,2,4,256,128]{5,4,3,2,1,0:T(8,128)(2,1)S(1)}) custom-call(bf16[6,256,2048]{2,1,0:T(8,128)(2,1)S(1)} %get-tuple-element.99.refs_0_, bf16[6,256,2048]{2,1,0:T(8,128)(2,1)S(1)} %get-tuple-element.100.refs_1_, ...), custom_call_target="tpu_custom_call", output_to_operand_aliasing={{0}: (5, {}), {1}: (6, {})} | custom-call | flops 6442450944 | bytes 5242880 | tf_op jit(solution)/shard_map/pallas_call | solution.py:224
  40.9 7.4 %shard_map.63 = (bf16[6,12,256,512]{3,2,1,0:T(8,128)(2,1)}, bf16[6,12,256,512]{3,2,1,0:T(8,128)(2,1)}, bf16[3,2,2,4,256,128]{5,4,3,2,1,0:T(8,128)(2,1)S(1)}) custom-call(bf16[6,256,2048]{2,1,0:T(8,128)(2,1)S(1)} %get-tuple-element.99.refs_0_, bf16[6,256,2048]{2,1,0:T(8,128)(2,1)S(1)} %get-tuple-element.100.refs_1_, ...), custom_call_target="tpu_custom_call", output_to_operand_aliasing={{0}: (5, {}), {1}: (6, {})} | custom-call | flops 6442450944 | bytes 5242880 | tf_op jit(solution)/shard_map/pallas_call | solution.py:224
  49.7 7.4 %shard_map.64 = (bf16[6,12,256,512]{3,2,1,0:T(8,128)(2,1)}, bf16[6,12,256,512]{3,2,1,0:T(8,128)(2,1)}, bf16[3,2,2,4,256,128]{5,4,3,2,1,0:T(8,128)(2,1)S(1)}) custom-call(bf16[6,256,2048]{2,1,0:T(8,128)(2,1)S(1)} %get-tuple-element.99.refs_0_, bf16[6,256,2048]{2,1,0:T(8,128)(2,1)S(1)} %get-tuple-element.100.refs_1_, ...), custom_call_target="tpu_custom_call", output_to_operand_aliasing={{0}: (5, {}), {1}: (6, {})} | custom-call | flops 6442450944 | bytes 5242880 | tf_op jit(solution)/shard_map/pallas_call | solution.py:224
  57.9 3.0 %collective-permute-start.11 = (bf16[2,128,2048]{2,1,0:T(8,128)(2,1)S(1)}, bf16[2,128,2048]{2,1,0:T(8,128)(2,1)S(1)}, u32[]{:S(2)}, u32[]{:S(2)}) collective-permute-start(bf16[2,128,2048]{2,1,0:T(8,128)(2,1)S(1)} %collective-permute-done.9.refs_2_), channel_id=1, source_target_pairs={{0,1},{1,0},{2,3},{3,2},{4,5},{5,4},{6,7},{7,6},{8,9},{9,8},{10,11... | collective-permute-start | bytes 3145736 | tf_op jit(solution)/shard_map/ppermute | solution.py:251
  61.0 7.4 %shard_map.65 = (bf16[6,12,256,512]{3,2,1,0:T(8,128)(2,1)}, bf16[6,12,256,512]{3,2,1,0:T(8,128)(2,1)}, bf16[3,2,2,4,256,128]{5,4,3,2,1,0:T(8,128)(2,1)S(1)}) custom-call(bf16[6,256,2048]{2,1,0:T(8,128)(2,1)S(1)} %get-tuple-element.99.refs_0_, bf16[6,256,2048]{2,1,0:T(8,128)(2,1)S(1)} %get-tuple-element.100.refs_1_, ...), custom_call_target="tpu_custom_call", output_to_operand_aliasing={{0}: (5, {}), {1}: (6, {})} | custom-call | flops 6442450944 | bytes 5242880 | tf_op jit(solution)/shard_map/pallas_call | solution.py:224
  68.4 7.4 %shard_map.66 = (bf16[6,12,256,512]{3,2,1,0:T(8,128)(2,1)}, bf16[6,12,256,512]{3,2,1,0:T(8,128)(2,1)}, bf16[3,2,2,4,256,128]{5,4,3,2,1,0:T(8,128)(2,1)S(1)}) custom-call(bf16[6,256,2048]{2,1,0:T(8,128)(2,1)S(1)} %get-tuple-element.99.refs_0_, bf16[6,256,2048]{2,1,0:T(8,128)(2,1)S(1)} %get-tuple-element.100.refs_1_, ...), custom_call_target="tpu_custom_call", output_to_operand_aliasing={{0}: (5, {}), {1}: (6, {})} | custom-call | flops 6442450944 | bytes 5242880 | tf_op jit(solution)/shard_map/pallas_call | solution.py:224
  78.9 4.1 %shard_map.67 = (bf16[6,12,256,512]{3,2,1,0:T(8,128)(2,1)}, bf16[6,12,256,512]{3,2,1,0:T(8,128)(2,1)}, bf16[3,2,2,2,256,128]{5,4,3,2,1,0:T(8,128)(2,1)S(1)}) custom-call(bf16[6,256,2048]{2,1,0:T(8,128)(2,1)S(1)} %get-tuple-element.99.refs_0_, bf16[6,256,2048]{2,1,0:T(8,128)(2,1)S(1)} %get-tuple-element.100.refs_1_, ...), custom_call_target="tpu_custom_call", output_to_operand_aliasing={{0}: (4, {}), {1}: (5, {})} | custom-call | flops 3221225472 | bytes 2621440 | tf_op jit(solution)/shard_map/pallas_call | solution.py:224
  83.0 4.0 %shard_map.68 = (bf16[6,12,256,512]{3,2,1,0:T(8,128)(2,1)}, bf16[6,12,256,512]{3,2,1,0:T(8,128)(2,1)}, bf16[3,2,2,2,256,128]{5,4,3,2,1,0:T(8,128)(2,1)S(1)}) custom-call(bf16[6,256,2048]{2,1,0:T(8,128)(2,1)S(1)} %get-tuple-element.99.refs_0_, bf16[6,256,2048]{2,1,0:T(8,128)(2,1)S(1)} %get-tuple-element.100.refs_1_, ...), custom_call_target="tpu_custom_call", output_to_operand_aliasing={{0}: (4, {}), {1}: (5, {})} | custom-call | flops 3221225472 | bytes 2621440 | tf_op jit(solution)/shard_map/pallas_call | solution.py:224
  87.0 3.9 %collective-permute-done.7.refs_2_ = bf16[2,128,2048]{2,1,0:T(8,128)(2,1)S(1)} collective-permute-done((bf16[2,128,2048]{2,1,0:T(8,128)(2,1)S(1)}, bf16[2,128,2048]{2,1,0:T(8,128)(2,1)S(1)}, u32[]{:S(2)}, u32[]{:S(2)}) %collective-permute-start.7) | collective-permute-done | bytes 1048608 | tf_op jit(solution)/shard_map/ppermute | solution.py:251
  93.8 4.0 %shard_map.69 = (bf16[6,12,256,512]{3,2,1,0:T(8,128)(2,1)}, bf16[6,12,256,512]{3,2,1,0:T(8,128)(2,1)}, bf16[3,2,2,2,256,128]{5,4,3,2,1,0:T(8,128)(2,1)S(1)}) custom-call(bf16[6,256,2048]{2,1,0:T(8,128)(2,1)S(1)} %get-tuple-element.99.refs_0_, bf16[6,256,2048]{2,1,0:T(8,128)(2,1)S(1)} %get-tuple-element.100.refs_1_, ...), custom_call_target="tpu_custom_call", output_to_operand_aliasing={{0}: (4, {}), {1}: (5, {})} | custom-call | flops 3221225472 | bytes 2621440 | tf_op jit(solution)/shard_map/pallas_call | solution.py:224
  97.8 4.0 %shard_map.70 = (bf16[6,12,256,512]{3,2,1,0:T(8,128)(2,1)}, bf16[6,12,256,512]{3,2,1,0:T(8,128)(2,1)}, bf16[3,2,2,2,256,128]{5,4,3,2,1,0:T(8,128)(2,1)S(1)}) custom-call(bf16[6,256,2048]{2,1,0:T(8,128)(2,1)S(1)} %get-tuple-element.99.refs_0_, bf16[6,256,2048]{2,1,0:T(8,128)(2,1)S(1)} %get-tuple-element.100.refs_1_, ...), custom_call_target="tpu_custom_call", output_to_operand_aliasing={{0}: (4, {}), {1}: (5, {})} | custom-call | flops 3221225472 | bytes 2621440 | tf_op jit(solution)/shard_map/pallas_call | solution.py:224
  101.9 5.1 %collective-permute-done.6.refs_2_ = bf16[2,128,2048]{2,1,0:T(8,128)(2,1)S(1)} collective-permute-done((bf16[2,128,2048]{2,1,0:T(8,128)(2,1)S(1)}, bf16[2,128,2048]{2,1,0:T(8,128)(2,1)S(1)}, u32[]{:S(2)}, u32[]{:S(2)}) %collective-permute-start.6) | collective-permute-done | bytes 1048608 | tf_op jit(solution)/shard_map/ppermute | solution.py:251
  109.1 4.0 %shard_map.71 = (bf16[6,12,256,512]{3,2,1,0:T(8,128)(2,1)}, bf16[6,12,256,512]{3,2,1,0:T(8,128)(2,1)}, bf16[3,2,2,2,256,128]{5,4,3,2,1,0:T(8,128)(2,1)S(1)}) custom-call(bf16[6,256,2048]{2,1,0:T(8,128)(2,1)S(1)} %get-tuple-element.99.refs_0_, bf16[6,256,2048]{2,1,0:T(8,128)(2,1)S(1)} %get-tuple-element.100.refs_1_, ...), custom_call_target="tpu_custom_call", output_to_operand_aliasing={{0}: (4, {}), {1}: (5, {})} | custom-call | flops 3221225472 | bytes 2621440 | tf_op jit(solution)/shard_map/pallas_call | solution.py:224
  113.1 4.0 %shard_map.72 = (bf16[6,12,256,512]{3,2,1,0:T(8,128)(2,1)}, bf16[6,12,256,512]{3,2,1,0:T(8,128)(2,1)}, bf16[3,2,2,2,256,128]{5,4,3,2,1,0:T(8,128)(2,1)S(1)}) custom-call(bf16[6,256,2048]{2,1,0:T(8,128)(2,1)S(1)} %get-tuple-element.99.refs_0_, bf16[6,256,2048]{2,1,0:T(8,128)(2,1)S(1)} %get-tuple-element.100.refs_1_, ...), custom_call_target="tpu_custom_call", output_to_operand_aliasing={{0}: (4, {}), {1}: (5, {})} | custom-call | flops 3221225472 | bytes 2621440 | tf_op jit(solution)/shard_map/pallas_call | solution.py:224
  117.1 5.9 %collective-permute-done.5.refs_2_ = bf16[2,128,2048]{2,1,0:T(8,128)(2,1)S(1)} collective-permute-done((bf16[2,128,2048]{2,1,0:T(8,128)(2,1)S(1)}, bf16[2,128,2048]{2,1,0:T(8,128)(2,1)S(1)}, u32[]{:S(2)}, u32[]{:S(2)}) %collective-permute-start.5) | collective-permute-done | bytes 1048608 | tf_op jit(solution)/shard_map/ppermute | solution.py:251
  125.0 4.0 %shard_map.73 = (bf16[6,12,256,512]{3,2,1,0:T(8,128)(2,1)}, bf16[6,12,256,512]{3,2,1,0:T(8,128)(2,1)}, bf16[3,2,2,2,256,128]{5,4,3,2,1,0:T(8,128)(2,1)S(1)}) custom-call(bf16[6,256,2048]{2,1,0:T(8,128)(2,1)S(1)} %get-tuple-element.99.refs_0_, bf16[6,256,2048]{2,1,0:T(8,128)(2,1)S(1)} %get-tuple-element.100.refs_1_, ...), custom_call_target="tpu_custom_call", output_to_operand_aliasing={{0}: (4, {}), {1}: (5, {})} | custom-call | flops 3221225472 | bytes 2621440 | tf_op jit(solution)/shard_map/pallas_call | solution.py:224
  129.1 4.0 %shard_map.74 = (bf16[6,12,256,512]{3,2,1,0:T(8,128)(2,1)}, bf16[6,12,256,512]{3,2,1,0:T(8,128)(2,1)}, bf16[3,2,2,2,256,128]{5,4,3,2,1,0:T(8,128)(2,1)S(1)}) custom-call(bf16[6,256,2048]{2,1,0:T(8,128)(2,1)S(1)} %get-tuple-element.99.refs_0_, bf16[6,256,2048]{2,1,0:T(8,128)(2,1)S(1)} %get-tuple-element.100.refs_1_, ...), custom_call_target="tpu_custom_call", output_to_operand_aliasing={{0}: (4, {}), {1}: (5, {})} | custom-call | flops 3221225472 | bytes 2621440 | tf_op jit(solution)/shard_map/pallas_call | solution.py:224
  133.1 5.9 %collective-permute-done.4.refs_2_ = bf16[2,128,2048]{2,1,0:T(8,128)(2,1)S(1)} collective-permute-done((bf16[2,128,2048]{2,1,0:T(8,128)(2,1)S(1)}, bf16[2,128,2048]{2,1,0:T(8,128)(2,1)S(1)}, u32[]{:S(2)}, u32[]{:S(2)}) %collective-permute-start.4) | collective-permute-done | bytes 1048608 | tf_op jit(solution)/shard_map/ppermute | solution.py:251
  141.1 4.0 %shard_map.75 = (bf16[6,12,256,512]{3,2,1,0:T(8,128)(2,1)}, bf16[6,12,256,512]{3,2,1,0:T(8,128)(2,1)}, bf16[3,2,2,2,256,128]{5,4,3,2,1,0:T(8,128)(2,1)S(1)}) custom-call(bf16[6,256,2048]{2,1,0:T(8,128)(2,1)S(1)} %get-tuple-element.99.refs_0_, bf16[6,256,2048]{2,1,0:T(8,128)(2,1)S(1)} %get-tuple-element.100.refs_1_, ...), custom_call_target="tpu_custom_call", output_to_operand_aliasing={{0}: (4, {}), {1}: (5, {})} | custom-call | flops 3221225472 | bytes 2621440 | tf_op jit(solution)/shard_map/pallas_call | solution.py:224
  145.1 6.0 %shard_map.76 = (bf16[6,12,256,512]{3,2,1,0:T(8,128)(2,1)}, bf16[6,12,256,512]{3,2,1,0:T(8,128)(2,1)}, bf16[3,2,2,2,256,128]{5,4,3,2,1,0:T(8,128)(2,1)}) custom-call(bf16[6,256,2048]{2,1,0:T(8,128)(2,1)S(1)} %get-tuple-element.99.refs_0_, bf16[6,256,2048]{2,1,0:T(8,128)(2,1)S(1)} %get-tuple-element.100.refs_1_, ...), custom_call_target="tpu_custom_call", output_to_operand_aliasing={{0}: (4, {}), {1}: (5, {})} | custom-call | flops 3221225472 | bytes 2621440 | tf_op jit(solution)/shard_map/pallas_call | solution.py:224
  (30 shorter events, 19.0 us)
Async XLA Ops:
  5.7 25.6 %collective-permute-start.1 = (bf16[2,128,2048]{2,1,0:T(8,128)(2,1)S(1)}, bf16[2,128,2048]{2,1,0:T(8,128)(2,1)S(1)}, u32[]{:S(2)}, u32[]{:S(2)}) collective-permute-start(bf16[2,128,2048]{2,1,0:T(8,128)(2,1)S(1)} %shard_map.59.refs_2_), channel_id=1, source_target_pairs={{0,2},{1,7},{2,4},{3,1},{4,6},{5,3},{6,0},{7,5},{8,10},{9,15},{10,... | collective-permute-start | bytes 3145736 | tf_op jit(solution)/shard_map/ppermute | solution.py:251
  21.4 17.3 %collective-permute-start.3 = (bf16[2,128,2048]{2,1,0:T(8,128)(2,1)S(1)}, bf16[2,128,2048]{2,1,0:T(8,128)(2,1)S(1)}, u32[]{:S(2)}, u32[]{:S(2)}) collective-permute-start(bf16[2,128,2048]{2,1,0:T(8,128)(2,1)S(1)} %get-tuple-element.113), channel_id=1, source_target_pairs={{0,2},{1,7},{2,4},{3,1},{4,6},{5,3},{6,0},{7,5},{8,10},{9,15},{10,... | collective-permute-start | bytes 3145736 | tf_op jit(solution)/shard_map/ppermute | solution.py:251
  22.7 25.5 %collective-permute-start = (bf16[2,128,2048]{2,1,0:T(8,128)(2,1)S(1)}, bf16[2,128,2048]{2,1,0:T(8,128)(2,1)S(1)}, u32[]{:S(2)}, u32[]{:S(2)}) collective-permute-start(bf16[2,128,2048]{2,1,0:T(8,128)(2,1)S(1)} %get-tuple-element.101.refs_2_), channel_id=1, source_target_pairs={{0,2},{1,7},{2,4},{3,1},{4,6},{5,3},{6,0},{7,5},{8,10},{9,15},{10,... | collective-permute-start | bytes 3145736 | tf_op jit(solution)/shard_map/ppermute | solution.py:251
  31.2 9.6 %collective-permute-start.2 = (bf16[2,128,2048]{2,1,0:T(8,128)(2,1)S(1)}, bf16[2,128,2048]{2,1,0:T(8,128)(2,1)S(1)}, u32[]{:S(2)}, u32[]{:S(2)}) collective-permute-start(bf16[2,128,2048]{2,1,0:T(8,128)(2,1)S(1)} %collective-permute-done.1.refs_2_), channel_id=1, source_target_pairs={{0,1},{1,0},{2,3},{3,2},{4,5},{5,4},{6,7},{7,6},{8,9},{9,8},{10,11... | collective-permute-start | bytes 3145736 | tf_op jit(solution)/shard_map/ppermute | solution.py:251
  38.8 10.9 %collective-permute-start.10 = (bf16[2,128,2048]{2,1,0:T(8,128)(2,1)S(1)}, bf16[2,128,2048]{2,1,0:T(8,128)(2,1)S(1)}, u32[]{:S(2)}, u32[]{:S(2)}) collective-permute-start(bf16[2,128,2048]{2,1,0:T(8,128)(2,1)S(1)} %collective-permute-done.3.refs_2_), channel_id=1, source_target_pairs={{0,1},{1,0},{2,3},{3,2},{4,5},{5,4},{6,7},{7,6},{8,9},{9,8},{10,11... | collective-permute-start | bytes 3145736 | tf_op jit(solution)/shard_map/ppermute | solution.py:251
  39.4 18.6 %collective-permute-start.9 = (bf16[2,128,2048]{2,1,0:T(8,128)(2,1)S(1)}, bf16[2,128,2048]{2,1,0:T(8,128)(2,1)S(1)}, u32[]{:S(2)}, u32[]{:S(2)}) collective-permute-start(bf16[2,128,2048]{2,1,0:T(8,128)(2,1)S(1)} %get-tuple-element.102.refs_3_), channel_id=1, source_target_pairs={{0,2},{1,7},{2,4},{3,1},{4,6},{5,3},{6,0},{7,5},{8,10},{9,15},{10,... | collective-permute-start | bytes 3145736 | tf_op jit(solution)/shard_map/ppermute | solution.py:251
  48.3 12.7 %collective-permute-start.12 = (bf16[2,128,2048]{2,1,0:T(8,128)(2,1)S(1)}, bf16[2,128,2048]{2,1,0:T(8,128)(2,1)S(1)}, u32[]{:S(2)}, u32[]{:S(2)}) collective-permute-start(bf16[2,128,2048]{2,1,0:T(8,128)(2,1)S(1)} %collective-permute-done.refs_2_), channel_id=1, source_target_pairs={{0,1},{1,0},{2,3},{3,2},{4,5},{5,4},{6,7},{7,6},{8,9},{9,8},{10,11... | collective-permute-start | bytes 3145736 | tf_op jit(solution)/shard_map/ppermute | solution.py:251
  57.9 10.4 %collective-permute-start.11 = (bf16[2,128,2048]{2,1,0:T(8,128)(2,1)S(1)}, bf16[2,128,2048]{2,1,0:T(8,128)(2,1)S(1)}, u32[]{:S(2)}, u32[]{:S(2)}) collective-permute-start(bf16[2,128,2048]{2,1,0:T(8,128)(2,1)S(1)} %collective-permute-done.9.refs_2_), channel_id=1, source_target_pairs={{0,1},{1,0},{2,3},{3,2},{4,5},{5,4},{6,7},{7,6},{8,9},{9,8},{10,11... | collective-permute-start | bytes 3145736 | tf_op jit(solution)/shard_map/ppermute | solution.py:251
  61.0 14.8 %collective-permute-start.8 = (bf16[2,128,2048]{2,1,0:T(8,128)(2,1)S(1)}, bf16[2,128,2048]{2,1,0:T(8,128)(2,1)S(1)}, u32[]{:S(2)}, u32[]{:S(2)}) collective-permute-start(bf16[2,128,2048]{2,1,0:T(8,128)(2,1)S(1)} %get-tuple-element.107.refs_2_), channel_id=1, source_target_pairs={{0,2},{1,7},{2,4},{3,1},{4,6},{5,3},{6,0},{7,5},{8,10},{9,15},{10,... | collective-permute-start | bytes 3145736 | tf_op jit(solution)/shard_map/ppermute | solution.py:251
  75.8 7.1 %collective-permute-start.13 = (bf16[2,128,2048]{2,1,0:T(8,128)(2,1)S(1)}, bf16[2,128,2048]{2,1,0:T(8,128)(2,1)S(1)}, u32[]{:S(2)}, u32[]{:S(2)}) collective-permute-start(bf16[2,128,2048]{2,1,0:T(8,128)(2,1)S(1)} %collective-permute-done.8.refs_2_), channel_id=1, source_target_pairs={{0,1},{1,0},{2,3},{3,2},{4,5},{5,4},{6,7},{7,6},{8,9},{9,8},{10,11... | collective-permute-start | bytes 3145736 | tf_op jit(solution)/shard_map/ppermute | solution.py:251
  77.0 13.9 %collective-permute-start.7 = (bf16[2,128,2048]{2,1,0:T(8,128)(2,1)S(1)}, bf16[2,128,2048]{2,1,0:T(8,128)(2,1)S(1)}, u32[]{:S(2)}, u32[]{:S(2)}) collective-permute-start(bf16[2,128,2048]{2,1,0:T(8,128)(2,1)S(1)} %get-tuple-element.108.refs_3_), channel_id=1, source_target_pairs={{0,2},{1,7},{2,4},{3,1},{4,6},{5,3},{6,0},{7,5},{8,10},{9,15},{10,... | collective-permute-start | bytes 3145736 | tf_op jit(solution)/shard_map/ppermute | solution.py:251
  90.9 6.9 %collective-permute-start.14 = (bf16[2,128,2048]{2,1,0:T(8,128)(2,1)S(1)}, bf16[2,128,2048]{2,1,0:T(8,128)(2,1)S(1)}, u32[]{:S(2)}, u32[]{:S(2)}) collective-permute-start(bf16[2,128,2048]{2,1,0:T(8,128)(2,1)S(1)} %collective-permute-done.7.refs_2_), channel_id=1, source_target_pairs={{0,1},{1,0},{2,3},{3,2},{4,5},{5,4},{6,7},{7,6},{8,9},{9,8},{10,11... | collective-permute-start | bytes 3145736 | tf_op jit(solution)/shard_map/ppermute | solution.py:251
  93.0 13.9 %collective-permute-start.6 = (bf16[2,128,2048]{2,1,0:T(8,128)(2,1)S(1)}, bf16[2,128,2048]{2,1,0:T(8,128)(2,1)S(1)}, u32[]{:S(2)}, u32[]{:S(2)}) collective-permute-start(bf16[2,128,2048]{2,1,0:T(8,128)(2,1)S(1)} %collective-permute-done.1.refs_2_), channel_id=1, source_target_pairs={{0,2},{1,7},{2,4},{3,1},{4,6},{5,3},{6,0},{7,5},{8,10},{9,15},{10,... | collective-permute-start | bytes 3145736 | tf_op jit(solution)/shard_map/ppermute | solution.py:251
  107.0 6.1 %collective-permute-start.15 = (bf16[2,128,2048]{2,1,0:T(8,128)(2,1)S(1)}, bf16[2,128,2048]{2,1,0:T(8,128)(2,1)S(1)}, u32[]{:S(2)}, u32[]{:S(2)}) collective-permute-start(bf16[2,128,2048]{2,1,0:T(8,128)(2,1)S(1)} %collective-permute-done.6.refs_2_), channel_id=1, source_target_pairs={{0,1},{1,0},{2,3},{3,2},{4,5},{5,4},{6,7},{7,6},{8,9},{9,8},{10,11... | collective-permute-start | bytes 3145736 | tf_op jit(solution)/shard_map/ppermute | solution.py:251
  109.0 13.9 %collective-permute-start.5 = (bf16[2,128,2048]{2,1,0:T(8,128)(2,1)S(1)}, bf16[2,128,2048]{2,1,0:T(8,128)(2,1)S(1)}, u32[]{:S(2)}, u32[]{:S(2)}) collective-permute-start(bf16[2,128,2048]{2,1,0:T(8,128)(2,1)S(1)} %collective-permute-done.3.refs_2_), channel_id=1, source_target_pairs={{0,2},{1,7},{2,4},{3,1},{4,6},{5,3},{6,0},{7,5},{8,10},{9,15},{10,... | collective-permute-start | bytes 3145736 | tf_op jit(solution)/shard_map/ppermute | solution.py:251
  123.0 6.1 %collective-permute-start.16 = (bf16[2,128,2048]{2,1,0:T(8,128)(2,1)S(1)}, bf16[2,128,2048]{2,1,0:T(8,128)(2,1)S(1)}, u32[]{:S(2)}, u32[]{:S(2)}) collective-permute-start(bf16[2,128,2048]{2,1,0:T(8,128)(2,1)S(1)} %collective-permute-done.5.refs_2_), channel_id=1, source_target_pairs={{0,1},{1,0},{2,3},{3,2},{4,5},{5,4},{6,7},{7,6},{8,9},{9,8},{10,11... | collective-permute-start | bytes 3145736 | tf_op jit(solution)/shard_map/ppermute | solution.py:251
  125.0 13.9 %collective-permute-start.4 = (bf16[2,128,2048]{2,1,0:T(8,128)(2,1)S(1)}, bf16[2,128,2048]{2,1,0:T(8,128)(2,1)S(1)}, u32[]{:S(2)}, u32[]{:S(2)}) collective-permute-start(bf16[2,128,2048]{2,1,0:T(8,128)(2,1)S(1)} %collective-permute-done.refs_2_), channel_id=1, source_target_pairs={{0,2},{1,7},{2,4},{3,1},{4,6},{5,3},{6,0},{7,5},{8,10},{9,15},{10,... | collective-permute-start | bytes 3145736 | tf_op jit(solution)/shard_map/ppermute | solution.py:251
  139.0 6.1 %collective-permute-start.17 = (bf16[2,128,2048]{2,1,0:T(8,128)(2,1)S(1)}, bf16[2,128,2048]{2,1,0:T(8,128)(2,1)S(1)}, u32[]{:S(2)}, u32[]{:S(2)}) collective-permute-start(bf16[2,128,2048]{2,1,0:T(8,128)(2,1)S(1)} %collective-permute-done.4.refs_2_), channel_id=1, source_target_pairs={{0,1},{1,0},{2,3},{3,2},{4,5},{5,4},{6,7},{7,6},{8,9},{9,8},{10,11... | collective-permute-start | bytes 3145736 | tf_op jit(solution)/shard_map/ppermute | solution.py:251

commit v3 on v2

--- a/solution.py
+++ b/solution.py
@@ -122,19 +122,15 @@
         send(pending).start()
         sent.append(pending)
     if n_weights:
-        first = sent[0]
-        send(first).wait_recv()
 
         @pl.loop(0, stage.shape[0])
         def _(c):
             for kv in range(n_weights):
                 load_weights(kv, c).wait()
-            matmul_block(w_out, [*made, outs[slots.index(there(needed[first]))]], stage, c)
+            matmul_block(w_out, made, stage, c)
 
     for j in sent:
-        send(j).wait_send()
-        if not n_weights or j != first:
-            send(j).wait_recv()
+        send(j).wait()
 
 
 def stage_shape(weights, seqs, group):
@@ -149,7 +145,7 @@
     piece = jax.ShapeDtypeStruct((PIECE, 2 * half, d), x.dtype)
     out_shape = (piece,) * len(slots) + tuple(jax.ShapeDtypeStruct(w.shape, w.dtype) for w in weights)
     if weights:
-        out_shape += (stage_shape(weights, PIECE * (len(early) + 1), 2 * half),)
+        out_shape += (stage_shape(weights, PIECE * len(early), 2 * half),)
     return pl.pallas_call(
         functools.partial(prep_kernel, slots, n_slots, len(early), len(weights)),
         out_shape=out_shape,
@@ -173,8 +169,7 @@
     w_refs, refs = refs[:2], refs[2:]
     pieces, refs = refs[:n_pieces], refs[n_pieces:]
     before, refs = refs[0], refs[1 + n_alias:]
-    outs, stage, refs = refs[:2], refs[2], refs[3:]
-    sem, before_sem = refs
+    outs, (stage, sem, before_sem) = refs[:2], refs[2:]
     chunks, _, per = stage.shape[:3]
     entry, old_chunks = carried
     late = [copy for c in old_chunks for copy in output_copies(outs, before, before_sem, entry, c, per)]
@@ -221,13 +216,13 @@
     stage = stage_shape(weights, sum(n for n, *_ in plan[0]), group)
     before, entry, chunks = carry
     tok = sum(p.shape[0] for p in pieces) * group
-    *out, stage_out = pl.pallas_call(
+    *out, = pl.pallas_call(
         functools.partial(project_kernel, plan, len(pieces), (entry, chunks), n_alias, keep),
-        out_shape=(shape, shape, stage),
+        out_shape=(shape, shape) + (stage,) * keep,
         in_specs=[VMEM] * n_in + [ANY] * n_alias,
-        out_specs=(ANY, ANY, VMEM),
+        out_specs=(ANY, ANY) + (VMEM,) * keep,
         input_output_aliases={n_in + i: i for i in range(n_alias)},
-        scratch_shapes=[
+        scratch_shapes=[pltpu.VMEM(stage.shape, stage.dtype)] * (not keep) + [
             pltpu.SemaphoreType.DMA((stage.shape[0], 2, len(plan[0]))),
             pltpu.SemaphoreType.DMA((stage.shape[0], 2, len(entry))),
         ],
@@ -238,7 +233,7 @@
             transcendentals=0,
         ),
     )(*weights, *pieces, before, *(out or ()))
-    return out, (stage_out, plan[-1], (stage.shape[0] - 1,))
+    return out[:2], (out[-1], plan[-1], (stage.shape[0] - 1,))
 
 
 def solution(mesh):
@@ -268,16 +263,15 @@
             arrays, state["out"] = lax.optimization_barrier((arrays, state["out"]))
             return arrays if len(arrays) > 1 else arrays[0]
 
-        s0, = prepare(enc_out, norm_scale, (0,), n, (), (), 0)
-        n0 = send(s0, ring)
-        *rest, wk, wv, stage = prepare(enc_out, norm_scale, tuple(range(1, n)), n, (s0,), (wk, wv), 1)
+        s0, s1 = prepare(enc_out, norm_scale, (0, 1), n, (), (), 0)
+        n0, n1 = send(s0, ring), send(s1, ring)
+        *rest, wk, wv, stage = prepare(enc_out, norm_scale, tuple(range(2, n)), n, (s0, s1), (wk, wv), 1)
         weights = (wk, wv)
-        slots = [s0, *rest]
+        slots = [s0, s1, *rest]
         own = [(slots[i], (0, seq(i)), (0, seq(i + h))) for i in range(n)]
         entry = tuple((PIECE, *where) for _, *where in own[:2])
         state["carry"] = (stage, entry, tuple(range(stage.shape[0])))
-        n1 = send(slots[1], ring)
-        n2 = send(slots[2], ring)
+        n2, n3 = send(slots[2], ring), send(slots[3], ring)
         run([own[2:4]])
 
         LEFT, RIGHT = chips - 1, 1
@@ -288,18 +282,19 @@
 
         p0 = hold(n0)
         q0 = send(p0, swap)
-        n3, n4, n5 = (send(slots[i], ring) for i in range(3, 6))
         run([own[4:6]])
         p1 = hold(n1)
+        n4, n5 = send(slots[4], ring), send(slots[5], ring)
         q1 = send(p1, swap)
         run([[mine(p0, near(0)), theirs(q0, near(0))]])
         p2 = hold(n2)
         q2 = send(p2, swap)
-        f0, f1, f2 = (send(p, ring) for p in (p0, p1, p2))
         run([[mine(p1, near(1)), theirs(q1, near(1))]])
         p3 = hold(n3)
         q3 = send(p3, swap)
         run([[mine(p2, near(2)), theirs(q2, near(2))]])
+        p0, p1, p2 = hold(p0, p1, p2)
+        f0, f1, f2 = (send(p, ring) for p in (p0, p1, p2))
         run([[mine(p3, near(3)), theirs(q3, near(3))]])
         for i, v, where in ((4, n4, near(4)), (5, n5, near(5)), (6, f0, far(0)), (7, f1, far(1)), (8, f2, far(2))):
             p = hold(v)

time: 151 us -> 146 us (0.967)
  starting transfers between devices: 23.6 us -> 19.3 us
    ppermute x18, starting transfers between devices: 23.6 us -> 19.3 us  [send(): return lax.ppermute(v, 'tp', perm)]
  transfers between devices with their start and end apart: 18 -> 18, of which waited for: 5 -> 4; matrix products, arithmetic and copies ran while one was open for 0% -> 0% of each run, Pallas kernels for 62% -> 64%
where the time goes in v3:
time: 146 us
  Pallas kernels  104 us (71%)
  waiting for transfers between devices  21.4 us (15%)
  starting transfers between devices  19.3 us (13%)
    pallas_call x16, Pallas kernels, project(): pl.pallas_call(functools.partial(project_kernel, plan, len(pieces), (entr...  85.4 us
    ppermute x18, waiting for transfers between devices, send(): return lax.ppermute(v, 'tp', perm)  21.4 us
    ppermute x18, starting transfers between devices, send(): return lax.ppermute(v, 'tp', perm)  19.3 us
    pallas_call x2, Pallas kernels, prepare(): pl.pallas_call(functools.partial(prep_kernel, slots, n_slots, len(early),...  19 us
  transfers between devices with their start and end apart: 18, of which 4 were waited for; matrix products, arithmetic and copies ran while one was open for 0% of the time, Pallas kernels for 64%

profile of v3, /device:TPU:81, one launch (start us, length us, event | category | flops | bytes accessed | tf_op | source)
XLA Modules:
  0.0 146.0 jit_solution(11291542562677021849)
XLA Ops:
  0.6 5.8 %shard_map.59 = (bf16[2,128,2048]{2,1,0:T(8,128)(2,1)S(1)}, bf16[2,128,2048]{2,1,0:T(8,128)(2,1)S(1)}) custom-call(bf16[12,64,2048]{2,1,0:T(8,128)(2,1)} %x_ref.3, bf16[2048]{0:T(1024)(128)(2,1)} %scale_ref.3), custom_call_target="tpu_custom_call" | custom-call | flops 100663296 | bytes 6291456 | tf_op jit(solution)/shard_map/pallas_call | solution.py:149
  6.5 2.4 %collective-permute-start = (bf16[2,128,2048]{2,1,0:T(8,128)(2,1)S(1)}, bf16[2,128,2048]{2,1,0:T(8,128)(2,1)S(1)}, u32[]{:S(2)}, u32[]{:S(2)}) collective-permute-start(bf16[2,128,2048]{2,1,0:T(8,128)(2,1)S(1)} %get-tuple-element.105.refs_2_), channel_id=1, source_target_pairs={{0,2},{1,7},{2,4},{3,1},{4,6},{5,3},{6,0},{7,5},{8,10},{9,15},{10,... | collective-permute-start | bytes 3145736 | tf_op jit(solution)/shard_map/ppermute | solution.py:246
  9.2 13.1 %shard_map.60 = (bf16[2,128,2048]{2,1,0:T(8,128)(2,1)S(1)}, bf16[2,128,2048]{2,1,0:T(8,128)(2,1)S(1)}, bf16[2,128,2048]{2,1,0:T(8,128)(2,1)S(1)}, bf16[2,128,204...) custom-call(bf16[12,64,2048]{2,1,0:T(8,128)(2,1)} %x_ref.3, ...), custom_call_target="tpu_custom_call" | custom-call | flops 100663296 | bytes 6291456 | tf_op jit(solution)/shard_map/pallas_call | solution.py:149
  22.6 7.4 %shard_map.61 = (bf16[6,12,256,512]{3,2,1,0:T(8,128)(2,1)}, bf16[6,12,256,512]{3,2,1,0:T(8,128)(2,1)}, bf16[3,2,2,4,256,128]{5,4,3,2,1,0:T(8,128)(2,1)S(1)}) custom-call(bf16[6,256,2048]{2,1,0:T(8,128)(2,1)S(1)} %get-tuple-element.107.refs_0_, bf16[6,256,2048]{2,1,0:T(8,128)(2,1)S(1)} %get-tuple-element.108.refs_1_, ...), custom_call_target="tpu_custom_call" | custom-call | flops 6442450944 | bytes 5242880 | tf_op jit(solution)/shard_map/pallas_call | solution.py:219
  31.4 7.4 %shard_map.62 = (bf16[6,12,256,512]{3,2,1,0:T(8,128)(2,1)}, bf16[6,12,256,512]{3,2,1,0:T(8,128)(2,1)}, bf16[3,2,2,4,256,128]{5,4,3,2,1,0:T(8,128)(2,1)S(1)}) custom-call(bf16[6,256,2048]{2,1,0:T(8,128)(2,1)S(1)} %get-tuple-element.107.refs_0_, bf16[6,256,2048]{2,1,0:T(8,128)(2,1)S(1)} %get-tuple-element.108.refs_1_, ...), custom_call_target="tpu_custom_call", output_to_operand_aliasing={{0}: (5, {}), {1}: (6, {})} | custom-call | flops 6442450944 | bytes 5242880 | tf_op jit(solution)/shard_map/pallas_call | solution.py:219
  40.9 7.4 %shard_map.63 = (bf16[6,12,256,512]{3,2,1,0:T(8,128)(2,1)}, bf16[6,12,256,512]{3,2,1,0:T(8,128)(2,1)}, bf16[3,2,2,4,256,128]{5,4,3,2,1,0:T(8,128)(2,1)S(1)}) custom-call(bf16[6,256,2048]{2,1,0:T(8,128)(2,1)S(1)} %get-tuple-element.107.refs_0_, bf16[6,256,2048]{2,1,0:T(8,128)(2,1)S(1)} %get-tuple-element.108.refs_1_, ...), custom_call_target="tpu_custom_call", output_to_operand_aliasing={{0}: (5, {}), {1}: (6, {})} | custom-call | flops 6442450944 | bytes 5242880 | tf_op jit(solution)/shard_map/pallas_call | solution.py:219
  48.4 7.4 %shard_map.64 = (bf16[6,12,256,512]{3,2,1,0:T(8,128)(2,1)}, bf16[6,12,256,512]{3,2,1,0:T(8,128)(2,1)}, bf16[3,2,2,4,256,128]{5,4,3,2,1,0:T(8,128)(2,1)S(1)}) custom-call(bf16[6,256,2048]{2,1,0:T(8,128)(2,1)S(1)} %get-tuple-element.107.refs_0_, bf16[6,256,2048]{2,1,0:T(8,128)(2,1)S(1)} %get-tuple-element.108.refs_1_, ...), custom_call_target="tpu_custom_call", output_to_operand_aliasing={{0}: (5, {}), {1}: (6, {})} | custom-call | flops 6442450944 | bytes 5242880 | tf_op jit(solution)/shard_map/pallas_call | solution.py:219
  57.5 7.4 %shard_map.65 = (bf16[6,12,256,512]{3,2,1,0:T(8,128)(2,1)}, bf16[6,12,256,512]{3,2,1,0:T(8,128)(2,1)}, bf16[3,2,2,4,256,128]{5,4,3,2,1,0:T(8,128)(2,1)S(1)}) custom-call(bf16[6,256,2048]{2,1,0:T(8,128)(2,1)S(1)} %get-tuple-element.107.refs_0_, bf16[6,256,2048]{2,1,0:T(8,128)(2,1)S(1)} %get-tuple-element.108.refs_1_, ...), custom_call_target="tpu_custom_call", output_to_operand_aliasing={{0}: (5, {}), {1}: (6, {})} | custom-call | flops 6442450944 | bytes 5242880 | tf_op jit(solution)/shard_map/pallas_call | solution.py:219
  64.9 7.4 %shard_map.66 = (bf16[6,12,256,512]{3,2,1,0:T(8,128)(2,1)}, bf16[6,12,256,512]{3,2,1,0:T(8,128)(2,1)}, bf16[3,2,2,4,256,128]{5,4,3,2,1,0:T(8,128)(2,1)S(1)}) custom-call(bf16[6,256,2048]{2,1,0:T(8,128)(2,1)S(1)} %get-tuple-element.107.refs_0_, bf16[6,256,2048]{2,1,0:T(8,128)(2,1)S(1)} %get-tuple-element.108.refs_1_, ...), custom_call_target="tpu_custom_call", output_to_operand_aliasing={{0}: (5, {}), {1}: (6, {})} | custom-call | flops 6442450944 | bytes 5242880 | tf_op jit(solution)/shard_map/pallas_call | solution.py:219
  74.4 4.1 %shard_map.67 = (bf16[6,12,256,512]{3,2,1,0:T(8,128)(2,1)}, bf16[6,12,256,512]{3,2,1,0:T(8,128)(2,1)}, bf16[3,2,2,2,256,128]{5,4,3,2,1,0:T(8,128)(2,1)S(1)}) custom-call(bf16[6,256,2048]{2,1,0:T(8,128)(2,1)S(1)} %get-tuple-element.107.refs_0_, bf16[6,256,2048]{2,1,0:T(8,128)(2,1)S(1)} %get-tuple-element.108.refs_1_, ...), custom_call_target="tpu_custom_call", output_to_operand_aliasing={{0}: (4, {}), {1}: (5, {})} | custom-call | flops 3221225472 | bytes 2621440 | tf_op jit(solution)/shard_map/pallas_call | solution.py:219
  78.5 4.0 %shard_map.68 = (bf16[6,12,256,512]{3,2,1,0:T(8,128)(2,1)}, bf16[6,12,256,512]{3,2,1,0:T(8,128)(2,1)}, bf16[3,2,2,2,256,128]{5,4,3,2,1,0:T(8,128)(2,1)S(1)}) custom-call(bf16[6,256,2048]{2,1,0:T(8,128)(2,1)S(1)} %get-tuple-element.107.refs_0_, bf16[6,256,2048]{2,1,0:T(8,128)(2,1)S(1)} %get-tuple-element.108.refs_1_, ...), custom_call_target="tpu_custom_call", output_to_operand_aliasing={{0}: (4, {}), {1}: (5, {})} | custom-call | flops 3221225472 | bytes 2621440 | tf_op jit(solution)/shard_map/pallas_call | solution.py:219
  82.5 4.0 %collective-permute-done.10.refs_2_ = bf16[2,128,2048]{2,1,0:T(8,128)(2,1)S(1)} collective-permute-done((bf16[2,128,2048]{2,1,0:T(8,128)(2,1)S(1)}, bf16[2,128,2048]{2,1,0:T(8,128)(2,1)S(1)}, u32[]{:S(2)}, u32[]{:S(2)}) %collective-permute-start.10) | collective-permute-done | bytes 1048608 | tf_op jit(solution)/shard_map/ppermute | solution.py:246
  86.5 2.5 %collective-permute-start.14 = (bf16[2,128,2048]{2,1,0:T(8,128)(2,1)S(1)}, bf16[2,128,2048]{2,1,0:T(8,128)(2,1)S(1)}, u32[]{:S(2)}, u32[]{:S(2)}) collective-permute-start(bf16[2,128,2048]{2,1,0:T(8,128)(2,1)S(1)} %collective-permute-done.10.refs_2_), channel_id=1, source_target_pairs={{0,1},{1,0},{2,3},{3,2},{4,5},{5,4},{6,7},{7,6},{8,9},{9,8},{10,11... | collective-permute-start | bytes 3145736 | tf_op jit(solution)/shard_map/ppermute | solution.py:246
  89.3 4.0 %shard_map.69 = (bf16[6,12,256,512]{3,2,1,0:T(8,128)(2,1)}, bf16[6,12,256,512]{3,2,1,0:T(8,128)(2,1)}, bf16[3,2,2,2,256,128]{5,4,3,2,1,0:T(8,128)(2,1)S(1)}) custom-call(bf16[6,256,2048]{2,1,0:T(8,128)(2,1)S(1)} %get-tuple-element.107.refs_0_, bf16[6,256,2048]{2,1,0:T(8,128)(2,1)S(1)} %get-tuple-element.108.refs_1_, ...), custom_call_target="tpu_custom_call", output_to_operand_aliasing={{0}: (4, {}), {1}: (5, {})} | custom-call | flops 3221225472 | bytes 2621440 | tf_op jit(solution)/shard_map/pallas_call | solution.py:219
  93.4 4.0 %shard_map.70 = (bf16[6,12,256,512]{3,2,1,0:T(8,128)(2,1)}, bf16[6,12,256,512]{3,2,1,0:T(8,128)(2,1)}, bf16[3,2,2,2,256,128]{5,4,3,2,1,0:T(8,128)(2,1)S(1)}) custom-call(bf16[6,256,2048]{2,1,0:T(8,128)(2,1)S(1)} %get-tuple-element.107.refs_0_, bf16[6,256,2048]{2,1,0:T(8,128)(2,1)S(1)} %get-tuple-element.108.refs_1_, ...), custom_call_target="tpu_custom_call", output_to_operand_aliasing={{0}: (4, {}), {1}: (5, {})} | custom-call | flops 3221225472 | bytes 2621440 | tf_op jit(solution)/shard_map/pallas_call | solution.py:219
  97.4 5.5 %collective-permute-done.9.refs_2_ = bf16[2,128,2048]{2,1,0:T(8,128)(2,1)S(1)} collective-permute-done((bf16[2,128,2048]{2,1,0:T(8,128)(2,1)S(1)}, bf16[2,128,2048]{2,1,0:T(8,128)(2,1)S(1)}, u32[]{:S(2)}, u32[]{:S(2)}) %collective-permute-start.9) | collective-permute-done | bytes 1048608 | tf_op jit(solution)/shard_map/ppermute | solution.py:246
  105.0 4.0 %shard_map.71 = (bf16[6,12,256,512]{3,2,1,0:T(8,128)(2,1)}, bf16[6,12,256,512]{3,2,1,0:T(8,128)(2,1)}, bf16[3,2,2,2,256,128]{5,4,3,2,1,0:T(8,128)(2,1)S(1)}) custom-call(bf16[6,256,2048]{2,1,0:T(8,128)(2,1)S(1)} %get-tuple-element.107.refs_0_, bf16[6,256,2048]{2,1,0:T(8,128)(2,1)S(1)} %get-tuple-element.108.refs_1_, ...), custom_call_target="tpu_custom_call", output_to_operand_aliasing={{0}: (4, {}), {1}: (5, {})} | custom-call | flops 3221225472 | bytes 2621440 | tf_op jit(solution)/shard_map/pallas_call | solution.py:219
  109.0 4.0 %shard_map.72 = (bf16[6,12,256,512]{3,2,1,0:T(8,128)(2,1)}, bf16[6,12,256,512]{3,2,1,0:T(8,128)(2,1)}, bf16[3,2,2,2,256,128]{5,4,3,2,1,0:T(8,128)(2,1)S(1)}) custom-call(bf16[6,256,2048]{2,1,0:T(8,128)(2,1)S(1)} %get-tuple-element.107.refs_0_, bf16[6,256,2048]{2,1,0:T(8,128)(2,1)S(1)} %get-tuple-element.108.refs_1_, ...), custom_call_target="tpu_custom_call", output_to_operand_aliasing={{0}: (4, {}), {1}: (5, {})} | custom-call | flops 3221225472 | bytes 2621440 | tf_op jit(solution)/shard_map/pallas_call | solution.py:219
  113.1 5.9 %collective-permute-done.8.refs_2_ = bf16[2,128,2048]{2,1,0:T(8,128)(2,1)S(1)} collective-permute-done((bf16[2,128,2048]{2,1,0:T(8,128)(2,1)S(1)}, bf16[2,128,2048]{2,1,0:T(8,128)(2,1)S(1)}, u32[]{:S(2)}, u32[]{:S(2)}) %collective-permute-start.8) | collective-permute-done | bytes 1048608 | tf_op jit(solution)/shard_map/ppermute | solution.py:246
  121.0 4.0 %shard_map.73 = (bf16[6,12,256,512]{3,2,1,0:T(8,128)(2,1)}, bf16[6,12,256,512]{3,2,1,0:T(8,128)(2,1)}, bf16[3,2,2,2,256,128]{5,4,3,2,1,0:T(8,128)(2,1)S(1)}) custom-call(bf16[6,256,2048]{2,1,0:T(8,128)(2,1)S(1)} %get-tuple-element.107.refs_0_, bf16[6,256,2048]{2,1,0:T(8,128)(2,1)S(1)} %get-tuple-element.108.refs_1_, ...), custom_call_target="tpu_custom_call", output_to_operand_aliasing={{0}: (4, {}), {1}: (5, {})} | custom-call | flops 3221225472 | bytes 2621440 | tf_op jit(solution)/shard_map/pallas_call | solution.py:219
  125.0 4.0 %shard_map.74 = (bf16[6,12,256,512]{3,2,1,0:T(8,128)(2,1)}, bf16[6,12,256,512]{3,2,1,0:T(8,128)(2,1)}, bf16[3,2,2,2,256,128]{5,4,3,2,1,0:T(8,128)(2,1)S(1)}) custom-call(bf16[6,256,2048]{2,1,0:T(8,128)(2,1)S(1)} %get-tuple-element.107.refs_0_, bf16[6,256,2048]{2,1,0:T(8,128)(2,1)S(1)} %get-tuple-element.108.refs_1_, ...), custom_call_target="tpu_custom_call", output_to_operand_aliasing={{0}: (4, {}), {1}: (5, {})} | custom-call | flops 3221225472 | bytes 2621440 | tf_op jit(solution)/shard_map/pallas_call | solution.py:219
  129.1 5.9 %collective-permute-done.7.refs_2_ = bf16[2,128,2048]{2,1,0:T(8,128)(2,1)S(1)} collective-permute-done((bf16[2,128,2048]{2,1,0:T(8,128)(2,1)S(1)}, bf16[2,128,2048]{2,1,0:T(8,128)(2,1)S(1)}, u32[]{:S(2)}, u32[]{:S(2)}) %collective-permute-start.7) | collective-permute-done | bytes 1048608 | tf_op jit(solution)/shard_map/ppermute | solution.py:246
  137.0 4.0 %shard_map.75 = (bf16[6,12,256,512]{3,2,1,0:T(8,128)(2,1)}, bf16[6,12,256,512]{3,2,1,0:T(8,128)(2,1)}, bf16[3,2,2,2,256,128]{5,4,3,2,1,0:T(8,128)(2,1)S(1)}) custom-call(bf16[6,256,2048]{2,1,0:T(8,128)(2,1)S(1)} %get-tuple-element.107.refs_0_, bf16[6,256,2048]{2,1,0:T(8,128)(2,1)S(1)} %get-tuple-element.108.refs_1_, ...), custom_call_target="tpu_custom_call", output_to_operand_aliasing={{0}: (4, {}), {1}: (5, {})} | custom-call | flops 3221225472 | bytes 2621440 | tf_op jit(solution)/shard_map/pallas_call | solution.py:219
  141.1 4.8 %shard_map.76 = (bf16[6,12,256,512]{3,2,1,0:T(8,128)(2,1)}, bf16[6,12,256,512]{3,2,1,0:T(8,128)(2,1)}) custom-call(bf16[6,256,2048]{2,1,0:T(8,128)(2,1)S(1)} %get-tuple-element.107.refs_0_, bf16[6,256,2048]{2,1,0:T(8,128)(2,1)S(1)} %get-tuple-element.108.refs_1_, ...), custom_call_target="tpu_custom_call", output_to_operand_aliasing={{0}: (4, {}), {1}: (5, {})} | custom-call | flops 3221225472 | bytes 2621440 | tf_op jit(solution)/shard_map/pallas_call | solution.py:219
  (30 shorter events, 14.5 us)
Async XLA Ops:
  6.5 23.5 %collective-permute-start = (bf16[2,128,2048]{2,1,0:T(8,128)(2,1)S(1)}, bf16[2,128,2048]{2,1,0:T(8,128)(2,1)S(1)}, u32[]{:S(2)}, u32[]{:S(2)}) collective-permute-start(bf16[2,128,2048]{2,1,0:T(8,128)(2,1)S(1)} %get-tuple-element.105.refs_2_), channel_id=1, source_target_pairs={{0,2},{1,7},{2,4},{3,1},{4,6},{5,3},{6,0},{7,5},{8,10},{9,15},{10,... | collective-permute-start | bytes 3145736 | tf_op jit(solution)/shard_map/ppermute | solution.py:246
  8.8 30.0 %collective-permute-start.1 = (bf16[2,128,2048]{2,1,0:T(8,128)(2,1)S(1)}, bf16[2,128,2048]{2,1,0:T(8,128)(2,1)S(1)}, u32[]{:S(2)}, u32[]{:S(2)}) collective-permute-start(bf16[2,128,2048]{2,1,0:T(8,128)(2,1)S(1)} %get-tuple-element.106.refs_3_), channel_id=1, source_target_pairs={{0,2},{1,7},{2,4},{3,1},{4,6},{5,3},{6,0},{7,5},{8,10},{9,15},{10,... | collective-permute-start | bytes 3145736 | tf_op jit(solution)/shard_map/ppermute | solution.py:246
  22.4 25.9 %collective-permute-start.2 = (bf16[2,128,2048]{2,1,0:T(8,128)(2,1)S(1)}, bf16[2,128,2048]{2,1,0:T(8,128)(2,1)S(1)}, u32[]{:S(2)}, u32[]{:S(2)}) collective-permute-start(bf16[2,128,2048]{2,1,0:T(8,128)(2,1)S(1)} %get-tuple-element.109.refs_2_), channel_id=1, source_target_pairs={{0,2},{1,7},{2,4},{3,1},{4,6},{5,3},{6,0},{7,5},{8,10},{9,15},{10,... | collective-permute-start | bytes 3145736 | tf_op jit(solution)/shard_map/ppermute | solution.py:246
  30.0 10.9 %collective-permute-start.3 = (bf16[2,128,2048]{2,1,0:T(8,128)(2,1)S(1)}, bf16[2,128,2048]{2,1,0:T(8,128)(2,1)S(1)}, u32[]{:S(2)}, u32[]{:S(2)}) collective-permute-start(bf16[2,128,2048]{2,1,0:T(8,128)(2,1)S(1)} %collective-permute-done.refs_2_), channel_id=1, source_target_pairs={{0,1},{1,0},{2,3},{3,2},{4,5},{5,4},{6,7},{7,6},{8,9},{9,8},{10,11... | collective-permute-start | bytes 3145736 | tf_op jit(solution)/shard_map/ppermute | solution.py:246
  38.8 9.6 %collective-permute-start.5 = (bf16[2,128,2048]{2,1,0:T(8,128)(2,1)S(1)}, bf16[2,128,2048]{2,1,0:T(8,128)(2,1)S(1)}, u32[]{:S(2)}, u32[]{:S(2)}) collective-permute-start(bf16[2,128,2048]{2,1,0:T(8,128)(2,1)S(1)} %collective-permute-done.1.refs_2_), channel_id=1, source_target_pairs={{0,1},{1,0},{2,3},{3,2},{4,5},{5,4},{6,7},{7,6},{8,9},{9,8},{10,11... | collective-permute-start | bytes 3145736 | tf_op jit(solution)/shard_map/ppermute | solution.py:246
  39.0 16.9 %collective-permute-start.6 = (bf16[2,128,2048]{2,1,0:T(8,128)(2,1)S(1)}, bf16[2,128,2048]{2,1,0:T(8,128)(2,1)S(1)}, u32[]{:S(2)}, u32[]{:S(2)}) collective-permute-start(bf16[2,128,2048]{2,1,0:T(8,128)(2,1)S(1)} %get-tuple-element.110.refs_3_), channel_id=1, source_target_pairs={{0,2},{1,7},{2,4},{3,1},{4,6},{5,3},{6,0},{7,5},{8,10},{9,15},{10,... | collective-permute-start | bytes 3145736 | tf_op jit(solution)/shard_map/ppermute | solution.py:246
  48.3 9.3 %collective-permute-start.4 = (bf16[2,128,2048]{2,1,0:T(8,128)(2,1)S(1)}, bf16[2,128,2048]{2,1,0:T(8,128)(2,1)S(1)}, u32[]{:S(2)}, u32[]{:S(2)}) collective-permute-start(bf16[2,128,2048]{2,1,0:T(8,128)(2,1)S(1)} %collective-permute-done.2.refs_2_), channel_id=1, source_target_pairs={{0,1},{1,0},{2,3},{3,2},{4,5},{5,4},{6,7},{7,6},{8,9},{9,8},{10,11... | collective-permute-start | bytes 3145736 | tf_op jit(solution)/shard_map/ppermute | solution.py:246
  55.9 9.1 %collective-permute-start.12 = (bf16[2,128,2048]{2,1,0:T(8,128)(2,1)S(1)}, bf16[2,128,2048]{2,1,0:T(8,128)(2,1)S(1)}, u32[]{:S(2)}, u32[]{:S(2)}) collective-permute-start(bf16[2,128,2048]{2,1,0:T(8,128)(2,1)S(1)} %collective-permute-done.6.refs_2_), channel_id=1, source_target_pairs={{0,1},{1,0},{2,3},{3,2},{4,5},{5,4},{6,7},{7,6},{8,9},{9,8},{10,11... | collective-permute-start | bytes 3145736 | tf_op jit(solution)/shard_map/ppermute | solution.py:246
  56.4 16.0 %collective-permute-start.11 = (bf16[2,128,2048]{2,1,0:T(8,128)(2,1)S(1)}, bf16[2,128,2048]{2,1,0:T(8,128)(2,1)S(1)}, u32[]{:S(2)}, u32[]{:S(2)}) collective-permute-start(bf16[2,128,2048]{2,1,0:T(8,128)(2,1)S(1)} %get-tuple-element.115.refs_2_), channel_id=1, source_target_pairs={{0,2},{1,7},{2,4},{3,1},{4,6},{5,3},{6,0},{7,5},{8,10},{9,15},{10,... | collective-permute-start | bytes 3145736 | tf_op jit(solution)/shard_map/ppermute | solution.py:246
  72.4 6.1 %collective-permute-start.13 = (bf16[2,128,2048]{2,1,0:T(8,128)(2,1)S(1)}, bf16[2,128,2048]{2,1,0:T(8,128)(2,1)S(1)}, u32[]{:S(2)}, u32[]{:S(2)}) collective-permute-start(bf16[2,128,2048]{2,1,0:T(8,128)(2,1)S(1)} %collective-permute-done.11.refs_2_), channel_id=1, source_target_pairs={{0,1},{1,0},{2,3},{3,2},{4,5},{5,4},{6,7},{7,6},{8,9},{9,8},{10,11... | collective-permute-start | bytes 3145736 | tf_op jit(solution)/shard_map/ppermute | solution.py:246
  72.5 14.0 %collective-permute-start.10 = (bf16[2,128,2048]{2,1,0:T(8,128)(2,1)S(1)}, bf16[2,128,2048]{2,1,0:T(8,128)(2,1)S(1)}, u32[]{:S(2)}, u32[]{:S(2)}) collective-permute-start(bf16[2,128,2048]{2,1,0:T(8,128)(2,1)S(1)} %get-tuple-element.116.refs_3_), channel_id=1, source_target_pairs={{0,2},{1,7},{2,4},{3,1},{4,6},{5,3},{6,0},{7,5},{8,10},{9,15},{10,... | collective-permute-start | bytes 3145736 | tf_op jit(solution)/shard_map/ppermute | solution.py:246
  86.5 6.8 %collective-permute-start.14 = (bf16[2,128,2048]{2,1,0:T(8,128)(2,1)S(1)}, bf16[2,128,2048]{2,1,0:T(8,128)(2,1)S(1)}, u32[]{:S(2)}, u32[]{:S(2)}) collective-permute-start(bf16[2,128,2048]{2,1,0:T(8,128)(2,1)S(1)} %collective-permute-done.10.refs_2_), channel_id=1, source_target_pairs={{0,1},{1,0},{2,3},{3,2},{4,5},{5,4},{6,7},{7,6},{8,9},{9,8},{10,11... | collective-permute-start | bytes 3145736 | tf_op jit(solution)/shard_map/ppermute | solution.py:246
  89.0 13.9 %collective-permute-start.9 = (bf16[2,128,2048]{2,1,0:T(8,128)(2,1)S(1)}, bf16[2,128,2048]{2,1,0:T(8,128)(2,1)S(1)}, u32[]{:S(2)}, u32[]{:S(2)}) collective-permute-start(bf16[2,128,2048]{2,1,0:T(8,128)(2,1)S(1)} %collective-permute-done.refs_2_), channel_id=1, source_target_pairs={{0,2},{1,7},{2,4},{3,1},{4,6},{5,3},{6,0},{7,5},{8,10},{9,15},{10,... | collective-permute-start | bytes 3145736 | tf_op jit(solution)/shard_map/ppermute | solution.py:246
  102.9 6.1 %collective-permute-start.15 = (bf16[2,128,2048]{2,1,0:T(8,128)(2,1)S(1)}, bf16[2,128,2048]{2,1,0:T(8,128)(2,1)S(1)}, u32[]{:S(2)}, u32[]{:S(2)}) collective-permute-start(bf16[2,128,2048]{2,1,0:T(8,128)(2,1)S(1)} %collective-permute-done.9.refs_2_), channel_id=1, source_target_pairs={{0,1},{1,0},{2,3},{3,2},{4,5},{5,4},{6,7},{7,6},{8,9},{9,8},{10,11... | collective-permute-start | bytes 3145736 | tf_op jit(solution)/shard_map/ppermute | solution.py:246
  105.0 13.9 %collective-permute-start.8 = (bf16[2,128,2048]{2,1,0:T(8,128)(2,1)S(1)}, bf16[2,128,2048]{2,1,0:T(8,128)(2,1)S(1)}, u32[]{:S(2)}, u32[]{:S(2)}) collective-permute-start(bf16[2,128,2048]{2,1,0:T(8,128)(2,1)S(1)} %collective-permute-done.1.refs_2_), channel_id=1, source_target_pairs={{0,2},{1,7},{2,4},{3,1},{4,6},{5,3},{6,0},{7,5},{8,10},{9,15},{10,... | collective-permute-start | bytes 3145736 | tf_op jit(solution)/shard_map/ppermute | solution.py:246
  119.0 6.1 %collective-permute-start.16 = (bf16[2,128,2048]{2,1,0:T(8,128)(2,1)S(1)}, bf16[2,128,2048]{2,1,0:T(8,128)(2,1)S(1)}, u32[]{:S(2)}, u32[]{:S(2)}) collective-permute-start(bf16[2,128,2048]{2,1,0:T(8,128)(2,1)S(1)} %collective-permute-done.8.refs_2_), channel_id=1, source_target_pairs={{0,1},{1,0},{2,3},{3,2},{4,5},{5,4},{6,7},{7,6},{8,9},{9,8},{10,11... | collective-permute-start | bytes 3145736 | tf_op jit(solution)/shard_map/ppermute | solution.py:246
  121.0 13.9 %collective-permute-start.7 = (bf16[2,128,2048]{2,1,0:T(8,128)(2,1)S(1)}, bf16[2,128,2048]{2,1,0:T(8,128)(2,1)S(1)}, u32[]{:S(2)}, u32[]{:S(2)}) collective-permute-start(bf16[2,128,2048]{2,1,0:T(8,128)(2,1)S(1)} %collective-permute-done.2.refs_2_), channel_id=1, source_target_pairs={{0,2},{1,7},{2,4},{3,1},{4,6},{5,3},{6,0},{7,5},{8,10},{9,15},{10,... | collective-permute-start | bytes 3145736 | tf_op jit(solution)/shard_map/ppermute | solution.py:246
  135.0 6.1 %collective-permute-start.17 = (bf16[2,128,2048]{2,1,0:T(8,128)(2,1)S(1)}, bf16[2,128,2048]{2,1,0:T(8,128)(2,1)S(1)}, u32[]{:S(2)}, u32[]{:S(2)}) collective-permute-start(bf16[2,128,2048]{2,1,0:T(8,128)(2,1)S(1)} %collective-permute-done.7.refs_2_), channel_id=1, source_target_pairs={{0,1},{1,0},{2,3},{3,2},{4,5},{5,4},{6,7},{7,6},{8,9},{9,8},{10,11... | collective-permute-start | bytes 3145736 | tf_op jit(solution)/shard_map/ppermute | solution.py:246

commit v4 on v3

v4 whole, which is shorter than its diff:
```python
import functools

import jax
import jax.numpy as jnp
from jax import lax
from jax.experimental import pallas as pl
from jax.experimental.pallas import tpu as pltpu
from jax.sharding import PartitionSpec as P


NORM_EPS = 1e-6
PIECE = 2
LAYERS = 2
ANY = pl.BlockSpec(memory_space=pl.ANY)
VMEM = pl.BlockSpec(memory_space=pltpu.VMEM)
NT = (((1,), (1,)), ((), ()))
MESH = pl.DeviceIdType.MESH


def in_hbm(x):
    return pltpu.with_memory_space_constraint(x, pltpu.HBM)


def rms_norm(x, scale):
    acts = x.astype(jnp.float32)
    mean_sq = jnp.mean(acts * acts, axis=-1, keepdims=True)
    return (acts * lax.rsqrt(mean_sq + NORM_EPS) * scale).astype(jnp.bfloat16)


def output_copies(outs, stage, sem, entry, c, per):
    chips = lax.axis_size("tp") // 2
    me = lax.axis_index("tp")
    core, chip = lax.rem(me, 2), me // 2
    group = stage.shape[-1]
    copies = []
    at = 0
    for j, (n, on0, on1) in enumerate(entry):
        off, first = (a if a is b else jnp.where(core == 0, a, b) for a, b in zip(on0, on1))
        lanes = pl.ds(pl.multiple_of(lax.rem(chip + off, chips) * group, group), group)
        for kv, out in enumerate(outs):
            dst = out.at[pl.ds(c * per, per), pl.ds(first, n), :, lanes]
            copies.append(pltpu.make_async_copy(stage.at[c, kv, :, pl.ds(at, n)], dst, sem.at[c, kv, j]))
        at += n
    return copies


def matmul_block(w_refs, pieces, stage, c):
    per, _, hk, group = stage.shape[2:]
    d = w_refs[0].shape[-1]
    tokens = [p[...].reshape(-1, d) for p in pieces]
    y = jnp.concatenate(tokens) if len(tokens) > 1 else tokens[0]
    for kv, w_ref in enumerate(w_refs):
        w = w_ref[pl.ds(c * per, per)].reshape(per * hk, d)
        res = lax.dot_general(w, y, NT, preferred_element_type=jnp.float32).astype(stage.dtype)
        for l in range(per):
            for s in range(y.shape[0] // group):
                stage[c, kv, l, s] = res[l * hk:(l + 1) * hk, s * group:(s + 1) * group]


def first_kernel(x_ref, scale_ref, y_ref, xbuf, scale_buf, sem, scale_sem):
    n = y_ref.shape[0]
    start = lax.rem(lax.axis_index("tp"), 2) * n
    load = lambda i: pltpu.make_async_copy(x_ref.at[pl.ds(start + i, 1)], xbuf.at[pl.ds(i, 1)], sem.at[i])
    get_scale = pltpu.make_async_copy(scale_ref, scale_buf, scale_sem)
    get_scale.start()
    for i in range(n):
        load(i).start()
    get_scale.wait()
    scale = scale_buf[...].astype(jnp.float32).reshape(1, -1)
    for i in range(n):
        load(i).wait()
        y_ref[i] = rms_norm(xbuf[i], scale)


def normalize_first(x, scale):
    batch, half, d = x.shape
    n = batch // 2
    return pl.pallas_call(
        first_kernel,
        out_shape=jax.ShapeDtypeStruct((n, half, d), x.dtype),
        in_specs=[ANY, ANY],
        out_specs=VMEM,
        scratch_shapes=[
            pltpu.VMEM((n, half, d), x.dtype),
            pltpu.VMEM(scale.shape, scale.dtype),
            pltpu.SemaphoreType.DMA((n,)),
            pltpu.SemaphoreType.DMA,
        ],
        compiler_params=pltpu.CompilerParams(vmem_limit_bytes=8 * 2**20),
        cost_estimate=pl.CostEstimate(flops=32 * x.size, bytes_accessed=2 * x.size, transcendentals=0),
        name="first",
    )(in_hbm(x), in_hbm(scale))


def join(joined, mine, first, theirs):
    n, half = theirs.shape[:2]
    core = lax.rem(lax.axis_index("tp"), 2)
    for s in range(n):
        joined[s, pl.ds(pl.multiple_of(core * half, half), half)] = mine[first + s]
        joined[s, pl.ds(pl.multiple_of((1 - core) * half, half), half)] = theirs[s]


def second_kernel(n_slots, x_ref, scale_ref, wk_ref, wv_ref, y_ref, *refs):
    theirs, refs = refs[:n_slots], refs[n_slots:]
    slots, refs = refs[:n_slots], refs[n_slots:]
    wk_out, wv_out, stage, xbuf, block, scale_buf, in_sem, scale_sem, w_sem, send_sem, recv_sem = refs
    half = x_ref.shape[1]
    me = lax.axis_index("tp")
    core = lax.rem(me, 2)
    other = me + 1 - 2 * core
    rows = pl.ds(pl.multiple_of(core * half, half), half)
    start = (1 - core) * n_slots * PIECE

    barrier = pltpu.get_barrier_semaphore()
    pl.semaphore_signal(barrier, inc=1, device_id={"tp": other}, device_id_type=MESH)

    def load(i):
        return pltpu.make_async_copy(x_ref.at[pl.ds(start + i * PIECE, PIECE)], xbuf.at[i], in_sem.at[i])

    def send(i, src, dst):
        return pltpu.make_async_remote_copy(
            src_ref=src,
            dst_ref=dst,
            send_sem=send_sem.at[i],
            recv_sem=recv_sem.at[i],
            device_id={"tp": other},
            device_id_type=MESH,
        )

    def load_weights(c):
        layers = pl.ds(c * LAYERS, LAYERS)
        pairs = ((wk_ref, wk_out), (wv_ref, wv_out))
        return [pltpu.make_async_copy(a.at[layers], b.at[layers], w_sem.at[kv, c]) for kv, (a, b) in enumerate(pairs)]

    get_scale = pltpu.make_async_copy(scale_ref, scale_buf, scale_sem)
    get_scale.start()
    for i in range(n_slots):
        load(i).start()
    for copy in load_weights(0):
        copy.start()
    to_theirs = [send(i, xbuf.at[i], theirs[i]) for i in range(n_slots)]
    to_slots = [send(n_slots + i, y_ref.at[pl.ds(i * PIECE, PIECE)], slots[i].at[:, rows]) for i in range(n_slots)]
    get_scale.wait()
    scale = scale_buf[...].astype(jnp.float32).reshape(1, -1)
    pl.semaphore_wait(barrier, 1)
    for i in range(n_slots):
        load(i).wait()
        y = rms_norm(xbuf[i], scale)
        xbuf[i] = y
        slots[i][:, rows] = y
        if i > 0:
            to_theirs[i - 1].start()
    for copy in to_slots:
        copy.start()
    to_theirs[-1].start()
    parts = block.shape[0]
    for i in range(parts):
        to_theirs[i].wait_recv()
        join(block.at[i], y_ref, i * PIECE, theirs[i])
    chunks = stage.shape[0]

    @pl.loop(0, chunks)
    def _(c):

        @pl.when(c + 1 < chunks)
        def _():
            for copy in load_weights(c + 1):
                copy.start()

        for copy in load_weights(c):
            copy.wait()
        matmul_block((wk_out, wv_out), [block.at[i] for i in range(parts)], stage, c)

    for i, copy in enumerate(to_theirs + to_slots):
        copy.wait_send()
        if i >= parts:
            copy.wait_recv()


def stage_shape(weights, seqs, group):
    layers, hk, _ = weights[0].shape
    return jax.ShapeDtypeStruct((layers // LAYERS, len(weights), LAYERS, seqs, hk, group), weights[0].dtype)


def prepare(x, scale, weights, y):
    batch, half, d = x.shape
    n_slots = batch // PIECE // 2
    parts = 2
    theirs = jax.ShapeDtypeStruct((PIECE, half, d), x.dtype)
    slot = jax.ShapeDtypeStruct((PIECE, 2 * half, d), x.dtype)
    out_shape = (theirs,) * n_slots + (slot,) * n_slots
    out_shape += tuple(jax.ShapeDtypeStruct(w.shape, w.dtype) for w in weights)
    out_shape += (stage_shape(weights, PIECE * parts, 2 * half),)
    outs = pl.pallas_call(
        functools.partial(second_kernel, n_slots),
        out_shape=out_shape,
        in_specs=[ANY] * 4 + [VMEM],
        out_specs=(VMEM,) * len(out_shape),
        scratch_shapes=[
            pltpu.VMEM((n_slots, PIECE, half, d), x.dtype),
            pltpu.VMEM((parts, PIECE, 2 * half, d), x.dtype),
            pltpu.VMEM(scale.shape, scale.dtype),
            pltpu.SemaphoreType.DMA((n_slots,)),
            pltpu.SemaphoreType.DMA,
            pltpu.SemaphoreType.DMA((2, weights[0].shape[0] // LAYERS)),
            pltpu.SemaphoreType.DMA((2 * n_slots,)),
            pltpu.SemaphoreType.DMA((2 * n_slots,)),
        ],
        compiler_params=pltpu.CompilerParams(vmem_limit_bytes=9 * 2**20, collective_id=0, has_side_effects=True),
        cost_estimate=pl.CostEstimate(flops=64 * x.size, bytes_accessed=4 * x.size, transcendentals=0),
        name="prep2",
    )(in_hbm(x), in_hbm(scale), *map(in_hbm, weights), y)
    return outs[:n_slots], outs[n_slots:2 * n_slots], outs[2 * n_slots:-1], outs[-1]


def project_kernel(plan, sources, n_pieces, carried, n_alias, keep, keep_joined, *refs):
    w_refs, refs = refs[:2], refs[2:]
    pieces, refs = refs[:n_pieces], refs[n_pieces:]
    before, refs = refs[0], refs[1 + n_alias:]
    n_joins = sum(len(source) > 1 for source in sources)
    outs, refs = refs[:2], refs[2:]
    refs, (sem, before_sem) = refs[:-2], refs[-2:]
    stage, *joined = refs if keep or not (keep_joined and n_joins) else refs[-1:] + refs[:-1]
    joined = iter(joined)
    chunks, _, per = stage.shape[:3]
    entry, old_chunks = carried
    late = [copy for c in old_chunks for copy in output_copies(outs, before, before_sem, entry, c, per)]
    for copy in late:
        copy.start()
    put = lambda i, c: output_copies(outs, stage, sem, plan[i], c, per)
    tokens = []
    for source in sources:
        if len(source) > 1:
            mine, first, theirs = source
            tokens.append(next(joined))
            join(tokens[-1], pieces[mine], first, pieces[theirs])
        else:
            tokens.append(pieces[source[0]])
    used = 0
    for i, block in enumerate(plan):
        mine = tokens[used:used + len(block)]
        used += len(block)
        last = i == len(plan) - 1 and keep

        @pl.loop(0, chunks)
        def _(c):
            if i > 0:
                for copy in put(i - 1, c):
                    copy.wait()
            matmul_block(w_refs, mine, stage, c)
            if last:

                @pl.when(c < chunks - 1)
                def _():
                    for copy in put(i, c):
                        copy.start()
            else:
                for copy in put(i, c):
                    copy.start()

    for copy in late:
        copy.wait()
    for c in range(chunks - 1 if keep else chunks):
        for copy in put(len(plan) - 1, c):
            copy.wait()


def project(weights, blocks, out, carry, batch, tp, keep, keep_joined):
    layers, hk, d = weights[0].shape
    pieces, sources, joined, plan = [], [], (), []
    for block in blocks:
        entry = []
        for piece, *where in block:
            if isinstance(piece, tuple):
                mine, first, theirs = piece
                sources.append((len(pieces), first, len(pieces) + 1))
                pieces += [mine, theirs]
                n, half, _ = theirs.shape
                joined += (jax.ShapeDtypeStruct((n, 2 * half, d), theirs.dtype),)
                group = 2 * half
            else:
                sources.append((len(pieces),))
                pieces.append(piece)
                n, group, _ = piece.shape
            entry.append((n, *where))
        plan.append(tuple(entry))
    plan = tuple(plan)
    shape = jax.ShapeDtypeStruct((layers, batch, hk, group * tp // 2), weights[0].dtype)
    n_alias = 0 if out is None else 2
    n_in = 3 + len(pieces)
    stage = stage_shape(weights, sum(n for n, *_ in plan[0]), group)
    before, before_entry, chunks = carry
    tok = sum(n for entry in plan for n, *_ in entry) * group
    outs = pl.pallas_call(
        functools.partial(project_kernel, plan, tuple(sources), len(pieces), (before_entry, chunks), n_alias, keep, keep_joined),
        out_shape=(shape, shape) + (stage,) * keep + joined * keep_joined,
        in_specs=[VMEM] * n_in + [ANY] * n_alias,
        out_specs=(ANY, ANY) + (VMEM,) * (keep + len(joined) * keep_joined),
        input_output_aliases={n_in + i: i for i in range(n_alias)},
        scratch_shapes=[pltpu.VMEM(stage.shape, stage.dtype)] * (not keep) + [pltpu.VMEM(j.shape, j.dtype) for j in joined * (not keep_joined)] + [
            pltpu.SemaphoreType.DMA((stage.shape[0], 2, len(plan[0]))),
            pltpu.SemaphoreType.DMA((stage.shape[0], 2, len(before_entry))),
        ],
        compiler_params=pltpu.CompilerParams(vmem_limit_bytes=5 * 2**20),
        cost_estimate=pl.CostEstimate(
            flops=2 * tok * d * hk * 2 * layers,
            bytes_accessed=2 * tok * (d + 2 * layers * hk),
            transcendentals=0,
        ),
    )(*weights, *pieces, before, *(out or ()))
    carry = (outs[2], plan[-1], (stage.shape[0] - 1,)) if keep else None
    return outs[:2], carry, outs[2 + keep:]


def solution(mesh):
    tp = mesh.shape["tp"]
    chips = tp // 2
    ring = [(i, (i + 2 - 4 * (i % 2)) % tp) for i in range(tp)]
    swap = [(i, i ^ 1) for i in range(tp)]

    def send(v, perm):
        return lax.ppermute(v, "tp", perm)

    def per_device(enc_out, norm_scale, w_key, w_value):
        layers, d, heads, k = w_key.shape
        batch = enc_out.shape[0]
        wk = w_key.reshape(layers, d, heads * k).transpose(0, 2, 1)
        wv = w_value.reshape(layers, d, heads * k).transpose(0, 2, 1)
        n = batch // PIECE
        h = n // 2
        seq = lambda i: (i % n) * PIECE

        state = {"out": None}

        def run(blocks, keep=True, keep_joined=True):
            state["out"], state["carry"], joined = project(weights, blocks, state["out"], state["carry"], batch, tp, keep, keep_joined)
            return joined

        def hold(*arrays):
            arrays, state["out"] = lax.optimization_barrier((arrays, state["out"]))
            return arrays if len(arrays) > 1 else arrays[0]

        y = normalize_first(enc_out, norm_scale)
        ny = send(y, ring)
        other, slots, weights, stage = prepare(enc_out, norm_scale, (wk, wv), y)
        own = lambda i: ((0, seq(i)), (0, seq(i + h)))
        state["carry"] = (stage, tuple((PIECE, *own(i)) for i in range(2)), tuple(range(stage.shape[0])))
        nz = [send(v, ring) for v in other]
        n3 = send(slots[0], ring)
        run([[((y, 2 * PIECE, other[2]), *own(2)), (slots[0], *own(3))]], keep_joined=False)
        run([[(slots[1], *own(4)), (slots[2], *own(5))]])

        LEFT, RIGHT = chips - 1, 1
        near = lambda i: ((LEFT, seq(i)), (RIGHT, seq(i + h)))
        far = lambda i: ((2, seq(i)), (2, seq(i + h)))
        mine = lambda p, where: (p, *where)
        theirs = lambda q, where: (q, *where[::-1])

        py, z0, z1 = hold(ny, nz[0], nz[1])
        n4, n5 = send(slots[1], ring), send(slots[2], ring)
        p0, p1 = run([[mine((py, 0, z0), near(0)), mine((py, PIECE, z1), near(1))]])
        q0, q1 = send(p0, swap), send(p1, swap)
        z2 = hold(nz[2])
        p2, = run([[mine((py, 2 * PIECE, z2), near(2))]])
        q2 = send(p2, swap)
        run([[theirs(q0, near(0)), theirs(q1, near(1))]])
        p3 = hold(n3)
        q3 = send(p3, swap)
        run([[theirs(q2, near(2)), mine(p3, near(3))]])
        p4, p0, p1, p2 = hold(n4, p0, p1, p2)
        q4 = send(p4, swap)
        f0, f1, f2 = (send(p, ring) for p in (p0, p1, p2))
        run([[theirs(q3, near(3)), mine(p4, near(4))]])
        p5 = hold(n5)
        q5 = send(p5, swap)
        run([[theirs(q4, near(4)), mine(p5, near(5))]])
        run([[theirs(q5, near(5))]])
        for i, v in enumerate((f0, f1, f2)):
            p = hold(v)
            q = send(p, swap)
            run([[mine(p, far(i))]])
            q = hold(q)
            run([[theirs(q, far(i))]], keep=i < 2)
        out = state["out"]
        to_cache = lambda o: o.reshape(layers, batch, heads, k, -1).transpose(0, 1, 4, 2, 3)
        return to_cache(out[0]), to_cache(out[1])

    weight_spec = P(None, None, "tp", None)
    cache_spec = P(None, "dp", None, "tp", None)
    step = jax.shard_map(per_device, mesh=mesh, in_specs=(P("dp", "tp", None), P(None), weight_spec, weight_spec), out_specs=(cache_spec, cache_spec), check_vma=False)

    def program(*args):
        jax.eval_shape(step, *args)
        return step(*args)

    return program
```

time: 146 us -> 147 us (level)
  Pallas kernels: 104 us -> 98.1 us
  starting transfers between devices: 19.3 us -> 24.7 us
  waiting for transfers between devices: 21.4 us -> 23.1 us
    pallas_call x18 -> x17, Pallas kernels: 104 us -> 98.1 us  [the longest x15 85.1 us: project(): pl.pallas_call(functools.partial(project_kernel, plan, tuple(sources), le...]
    ppermute x18 -> x19, starting transfers between devices: 19.3 us -> 24.7 us  [send(): return lax.ppermute(v, 'tp', perm)]
    ppermute x18 -> x19, waiting for transfers between devices: 21.4 us -> 23.1 us  [send(): return lax.ppermute(v, 'tp', perm)]
  transfers between devices with their start and end apart: 18 -> 19, of which waited for: 4 -> 6; matrix products, arithmetic and copies ran while one was open for 0% -> 0% of each run, Pallas kernels for 64% -> 57%
where the time goes in v4:
time: 147 us
  Pallas kernels  98.1 us (67%)
  starting transfers between devices  24.7 us (17%)
  waiting for transfers between devices  23.1 us (16%)
    pallas_call x15, Pallas kernels, project(): pl.pallas_call(functools.partial(project_kernel, plan, tuple(sources), le...  85.1 us
    ppermute x19, starting transfers between devices, send(): return lax.ppermute(v, 'tp', perm)  24.7 us
    ppermute x19, waiting for transfers between devices, send(): return lax.ppermute(v, 'tp', perm)  23.1 us
    pallas_call x1, Pallas kernels, prepare(): pl.pallas_call(functools.partial(second_kernel, n_slots), out_shape=out_s...  11 us
  transfers between devices with their start and end apart: 19, of which 6 were waited for; matrix products, arithmetic and copies ran while one was open for 0% of the time, Pallas kernels for 57%

profile of v4, /device:TPU:81, one launch (start us, length us, event | category | flops | bytes accessed | tf_op | source)
XLA Modules:
  0.0 146.9 jit_solution(14732139168744349071)
XLA Ops:
  2.7 3.8 %collective-permute-start.1 = (bf16[6,64,2048]{2,1,0:T(8,128)(2,1)S(1)}, bf16[6,64,2048]{2,1,0:T(8,128)(2,1)S(1)}, u32[]{:S(2)}, u32[]{:S(2)}) collective-permute-start(bf16[6,64,2048]{2,1,0:T(8,128)(2,1)S(1)} %first.1.y_ref.refs_2_), channel_id=1, source_target_pairs={{0,2},{1,7},{2,4},{3,1},{4,6},{5,3},{6,0},{7,5},{8,10},{9,15},{10,... | collective-permute-start | bytes 4718600 | tf_op jit(solution)/shard_map/ppermute | solution.py:322
  6.5 11.0 %prep2.1 = (bf16[2,64,2048]{2,1,0:T(8,128)(2,1)S(1)}, bf16[2,64,2048]{2,1,0:T(8,128)(2,1)S(1)}, bf16[2,64,2048]{2,1,0:T(8,128)(2,1)S(1)}, bf16[2,128,2048]{2,1,0...) custom-call(bf16[12,64,2048]{2,1,0:T(8,128)(2,1)} %x_ref.3, ...), custom_call_target="tpu_custom_call" | custom-call | flops 100663296 | bytes 6291456 | tf_op jit(solution)/shard_map/prep2/pallas_call | solution.py:194
  20.6 7.5 %shard_map.59 = (bf16[6,12,256,512]{3,2,1,0:T(8,128)(2,1)}, bf16[6,12,256,512]{3,2,1,0:T(8,128)(2,1)}, bf16[3,2,2,4,256,128]{5,4,3,2,1,0:T(8,128)(2,1)S(1)}) custom-call(bf16[6,256,2048]{2,1,0:T(8,128)(2,1)S(1)} %get-tuple-element.96.refs_0_, bf16[6,256,2048]{2,1,0:T(8,128)(2,1)S(1)} %get-tuple-element.97.refs_1_, ...), custom_call_target="tpu_custom_call" | custom-call | flops 6442450944 | bytes 5242880 | tf_op jit(solution)/shard_map/pallas_call | solution.py:294
  28.1 7.4 %shard_map.60 = (bf16[6,12,256,512]{3,2,1,0:T(8,128)(2,1)}, bf16[6,12,256,512]{3,2,1,0:T(8,128)(2,1)}, bf16[3,2,2,4,256,128]{5,4,3,2,1,0:T(8,128)(2,1)S(1)}) custom-call(bf16[6,256,2048]{2,1,0:T(8,128)(2,1)S(1)} %get-tuple-element.96.refs_0_, bf16[6,256,2048]{2,1,0:T(8,128)(2,1)S(1)} %get-tuple-element.97.refs_1_, ...), custom_call_target="tpu_custom_call", output_to_operand_aliasing={{0}: (5, {}), {1}: (6, {})} | custom-call | flops 6442450944 | bytes 5242880 | tf_op jit(solution)/shard_map/pallas_call | solution.py:294
  35.5 7.6 %shard_map.61 = (bf16[6,12,256,512]{3,2,1,0:T(8,128)(2,1)}, bf16[6,12,256,512]{3,2,1,0:T(8,128)(2,1)}, bf16[3,2,2,4,256,128]{5,4,3,2,1,0:T(8,128)(2,1)S(1)}, bf1...) custom-call(bf16[6,256,2048]{2,1,0:T(8,128)(2,1)S(1)} %get-tuple-element.96.r, ...), custom_call_target="tpu_custom_call", output_to_operand_aliasing={{0}: (7, {}), {1}: (8, {})} | custom-call | flops 6442450944 | bytes 5242880 | tf_op jit(solution)/shard_map/pallas_call | solution.py:294
  47.0 6.7 %collective-permute-done.4.refs_3_ = bf16[2,64,2048]{2,1,0:T(8,128)(2,1)S(1)} collective-permute-done((bf16[2,64,2048]{2,1,0:T(8,128)(2,1)S(1)}, bf16[2,64,2048]{2,1,0:T(8,128)(2,1)S(1)}, u32[]{:S(2)}, u32[]{:S(2)}) %collective-permute-start.4) | collective-permute-done | bytes 524320 | tf_op jit(solution)/shard_map/ppermute | solution.py:322
  53.7 4.1 %shard_map.62 = (bf16[6,12,256,512]{3,2,1,0:T(8,128)(2,1)}, bf16[6,12,256,512]{3,2,1,0:T(8,128)(2,1)}, bf16[3,2,2,2,256,128]{5,4,3,2,1,0:T(8,128)(2,1)S(1)}, bf16[2,128,2048]{2,1,0:T(8,128)(2,1)S(1)}) custom-call(bf16[6,256,2048]{2,1,0:T(8,128)(2,1)S(1)} %get-tuple-element.96.refs_0_, ...), custom_call_target="tpu_custom_call", output_to_operand_aliasing={{0}: (5, {}), {1}: (6, {})} | custom-call | flops 3221225472 | bytes 2621440 | tf_op jit(solution)/shard_map/pallas_call | solution.py:294
  57.9 2.5 %collective-permute-start.5 = (bf16[2,128,2048]{2,1,0:T(8,128)(2,1)S(1)}, bf16[2,128,2048]{2,1,0:T(8,128)(2,1)S(1)}, u32[]{:S(2)}, u32[]{:S(2)}) collective-permute-start(bf16[2,128,2048]{2,1,0:T(8,128)(2,1)S(1)} %get-tuple-element.136), channel_id=1, source_target_pairs={{0,1},{1,0},{2,3},{3,2},{4,5},{5,4},{6,7},{7,6},{8,9},{9,8},{10,11... | collective-permute-start | bytes 3145736 | tf_op jit(solution)/shard_map/ppermute | solution.py:322
  60.4 7.3 %shard_map.63 = (bf16[6,12,256,512]{3,2,1,0:T(8,128)(2,1)}, bf16[6,12,256,512]{3,2,1,0:T(8,128)(2,1)}, bf16[3,2,2,4,256,128]{5,4,3,2,1,0:T(8,128)(2,1)S(1)}) custom-call(bf16[6,256,2048]{2,1,0:T(8,128)(2,1)S(1)} %get-tuple-element.96.refs_0_, bf16[6,256,2048]{2,1,0:T(8,128)(2,1)S(1)} %get-tuple-element.97.refs_1_, ...), custom_call_target="tpu_custom_call", output_to_operand_aliasing={{0}: (5, {}), {1}: (6, {})} | custom-call | flops 6442450944 | bytes 5242880 | tf_op jit(solution)/shard_map/pallas_call | solution.py:294
  68.0 7.4 %shard_map.64 = (bf16[6,12,256,512]{3,2,1,0:T(8,128)(2,1)}, bf16[6,12,256,512]{3,2,1,0:T(8,128)(2,1)}, bf16[3,2,2,4,256,128]{5,4,3,2,1,0:T(8,128)(2,1)S(1)}) custom-call(bf16[6,256,2048]{2,1,0:T(8,128)(2,1)S(1)} %get-tuple-element.96.refs_0_, bf16[6,256,2048]{2,1,0:T(8,128)(2,1)S(1)} %get-tuple-element.97.refs_1_, ...), custom_call_target="tpu_custom_call", output_to_operand_aliasing={{0}: (5, {}), {1}: (6, {})} | custom-call | flops 6442450944 | bytes 5242880 | tf_op jit(solution)/shard_map/pallas_call | solution.py:294
  76.2 2.5 %collective-permute-start.15 = (bf16[2,128,2048]{2,1,0:T(8,128)(2,1)S(1)}, bf16[2,128,2048]{2,1,0:T(8,128)(2,1)S(1)}, u32[]{:S(2)}, u32[]{:S(2)}) collective-permute-start(bf16[2,128,2048]{2,1,0:T(8,128)(2,1)S(1)} %collective-permute-done.refs_3_), channel_id=1, source_target_pairs={{0,1},{1,0},{2,3},{3,2},{4,5},{5,4},{6,7},{7,6},{8,9},{9,8},{10,11... | collective-permute-start | bytes 3145736 | tf_op jit(solution)/shard_map/ppermute | solution.py:322
  78.6 7.4 %shard_map.65 = (bf16[6,12,256,512]{3,2,1,0:T(8,128)(2,1)}, bf16[6,12,256,512]{3,2,1,0:T(8,128)(2,1)}, bf16[3,2,2,4,256,128]{5,4,3,2,1,0:T(8,128)(2,1)S(1)}) custom-call(bf16[6,256,2048]{2,1,0:T(8,128)(2,1)S(1)} %get-tuple-element.96.refs_0_, bf16[6,256,2048]{2,1,0:T(8,128)(2,1)S(1)} %get-tuple-element.97.refs_1_, ...), custom_call_target="tpu_custom_call", output_to_operand_aliasing={{0}: (5, {}), {1}: (6, {})} | custom-call | flops 6442450944 | bytes 5242880 | tf_op jit(solution)/shard_map/pallas_call | solution.py:294
  87.4 2.5 %collective-permute-start.14 = (bf16[2,128,2048]{2,1,0:T(8,128)(2,1)S(1)}, bf16[2,128,2048]{2,1,0:T(8,128)(2,1)S(1)}, u32[]{:S(2)}, u32[]{:S(2)}) collective-permute-start(bf16[2,128,2048]{2,1,0:T(8,128)(2,1)S(1)} %collective-permute-done.12.refs_3_), channel_id=1, source_target_pairs={{0,1},{1,0},{2,3},{3,2},{4,5},{5,4},{6,7},{7,6},{8,9},{9,8},{10,11... | collective-permute-start | bytes 3145736 | tf_op jit(solution)/shard_map/ppermute | solution.py:322
  89.9 7.4 %shard_map.66 = (bf16[6,12,256,512]{3,2,1,0:T(8,128)(2,1)}, bf16[6,12,256,512]{3,2,1,0:T(8,128)(2,1)}, bf16[3,2,2,4,256,128]{5,4,3,2,1,0:T(8,128)(2,1)S(1)}) custom-call(bf16[6,256,2048]{2,1,0:T(8,128)(2,1)S(1)} %get-tuple-element.96.refs_0_, bf16[6,256,2048]{2,1,0:T(8,128)(2,1)S(1)} %get-tuple-element.97.refs_1_, ...), custom_call_target="tpu_custom_call", output_to_operand_aliasing={{0}: (5, {}), {1}: (6, {})} | custom-call | flops 6442450944 | bytes 5242880 | tf_op jit(solution)/shard_map/pallas_call | solution.py:294
  97.3 4.1 %shard_map.67 = (bf16[6,12,256,512]{3,2,1,0:T(8,128)(2,1)}, bf16[6,12,256,512]{3,2,1,0:T(8,128)(2,1)}, bf16[3,2,2,2,256,128]{5,4,3,2,1,0:T(8,128)(2,1)S(1)}) custom-call(bf16[6,256,2048]{2,1,0:T(8,128)(2,1)S(1)} %get-tuple-element.96.refs_0_, bf16[6,256,2048]{2,1,0:T(8,128)(2,1)S(1)} %get-tuple-element.97.refs_1_, ...), custom_call_target="tpu_custom_call", output_to_operand_aliasing={{0}: (4, {}), {1}: (5, {})} | custom-call | flops 3221225472 | bytes 2621440 | tf_op jit(solution)/shard_map/pallas_call | solution.py:294
  101.4 2.4 %collective-permute-done.11.refs_2_ = bf16[2,128,2048]{2,1,0:T(8,128)(2,1)S(1)} collective-permute-done((bf16[2,128,2048]{2,1,0:T(8,128)(2,1)S(1)}, bf16[2,128,2048]{2,1,0:T(8,128)(2,1)S(1)}, u32[]{:S(2)}, u32[]{:S(2)}) %collective-permute-start.11) | collective-permute-done | bytes 1048608 | tf_op jit(solution)/shard_map/ppermute | solution.py:322
  105.9 4.0 %shard_map.68 = (bf16[6,12,256,512]{3,2,1,0:T(8,128)(2,1)}, bf16[6,12,256,512]{3,2,1,0:T(8,128)(2,1)}, bf16[3,2,2,2,256,128]{5,4,3,2,1,0:T(8,128)(2,1)S(1)}) custom-call(bf16[6,256,2048]{2,1,0:T(8,128)(2,1)S(1)} %get-tuple-element.96.refs_0_, bf16[6,256,2048]{2,1,0:T(8,128)(2,1)S(1)} %get-tuple-element.97.refs_1_, ...), custom_call_target="tpu_custom_call", output_to_operand_aliasing={{0}: (4, {}), {1}: (5, {})} | custom-call | flops 3221225472 | bytes 2621440 | tf_op jit(solution)/shard_map/pallas_call | solution.py:294
  109.9 4.0 %shard_map.69 = (bf16[6,12,256,512]{3,2,1,0:T(8,128)(2,1)}, bf16[6,12,256,512]{3,2,1,0:T(8,128)(2,1)}, bf16[3,2,2,2,256,128]{5,4,3,2,1,0:T(8,128)(2,1)S(1)}) custom-call(bf16[6,256,2048]{2,1,0:T(8,128)(2,1)S(1)} %get-tuple-element.96.refs_0_, bf16[6,256,2048]{2,1,0:T(8,128)(2,1)S(1)} %get-tuple-element.97.refs_1_, ...), custom_call_target="tpu_custom_call", output_to_operand_aliasing={{0}: (4, {}), {1}: (5, {})} | custom-call | flops 3221225472 | bytes 2621440 | tf_op jit(solution)/shard_map/pallas_call | solution.py:294
  114.0 5.9 %collective-permute-done.10.refs_2_ = bf16[2,128,2048]{2,1,0:T(8,128)(2,1)S(1)} collective-permute-done((bf16[2,128,2048]{2,1,0:T(8,128)(2,1)S(1)}, bf16[2,128,2048]{2,1,0:T(8,128)(2,1)S(1)}, u32[]{:S(2)}, u32[]{:S(2)}) %collective-permute-start.10) | collective-permute-done | bytes 1048608 | tf_op jit(solution)/shard_map/ppermute | solution.py:322
  121.9 4.0 %shard_map.70 = (bf16[6,12,256,512]{3,2,1,0:T(8,128)(2,1)}, bf16[6,12,256,512]{3,2,1,0:T(8,128)(2,1)}, bf16[3,2,2,2,256,128]{5,4,3,2,1,0:T(8,128)(2,1)S(1)}) custom-call(bf16[6,256,2048]{2,1,0:T(8,128)(2,1)S(1)} %get-tuple-element.96.refs_0_, bf16[6,256,2048]{2,1,0:T(8,128)(2,1)S(1)} %get-tuple-element.97.refs_1_, ...), custom_call_target="tpu_custom_call", output_to_operand_aliasing={{0}: (4, {}), {1}: (5, {})} | custom-call | flops 3221225472 | bytes 2621440 | tf_op jit(solution)/shard_map/pallas_call | solution.py:294
  125.9 4.0 %shard_map.71 = (bf16[6,12,256,512]{3,2,1,0:T(8,128)(2,1)}, bf16[6,12,256,512]{3,2,1,0:T(8,128)(2,1)}, bf16[3,2,2,2,256,128]{5,4,3,2,1,0:T(8,128)(2,1)S(1)}) custom-call(bf16[6,256,2048]{2,1,0:T(8,128)(2,1)S(1)} %get-tuple-element.96.refs_0_, bf16[6,256,2048]{2,1,0:T(8,128)(2,1)S(1)} %get-tuple-element.97.refs_1_, ...), custom_call_target="tpu_custom_call", output_to_operand_aliasing={{0}: (4, {}), {1}: (5, {})} | custom-call | flops 3221225472 | bytes 2621440 | tf_op jit(solution)/shard_map/pallas_call | solution.py:294
  130.0 5.9 %collective-permute-done.9.refs_2_ = bf16[2,128,2048]{2,1,0:T(8,128)(2,1)S(1)} collective-permute-done((bf16[2,128,2048]{2,1,0:T(8,128)(2,1)S(1)}, bf16[2,128,2048]{2,1,0:T(8,128)(2,1)S(1)}, u32[]{:S(2)}, u32[]{:S(2)}) %collective-permute-start.9) | collective-permute-done | bytes 1048608 | tf_op jit(solution)/shard_map/ppermute | solution.py:322
  137.9 4.0 %shard_map.72 = (bf16[6,12,256,512]{3,2,1,0:T(8,128)(2,1)}, bf16[6,12,256,512]{3,2,1,0:T(8,128)(2,1)}, bf16[3,2,2,2,256,128]{5,4,3,2,1,0:T(8,128)(2,1)S(1)}) custom-call(bf16[6,256,2048]{2,1,0:T(8,128)(2,1)S(1)} %get-tuple-element.96.refs_0_, bf16[6,256,2048]{2,1,0:T(8,128)(2,1)S(1)} %get-tuple-element.97.refs_1_, ...), custom_call_target="tpu_custom_call", output_to_operand_aliasing={{0}: (4, {}), {1}: (5, {})} | custom-call | flops 3221225472 | bytes 2621440 | tf_op jit(solution)/shard_map/pallas_call | solution.py:294
  141.9 4.8 %shard_map.73 = (bf16[6,12,256,512]{3,2,1,0:T(8,128)(2,1)}, bf16[6,12,256,512]{3,2,1,0:T(8,128)(2,1)}) custom-call(bf16[6,256,2048]{2,1,0:T(8,128)(2,1)S(1)} %get-tuple-element.96.refs_0_, bf16[6,256,2048]{2,1,0:T(8,128)(2,1)S(1)} %get-tuple-element.97.refs_1_, ...), custom_call_target="tpu_custom_call", output_to_operand_aliasing={{0}: (4, {}), {1}: (5, {})} | custom-call | flops 3221225472 | bytes 2621440 | tf_op jit(solution)/shard_map/pallas_call | solution.py:294
  (31 shorter events, 17.6 us)
Async XLA Ops:
  2.7 32.8 %collective-permute-start.1 = (bf16[6,64,2048]{2,1,0:T(8,128)(2,1)S(1)}, bf16[6,64,2048]{2,1,0:T(8,128)(2,1)S(1)}, u32[]{:S(2)}, u32[]{:S(2)}) collective-permute-start(bf16[6,64,2048]{2,1,0:T(8,128)(2,1)S(1)} %first.1.y_ref.refs_2_), channel_id=1, source_target_pairs={{0,2},{1,7},{2,4},{3,1},{4,6},{5,3},{6,0},{7,5},{8,10},{9,15},{10,... | collective-permute-start | bytes 4718600 | tf_op jit(solution)/shard_map/ppermute | solution.py:322
  17.5 18.0 %collective-permute-start.2 = (bf16[2,64,2048]{2,1,0:T(8,128)(2,1)S(1)}, bf16[2,64,2048]{2,1,0:T(8,128)(2,1)S(1)}, u32[]{:S(2)}, u32[]{:S(2)}) collective-permute-start(bf16[2,64,2048]{2,1,0:T(8,128)(2,1)S(1)} %get-tuple-element.99), channel_id=1, source_target_pairs={{0,2},{1,7},{2,4},{3,1},{4,6},{5,3},{6,0},{7,5},{8,10},{9,15},{10,... | collective-permute-start | bytes 1572872 | tf_op jit(solution)/shard_map/ppermute | solution.py:322
  19.5 16.0 %collective-permute-start.3 = (bf16[2,64,2048]{2,1,0:T(8,128)(2,1)S(1)}, bf16[2,64,2048]{2,1,0:T(8,128)(2,1)S(1)}, u32[]{:S(2)}, u32[]{:S(2)}) collective-permute-start(bf16[2,64,2048]{2,1,0:T(8,128)(2,1)S(1)} %get-tuple-element.100), channel_id=1, source_target_pairs={{0,2},{1,7},{2,4},{3,1},{4,6},{5,3},{6,0},{7,5},{8,10},{9,15},{10,... | collective-permute-start | bytes 1572872 | tf_op jit(solution)/shard_map/ppermute | solution.py:322
  43.1 17.3 %collective-permute-start.7 = (bf16[2,128,2048]{2,1,0:T(8,128)(2,1)S(1)}, bf16[2,128,2048]{2,1,0:T(8,128)(2,1)S(1)}, u32[]{:S(2)}, u32[]{:S(2)}) collective-permute-start(bf16[2,128,2048]{2,1,0:T(8,128)(2,1)S(1)} %get-tuple-element.138), channel_id=1, source_target_pairs={{0,1},{1,0},{2,3},{3,2},{4,5},{5,4},{6,7},{7,6},{8,9},{9,8},{10,11... | collective-permute-start | bytes 3145736 | tf_op jit(solution)/shard_map/ppermute | solution.py:322
  45.3 15.2 %collective-permute-start.8 = (bf16[2,128,2048]{2,1,0:T(8,128)(2,1)S(1)}, bf16[2,128,2048]{2,1,0:T(8,128)(2,1)S(1)}, u32[]{:S(2)}, u32[]{:S(2)}) collective-permute-start(bf16[2,128,2048]{2,1,0:T(8,128)(2,1)S(1)} %get-tuple-element.137), channel_id=1, source_target_pairs={{0,1},{1,0},{2,3},{3,2},{4,5},{5,4},{6,7},{7,6},{8,9},{9,8},{10,11... | collective-permute-start | bytes 3145736 | tf_op jit(solution)/shard_map/ppermute | solution.py:322
  45.4 8.3 %collective-permute-start.4 = (bf16[2,64,2048]{2,1,0:T(8,128)(2,1)S(1)}, bf16[2,64,2048]{2,1,0:T(8,128)(2,1)S(1)}, u32[]{:S(2)}, u32[]{:S(2)}) collective-permute-start(bf16[2,64,2048]{2,1,0:T(8,128)(2,1)S(1)} %get-tuple-element.102.refs_3_), channel_id=1, source_target_pairs={{0,2},{1,7},{2,4},{3,1},{4,6},{5,3},{6,0},{7,5},{8,10},{9,15},{10,... | collective-permute-start | bytes 1572872 | tf_op jit(solution)/shard_map/ppermute | solution.py:322
  46.5 21.3 %collective-permute-start.6 = (bf16[2,128,2048]{2,1,0:T(8,128)(2,1)S(1)}, bf16[2,128,2048]{2,1,0:T(8,128)(2,1)S(1)}, u32[]{:S(2)}, u32[]{:S(2)}) collective-permute-start(bf16[2,128,2048]{2,1,0:T(8,128)(2,1)S(1)} %get-tuple-element.103.refs_4_), channel_id=1, source_target_pairs={{0,2},{1,7},{2,4},{3,1},{4,6},{5,3},{6,0},{7,5},{8,10},{9,15},{10,... | collective-permute-start | bytes 3145736 | tf_op jit(solution)/shard_map/ppermute | solution.py:322
  46.9 29.3 %collective-permute-start = (bf16[2,128,2048]{2,1,0:T(8,128)(2,1)S(1)}, bf16[2,128,2048]{2,1,0:T(8,128)(2,1)S(1)}, u32[]{:S(2)}, u32[]{:S(2)}) collective-permute-start(bf16[2,128,2048]{2,1,0:T(8,128)(2,1)S(1)} %get-tuple-element.98.refs_2_), channel_id=1, source_target_pairs={{0,2},{1,7},{2,4},{3,1},{4,6},{5,3},{6,0},{7,5},{8,10},{9,15},{10,... | collective-permute-start | bytes 3145736 | tf_op jit(solution)/shard_map/ppermute | solution.py:322
  57.9 10.1 %collective-permute-start.5 = (bf16[2,128,2048]{2,1,0:T(8,128)(2,1)S(1)}, bf16[2,128,2048]{2,1,0:T(8,128)(2,1)S(1)}, u32[]{:S(2)}, u32[]{:S(2)}) collective-permute-start(bf16[2,128,2048]{2,1,0:T(8,128)(2,1)S(1)} %get-tuple-element.136), channel_id=1, source_target_pairs={{0,1},{1,0},{2,3},{3,2},{4,5},{5,4},{6,7},{7,6},{8,9},{9,8},{10,11... | collective-permute-start | bytes 3145736 | tf_op jit(solution)/shard_map/ppermute | solution.py:322
  67.8 10.9 %collective-permute-start.13 = (bf16[2,128,2048]{2,1,0:T(8,128)(2,1)S(1)}, bf16[2,128,2048]{2,1,0:T(8,128)(2,1)S(1)}, u32[]{:S(2)}, u32[]{:S(2)}) collective-permute-start(bf16[2,128,2048]{2,1,0:T(8,128)(2,1)S(1)} %collective-permute-done.6.refs_3_), channel_id=1, source_target_pairs={{0,1},{1,0},{2,3},{3,2},{4,5},{5,4},{6,7},{7,6},{8,9},{9,8},{10,11... | collective-permute-start | bytes 3145736 | tf_op jit(solution)/shard_map/ppermute | solution.py:322
  67.9 19.5 %collective-permute-start.12 = (bf16[2,128,2048]{2,1,0:T(8,128)(2,1)S(1)}, bf16[2,128,2048]{2,1,0:T(8,128)(2,1)S(1)}, u32[]{:S(2)}, u32[]{:S(2)}) collective-permute-start(bf16[2,128,2048]{2,1,0:T(8,128)(2,1)S(1)} %get-tuple-element.101.refs_3_), channel_id=1, source_target_pairs={{0,2},{1,7},{2,4},{3,1},{4,6},{5,3},{6,0},{7,5},{8,10},{9,15},{10,... | collective-permute-start | bytes 3145736 | tf_op jit(solution)/shard_map/ppermute | solution.py:322
  76.2 13.7 %collective-permute-start.15 = (bf16[2,128,2048]{2,1,0:T(8,128)(2,1)S(1)}, bf16[2,128,2048]{2,1,0:T(8,128)(2,1)S(1)}, u32[]{:S(2)}, u32[]{:S(2)}) collective-permute-start(bf16[2,128,2048]{2,1,0:T(8,128)(2,1)S(1)} %collective-permute-done.refs_3_), channel_id=1, source_target_pairs={{0,1},{1,0},{2,3},{3,2},{4,5},{5,4},{6,7},{7,6},{8,9},{9,8},{10,11... | collective-permute-start | bytes 3145736 | tf_op jit(solution)/shard_map/ppermute | solution.py:322
  87.4 9.9 %collective-permute-start.14 = (bf16[2,128,2048]{2,1,0:T(8,128)(2,1)S(1)}, bf16[2,128,2048]{2,1,0:T(8,128)(2,1)S(1)}, u32[]{:S(2)}, u32[]{:S(2)}) collective-permute-start(bf16[2,128,2048]{2,1,0:T(8,128)(2,1)S(1)} %collective-permute-done.12.refs_3_), channel_id=1, source_target_pairs={{0,1},{1,0},{2,3},{3,2},{4,5},{5,4},{6,7},{7,6},{8,9},{9,8},{10,11... | collective-permute-start | bytes 3145736 | tf_op jit(solution)/shard_map/ppermute | solution.py:322
  89.9 13.9 %collective-permute-start.11 = (bf16[2,128,2048]{2,1,0:T(8,128)(2,1)S(1)}, bf16[2,128,2048]{2,1,0:T(8,128)(2,1)S(1)}, u32[]{:S(2)}, u32[]{:S(2)}) collective-permute-start(bf16[2,128,2048]{2,1,0:T(8,128)(2,1)S(1)} %get-tuple-element.138), channel_id=1, source_target_pairs={{0,2},{1,7},{2,4},{3,1},{4,6},{5,3},{6,0},{7,5},{8,10},{9,15},{10,... | collective-permute-start | bytes 3145736 | tf_op jit(solution)/shard_map/ppermute | solution.py:322
  103.8 6.1 %collective-permute-start.16 = (bf16[2,128,2048]{2,1,0:T(8,128)(2,1)S(1)}, bf16[2,128,2048]{2,1,0:T(8,128)(2,1)S(1)}, u32[]{:S(2)}, u32[]{:S(2)}) collective-permute-start(bf16[2,128,2048]{2,1,0:T(8,128)(2,1)S(1)} %collective-permute-done.11.refs_2_), channel_id=1, source_target_pairs={{0,1},{1,0},{2,3},{3,2},{4,5},{5,4},{6,7},{7,6},{8,9},{9,8},{10,11... | collective-permute-start | bytes 3145736 | tf_op jit(solution)/shard_map/ppermute | solution.py:322
  105.9 13.9 %collective-permute-start.10 = (bf16[2,128,2048]{2,1,0:T(8,128)(2,1)S(1)}, bf16[2,128,2048]{2,1,0:T(8,128)(2,1)S(1)}, u32[]{:S(2)}, u32[]{:S(2)}) collective-permute-start(bf16[2,128,2048]{2,1,0:T(8,128)(2,1)S(1)} %get-tuple-element.137), channel_id=1, source_target_pairs={{0,2},{1,7},{2,4},{3,1},{4,6},{5,3},{6,0},{7,5},{8,10},{9,15},{10,... | collective-permute-start | bytes 3145736 | tf_op jit(solution)/shard_map/ppermute | solution.py:322
  119.8 6.1 %collective-permute-start.17 = (bf16[2,128,2048]{2,1,0:T(8,128)(2,1)S(1)}, bf16[2,128,2048]{2,1,0:T(8,128)(2,1)S(1)}, u32[]{:S(2)}, u32[]{:S(2)}) collective-permute-start(bf16[2,128,2048]{2,1,0:T(8,128)(2,1)S(1)} %collective-permute-done.10.refs_2_), channel_id=1, source_target_pairs={{0,1},{1,0},{2,3},{3,2},{4,5},{5,4},{6,7},{7,6},{8,9},{9,8},{10,11... | collective-permute-start | bytes 3145736 | tf_op jit(solution)/shard_map/ppermute | solution.py:322
  121.9 13.9 %collective-permute-start.9 = (bf16[2,128,2048]{2,1,0:T(8,128)(2,1)S(1)}, bf16[2,128,2048]{2,1,0:T(8,128)(2,1)S(1)}, u32[]{:S(2)}, u32[]{:S(2)}) collective-permute-start(bf16[2,128,2048]{2,1,0:T(8,128)(2,1)S(1)} %get-tuple-element.136), channel_id=1, source_target_pairs={{0,2},{1,7},{2,4},{3,1},{4,6},{5,3},{6,0},{7,5},{8,10},{9,15},{10,... | collective-permute-start | bytes 3145736 | tf_op jit(solution)/shard_map/ppermute | solution.py:322
  135.9 6.1 %collective-permute-start.18 = (bf16[2,128,2048]{2,1,0:T(8,128)(2,1)S(1)}, bf16[2,128,2048]{2,1,0:T(8,128)(2,1)S(1)}, u32[]{:S(2)}, u32[]{:S(2)}) collective-permute-start(bf16[2,128,2048]{2,1,0:T(8,128)(2,1)S(1)} %collective-permute-done.9.refs_2_), channel_id=1, source_target_pairs={{0,1},{1,0},{2,3},{3,2},{4,5},{5,4},{6,7},{7,6},{8,9},{9,8},{10,11... | collective-permute-start | bytes 3145736 | tf_op jit(solution)/shard_map/ppermute | solution.py:322

commit v5 on v4

--- a/solution.py
+++ b/solution.py
@@ -92,16 +92,16 @@
     )(in_hbm(x), in_hbm(scale))
 
 
-def join(joined, mine, first, theirs):
-    n, half = theirs.shape[:2]
+def join(joined, mine, theirs, first, at):
+    n, half = joined.shape[0], theirs.shape[1]
     core = lax.rem(lax.axis_index("tp"), 2)
     for s in range(n):
         joined[s, pl.ds(pl.multiple_of(core * half, half), half)] = mine[first + s]
-        joined[s, pl.ds(pl.multiple_of((1 - core) * half, half), half)] = theirs[s]
+        joined[s, pl.ds(pl.multiple_of((1 - core) * half, half), half)] = theirs[at + s]
 
 
 def second_kernel(n_slots, x_ref, scale_ref, wk_ref, wv_ref, y_ref, *refs):
-    theirs, refs = refs[:n_slots], refs[n_slots:]
+    theirs, refs = refs[:2], refs[2:]
     slots, refs = refs[:n_slots], refs[n_slots:]
     wk_out, wv_out, stage, xbuf, block, scale_buf, in_sem, scale_sem, w_sem, send_sem, recv_sem = refs
     half = x_ref.shape[1]
@@ -138,7 +138,8 @@
         load(i).start()
     for copy in load_weights(0):
         copy.start()
-    to_theirs = [send(i, xbuf.at[i], theirs[i]) for i in range(n_slots)]
+    parts = block.shape[0]
+    to_theirs = [send(i, xbuf.at[i], theirs[i // parts].at[pl.ds(i % parts * PIECE, PIECE)]) for i in range(n_slots)]
     to_slots = [send(n_slots + i, y_ref.at[pl.ds(i * PIECE, PIECE)], slots[i].at[:, rows]) for i in range(n_slots)]
     get_scale.wait()
     scale = scale_buf[...].astype(jnp.float32).reshape(1, -1)
@@ -153,10 +154,9 @@
     for copy in to_slots:
         copy.start()
     to_theirs[-1].start()
-    parts = block.shape[0]
     for i in range(parts):
         to_theirs[i].wait_recv()
-        join(block.at[i], y_ref, i * PIECE, theirs[i])
+        join(block.at[i], y_ref, theirs[0], i * PIECE, i * PIECE)
     chunks = stage.shape[0]
 
     @pl.loop(0, chunks)
@@ -186,9 +186,9 @@
     batch, half, d = x.shape
     n_slots = batch // PIECE // 2
     parts = 2
-    theirs = jax.ShapeDtypeStruct((PIECE, half, d), x.dtype)
+    theirs = tuple(jax.ShapeDtypeStruct((n * PIECE, half, d), x.dtype) for n in (parts, n_slots - parts))
     slot = jax.ShapeDtypeStruct((PIECE, 2 * half, d), x.dtype)
-    out_shape = (theirs,) * n_slots + (slot,) * n_slots
+    out_shape = theirs + (slot,) * n_slots
     out_shape += tuple(jax.ShapeDtypeStruct(w.shape, w.dtype) for w in weights)
     out_shape += (stage_shape(weights, PIECE * parts, 2 * half),)
     outs = pl.pallas_call(
@@ -210,10 +210,10 @@
         cost_estimate=pl.CostEstimate(flops=64 * x.size, bytes_accessed=4 * x.size, transcendentals=0),
         name="prep2",
     )(in_hbm(x), in_hbm(scale), *map(in_hbm, weights), y)
-    return outs[:n_slots], outs[n_slots:2 * n_slots], outs[2 * n_slots:-1], outs[-1]
-
-
-def project_kernel(plan, sources, n_pieces, carried, n_alias, keep, keep_joined, *refs):
+    return outs[:2], outs[2:2 + n_slots], outs[2 + n_slots:-1], outs[-1]
+
+
+def project_kernel(plan, sources, n_pieces, carried, n_alias, keep, keep_joined, unroll, *refs):
     w_refs, refs = refs[:2], refs[2:]
     pieces, refs = refs[:n_pieces], refs[n_pieces:]
     before, refs = refs[0], refs[1 + n_alias:]
@@ -231,9 +231,9 @@
     tokens = []
     for source in sources:
         if len(source) > 1:
-            mine, first, theirs = source
+            mine, theirs, first, at = source
             tokens.append(next(joined))
-            join(tokens[-1], pieces[mine], first, pieces[theirs])
+            join(tokens[-1], pieces[mine], pieces[theirs], first, at)
         else:
             tokens.append(pieces[source[0]])
     used = 0
@@ -241,6 +241,13 @@
         mine = tokens[used:used + len(block)]
         used += len(block)
         last = i == len(plan) - 1 and keep
+        if unroll:
+            for c in range(chunks):
+                matmul_block(w_refs, mine, stage, c)
+                if not keep and c >= chunks - 2:
+                    for copy in [copy for done in (range(c + 1) if c == chunks - 2 else [c]) for copy in put(i, done)]:
+                        copy.start()
+            continue
 
         @pl.loop(0, chunks)
         def _(c):
@@ -260,22 +267,22 @@
 
     for copy in late:
         copy.wait()
-    for c in range(chunks - 1 if keep else chunks):
+    for c in range((0 if unroll else chunks - 1) if keep else chunks):
         for copy in put(len(plan) - 1, c):
             copy.wait()
 
 
-def project(weights, blocks, out, carry, batch, tp, keep, keep_joined):
+def project(weights, blocks, out, carry, batch, tp, keep, keep_joined, unroll):
     layers, hk, d = weights[0].shape
     pieces, sources, joined, plan = [], [], (), []
     for block in blocks:
         entry = []
         for piece, *where in block:
             if isinstance(piece, tuple):
-                mine, first, theirs = piece
-                sources.append((len(pieces), first, len(pieces) + 1))
+                mine, theirs, first, at = piece
+                sources.append((len(pieces), len(pieces) + 1, first, at))
                 pieces += [mine, theirs]
-                n, half, _ = theirs.shape
+                n, half = PIECE, theirs.shape[1]
                 joined += (jax.ShapeDtypeStruct((n, 2 * half, d), theirs.dtype),)
                 group = 2 * half
             else:
@@ -292,7 +299,7 @@
     before, before_entry, chunks = carry
     tok = sum(n for entry in plan for n, *_ in entry) * group
     outs = pl.pallas_call(
-        functools.partial(project_kernel, plan, tuple(sources), len(pieces), (before_entry, chunks), n_alias, keep, keep_joined),
+        functools.partial(project_kernel, plan, tuple(sources), len(pieces), (before_entry, chunks), n_alias, keep, keep_joined, unroll),
         out_shape=(shape, shape) + (stage,) * keep + joined * keep_joined,
         in_specs=[VMEM] * n_in + [ANY] * n_alias,
         out_specs=(ANY, ANY) + (VMEM,) * (keep + len(joined) * keep_joined),
@@ -308,7 +315,8 @@
             transcendentals=0,
         ),
     )(*weights, *pieces, before, *(out or ()))
-    carry = (outs[2], plan[-1], (stage.shape[0] - 1,)) if keep else None
+    chunks = stage.shape[0]
+    carry = (outs[2], plan[-1], tuple(range(0 if unroll else chunks - 1, chunks))) if keep else None
     return outs[:2], carry, outs[2 + keep:]
 
 
@@ -332,8 +340,8 @@
 
         state = {"out": None}
 
-        def run(blocks, keep=True, keep_joined=True):
-            state["out"], state["carry"], joined = project(weights, blocks, state["out"], state["carry"], batch, tp, keep, keep_joined)
+        def run(blocks, keep=True, keep_joined=True, unroll=False):
+            state["out"], state["carry"], joined = project(weights, blocks, state["out"], state["carry"], batch, tp, keep, keep_joined, unroll)
             return joined
 
         def hold(*arrays):
@@ -347,7 +355,7 @@
         state["carry"] = (stage, tuple((PIECE, *own(i)) for i in range(2)), tuple(range(stage.shape[0])))
         nz = [send(v, ring) for v in other]
         n3 = send(slots[0], ring)
-        run([[((y, 2 * PIECE, other[2]), *own(2)), (slots[0], *own(3))]], keep_joined=False)
+        run([[((y, other[1], 2 * PIECE, 0), *own(2)), (slots[0], *own(3))]], keep_joined=False)
         run([[(slots[1], *own(4)), (slots[2], *own(5))]])
 
         LEFT, RIGHT = chips - 1, 1
@@ -356,12 +364,12 @@
         mine = lambda p, where: (p, *where)
         theirs = lambda q, where: (q, *where[::-1])
 
-        py, z0, z1 = hold(ny, nz[0], nz[1])
+        py, z0 = hold(ny, nz[0])
         n4, n5 = send(slots[1], ring), send(slots[2], ring)
-        p0, p1 = run([[mine((py, 0, z0), near(0)), mine((py, PIECE, z1), near(1))]])
+        p0, p1 = run([[mine((py, z0, 0, 0), near(0)), mine((py, z0, PIECE, PIECE), near(1))]])
         q0, q1 = send(p0, swap), send(p1, swap)
-        z2 = hold(nz[2])
-        p2, = run([[mine((py, 2 * PIECE, z2), near(2))]])
+        z1 = hold(nz[1])
+        p2, = run([[mine((py, z1, 2 * PIECE, 0), near(2))]])
         q2 = send(p2, swap)
         run([[theirs(q0, near(0)), theirs(q1, near(1))]])
         p3 = hold(n3)
@@ -378,9 +386,9 @@
         for i, v in enumerate((f0, f1, f2)):
             p = hold(v)
             q = send(p, swap)
-            run([[mine(p, far(i))]])
+            run([[mine(p, far(i))]], unroll=i == 2)
             q = hold(q)
-            run([[theirs(q, far(i))]], keep=i < 2)
+            run([[theirs(q, far(i))]], keep=i < 2, unroll=i == 2)
         out = state["out"]
         to_cache = lambda o: o.reshape(layers, batch, heads, k, -1).transpose(0, 1, 4, 2, 3)
         return to_cache(out[0]), to_cache(out[1])

time: 147 us -> 146 us (level)
    ppermute x19 -> x18, waiting for transfers between devices: 23.1 us -> 23.7 us  [send(): return lax.ppermute(v, 'tp', perm)]
    ppermute x19 -> x18, starting transfers between devices: 24.7 us -> 24.1 us  [send(): return lax.ppermute(v, 'tp', perm)]
  transfers between devices with their start and end apart: 19 -> 18, of which waited for: 6 -> 7; matrix products, arithmetic and copies ran while one was open for 0% -> 0% of each run, Pallas kernels for 57% -> 57%
where the time goes in v5:
time: 146 us
  Pallas kernels  97.5 us (67%)
  starting transfers between devices  24.1 us (17%)
  waiting for transfers between devices  23.7 us (16%)
    pallas_call x15, Pallas kernels, project(): pl.pallas_call(functools.partial(project_kernel, plan, tuple(sources), le...  84.4 us
    ppermute x18, starting transfers between devices, send(): return lax.ppermute(v, 'tp', perm)  24.1 us
    ppermute x18, waiting for transfers between devices, send(): return lax.ppermute(v, 'tp', perm)  23.7 us
    pallas_call x1, Pallas kernels, prepare(): pl.pallas_call(functools.partial(second_kernel, n_slots), out_shape=out_s...  11 us
  transfers between devices with their start and end apart: 18, of which 7 were waited for; matrix products, arithmetic and copies ran while one was open for 0% of the time, Pallas kernels for 57%

profile of v5, /device:TPU:81, one launch (start us, length us, event | category | flops | bytes accessed | tf_op | source)
XLA Modules:
  0.0 146.3 jit_solution(4856899571882991905)
XLA Ops:
  2.7 3.8 %collective-permute-start.1 = (bf16[6,64,2048]{2,1,0:T(8,128)(2,1)S(1)}, bf16[6,64,2048]{2,1,0:T(8,128)(2,1)S(1)}, u32[]{:S(2)}, u32[]{:S(2)}) collective-permute-start(bf16[6,64,2048]{2,1,0:T(8,128)(2,1)S(1)} %first.1.y_ref.refs_2_), channel_id=1, source_target_pairs={{0,2},{1,7},{2,4},{3,1},{4,6},{5,3},{6,0},{7,5},{8,10},{9,15},{10,... | collective-permute-start | bytes 4718600 | tf_op jit(solution)/shard_map/ppermute | solution.py:330
  6.5 11.0 %prep2.1 = (bf16[4,64,2048]{2,1,0:T(8,128)(2,1)S(1)}, bf16[2,64,2048]{2,1,0:T(8,128)(2,1)S(1)}, bf16[2,128,2048]{2,1,0:T(8,128)(2,1)S(1)}, bf16[2,128,2048]{2,1,...) custom-call(bf16[12,64,2048]{2,1,0:T(8,128)(2,1)} %x_ref.3, ...), custom_call_target="tpu_custom_call" | custom-call | flops 100663296 | bytes 6291456 | tf_op jit(solution)/shard_map/prep2/pallas_call | solution.py:194
  19.5 7.5 %shard_map.59 = (bf16[6,12,256,512]{3,2,1,0:T(8,128)(2,1)}, bf16[6,12,256,512]{3,2,1,0:T(8,128)(2,1)}, bf16[3,2,2,4,256,128]{5,4,3,2,1,0:T(8,128)(2,1)S(1)}) custom-call(bf16[6,256,2048]{2,1,0:T(8,128)(2,1)S(1)} %get-tuple-element.94.refs_0_, bf16[6,256,2048]{2,1,0:T(8,128)(2,1)S(1)} %get-tuple-element.95.refs_1_, ...), custom_call_target="tpu_custom_call" | custom-call | flops 6442450944 | bytes 5242880 | tf_op jit(solution)/shard_map/pallas_call | solution.py:301
  27.0 7.4 %shard_map.60 = (bf16[6,12,256,512]{3,2,1,0:T(8,128)(2,1)}, bf16[6,12,256,512]{3,2,1,0:T(8,128)(2,1)}, bf16[3,2,2,4,256,128]{5,4,3,2,1,0:T(8,128)(2,1)S(1)}) custom-call(bf16[6,256,2048]{2,1,0:T(8,128)(2,1)S(1)} %get-tuple-element.94.refs_0_, bf16[6,256,2048]{2,1,0:T(8,128)(2,1)S(1)} %get-tuple-element.95.refs_1_, ...), custom_call_target="tpu_custom_call", output_to_operand_aliasing={{0}: (5, {}), {1}: (6, {})} | custom-call | flops 6442450944 | bytes 5242880 | tf_op jit(solution)/shard_map/pallas_call | solution.py:301
  35.1 7.5 %shard_map.61 = (bf16[6,12,256,512]{3,2,1,0:T(8,128)(2,1)}, bf16[6,12,256,512]{3,2,1,0:T(8,128)(2,1)}, bf16[3,2,2,4,256,128]{5,4,3,2,1,0:T(8,128)(2,1)S(1)}, bf1...) custom-call(bf16[6,256,2048]{2,1,0:T(8,128)(2,1)S(1)} %get-tuple-element.94.r, ...), custom_call_target="tpu_custom_call", output_to_operand_aliasing={{0}: (7, {}), {1}: (8, {})} | custom-call | flops 6442450944 | bytes 5242880 | tf_op jit(solution)/shard_map/pallas_call | solution.py:301
  42.6 2.7 %collective-permute-start.6 = (bf16[2,128,2048]{2,1,0:T(8,128)(2,1)S(1)}, bf16[2,128,2048]{2,1,0:T(8,128)(2,1)S(1)}, u32[]{:S(2)}, u32[]{:S(2)}) collective-permute-start(bf16[2,128,2048]{2,1,0:T(8,128)(2,1)S(1)} %get-tuple-element.134), channel_id=1, source_target_pairs={{0,1},{1,0},{2,3},{3,2},{4,5},{5,4},{6,7},{7,6},{8,9},{9,8},{10,11... | collective-permute-start | bytes 3145736 | tf_op jit(solution)/shard_map/ppermute | solution.py:330
  47.0 6.7 %collective-permute-done.3.refs_3_ = bf16[2,64,2048]{2,1,0:T(8,128)(2,1)S(1)} collective-permute-done((bf16[2,64,2048]{2,1,0:T(8,128)(2,1)S(1)}, bf16[2,64,2048]{2,1,0:T(8,128)(2,1)S(1)}, u32[]{:S(2)}, u32[]{:S(2)}) %collective-permute-start.3) | collective-permute-done | bytes 524320 | tf_op jit(solution)/shard_map/ppermute | solution.py:330
  53.7 4.1 %shard_map.62 = (bf16[6,12,256,512]{3,2,1,0:T(8,128)(2,1)}, bf16[6,12,256,512]{3,2,1,0:T(8,128)(2,1)}, bf16[3,2,2,2,256,128]{5,4,3,2,1,0:T(8,128)(2,1)S(1)}, bf16[2,128,2048]{2,1,0:T(8,128)(2,1)S(1)}) custom-call(bf16[6,256,2048]{2,1,0:T(8,128)(2,1)S(1)} %get-tuple-element.94.refs_0_, ...), custom_call_target="tpu_custom_call", output_to_operand_aliasing={{0}: (5, {}), {1}: (6, {})} | custom-call | flops 3221225472 | bytes 2621440 | tf_op jit(solution)/shard_map/pallas_call | solution.py:301
  57.9 2.5 %collective-permute-start.4 = (bf16[2,128,2048]{2,1,0:T(8,128)(2,1)S(1)}, bf16[2,128,2048]{2,1,0:T(8,128)(2,1)S(1)}, u32[]{:S(2)}, u32[]{:S(2)}) collective-permute-start(bf16[2,128,2048]{2,1,0:T(8,128)(2,1)S(1)} %get-tuple-element.132), channel_id=1, source_target_pairs={{0,1},{1,0},{2,3},{3,2},{4,5},{5,4},{6,7},{7,6},{8,9},{9,8},{10,11... | collective-permute-start | bytes 3145736 | tf_op jit(solution)/shard_map/ppermute | solution.py:330
  60.4 7.3 %shard_map.63 = (bf16[6,12,256,512]{3,2,1,0:T(8,128)(2,1)}, bf16[6,12,256,512]{3,2,1,0:T(8,128)(2,1)}, bf16[3,2,2,4,256,128]{5,4,3,2,1,0:T(8,128)(2,1)S(1)}) custom-call(bf16[6,256,2048]{2,1,0:T(8,128)(2,1)S(1)} %get-tuple-element.94.refs_0_, bf16[6,256,2048]{2,1,0:T(8,128)(2,1)S(1)} %get-tuple-element.95.refs_1_, ...), custom_call_target="tpu_custom_call", output_to_operand_aliasing={{0}: (5, {}), {1}: (6, {})} | custom-call | flops 6442450944 | bytes 5242880 | tf_op jit(solution)/shard_map/pallas_call | solution.py:301
  68.0 7.4 %shard_map.64 = (bf16[6,12,256,512]{3,2,1,0:T(8,128)(2,1)}, bf16[6,12,256,512]{3,2,1,0:T(8,128)(2,1)}, bf16[3,2,2,4,256,128]{5,4,3,2,1,0:T(8,128)(2,1)S(1)}) custom-call(bf16[6,256,2048]{2,1,0:T(8,128)(2,1)S(1)} %get-tuple-element.94.refs_0_, bf16[6,256,2048]{2,1,0:T(8,128)(2,1)S(1)} %get-tuple-element.95.refs_1_, ...), custom_call_target="tpu_custom_call", output_to_operand_aliasing={{0}: (5, {}), {1}: (6, {})} | custom-call | flops 6442450944 | bytes 5242880 | tf_op jit(solution)/shard_map/pallas_call | solution.py:301
  76.2 2.5 %collective-permute-start.14 = (bf16[2,128,2048]{2,1,0:T(8,128)(2,1)S(1)}, bf16[2,128,2048]{2,1,0:T(8,128)(2,1)S(1)}, u32[]{:S(2)}, u32[]{:S(2)}) collective-permute-start(bf16[2,128,2048]{2,1,0:T(8,128)(2,1)S(1)} %collective-permute-done.refs_3_), channel_id=1, source_target_pairs={{0,1},{1,0},{2,3},{3,2},{4,5},{5,4},{6,7},{7,6},{8,9},{9,8},{10,11... | collective-permute-start | bytes 3145736 | tf_op jit(solution)/shard_map/ppermute | solution.py:330
  78.6 7.4 %shard_map.65 = (bf16[6,12,256,512]{3,2,1,0:T(8,128)(2,1)}, bf16[6,12,256,512]{3,2,1,0:T(8,128)(2,1)}, bf16[3,2,2,4,256,128]{5,4,3,2,1,0:T(8,128)(2,1)S(1)}) custom-call(bf16[6,256,2048]{2,1,0:T(8,128)(2,1)S(1)} %get-tuple-element.94.refs_0_, bf16[6,256,2048]{2,1,0:T(8,128)(2,1)S(1)} %get-tuple-element.95.refs_1_, ...), custom_call_target="tpu_custom_call", output_to_operand_aliasing={{0}: (5, {}), {1}: (6, {})} | custom-call | flops 6442450944 | bytes 5242880 | tf_op jit(solution)/shard_map/pallas_call | solution.py:301
  87.4 2.5 %collective-permute-start.13 = (bf16[2,128,2048]{2,1,0:T(8,128)(2,1)S(1)}, bf16[2,128,2048]{2,1,0:T(8,128)(2,1)S(1)}, u32[]{:S(2)}, u32[]{:S(2)}) collective-permute-start(bf16[2,128,2048]{2,1,0:T(8,128)(2,1)S(1)} %collective-permute-done.11.refs_3_), channel_id=1, source_target_pairs={{0,1},{1,0},{2,3},{3,2},{4,5},{5,4},{6,7},{7,6},{8,9},{9,8},{10,11... | collective-permute-start | bytes 3145736 | tf_op jit(solution)/shard_map/ppermute | solution.py:330
  89.9 7.4 %shard_map.66 = (bf16[6,12,256,512]{3,2,1,0:T(8,128)(2,1)}, bf16[6,12,256,512]{3,2,1,0:T(8,128)(2,1)}, bf16[3,2,2,4,256,128]{5,4,3,2,1,0:T(8,128)(2,1)S(1)}) custom-call(bf16[6,256,2048]{2,1,0:T(8,128)(2,1)S(1)} %get-tuple-element.94.refs_0_, bf16[6,256,2048]{2,1,0:T(8,128)(2,1)S(1)} %get-tuple-element.95.refs_1_, ...), custom_call_target="tpu_custom_call", output_to_operand_aliasing={{0}: (5, {}), {1}: (6, {})} | custom-call | flops 6442450944 | bytes 5242880 | tf_op jit(solution)/shard_map/pallas_call | solution.py:301
  97.3 4.1 %shard_map.67 = (bf16[6,12,256,512]{3,2,1,0:T(8,128)(2,1)}, bf16[6,12,256,512]{3,2,1,0:T(8,128)(2,1)}, bf16[3,2,2,2,256,128]{5,4,3,2,1,0:T(8,128)(2,1)S(1)}) custom-call(bf16[6,256,2048]{2,1,0:T(8,128)(2,1)S(1)} %get-tuple-element.94.refs_0_, bf16[6,256,2048]{2,1,0:T(8,128)(2,1)S(1)} %get-tuple-element.95.refs_1_, ...), custom_call_target="tpu_custom_call", output_to_operand_aliasing={{0}: (4, {}), {1}: (5, {})} | custom-call | flops 3221225472 | bytes 2621440 | tf_op jit(solution)/shard_map/pallas_call | solution.py:301
  105.9 4.0 %shard_map.68 = (bf16[6,12,256,512]{3,2,1,0:T(8,128)(2,1)}, bf16[6,12,256,512]{3,2,1,0:T(8,128)(2,1)}, bf16[3,2,2,2,256,128]{5,4,3,2,1,0:T(8,128)(2,1)S(1)}) custom-call(bf16[6,256,2048]{2,1,0:T(8,128)(2,1)S(1)} %get-tuple-element.94.refs_0_, bf16[6,256,2048]{2,1,0:T(8,128)(2,1)S(1)} %get-tuple-element.95.refs_1_, ...), custom_call_target="tpu_custom_call", output_to_operand_aliasing={{0}: (4, {}), {1}: (5, {})} | custom-call | flops 3221225472 | bytes 2621440 | tf_op jit(solution)/shard_map/pallas_call | solution.py:301
  109.9 4.0 %shard_map.69 = (bf16[6,12,256,512]{3,2,1,0:T(8,128)(2,1)}, bf16[6,12,256,512]{3,2,1,0:T(8,128)(2,1)}, bf16[3,2,2,2,256,128]{5,4,3,2,1,0:T(8,128)(2,1)S(1)}) custom-call(bf16[6,256,2048]{2,1,0:T(8,128)(2,1)S(1)} %get-tuple-element.94.refs_0_, bf16[6,256,2048]{2,1,0:T(8,128)(2,1)S(1)} %get-tuple-element.95.refs_1_, ...), custom_call_target="tpu_custom_call", output_to_operand_aliasing={{0}: (4, {}), {1}: (5, {})} | custom-call | flops 3221225472 | bytes 2621440 | tf_op jit(solution)/shard_map/pallas_call | solution.py:301
  114.0 5.9 %collective-permute-done.9.refs_2_ = bf16[2,128,2048]{2,1,0:T(8,128)(2,1)S(1)} collective-permute-done((bf16[2,128,2048]{2,1,0:T(8,128)(2,1)S(1)}, bf16[2,128,2048]{2,1,0:T(8,128)(2,1)S(1)}, u32[]{:S(2)}, u32[]{:S(2)}) %collective-permute-start.9) | collective-permute-done | bytes 1048608 | tf_op jit(solution)/shard_map/ppermute | solution.py:330
  121.9 4.0 %shard_map.70 = (bf16[6,12,256,512]{3,2,1,0:T(8,128)(2,1)}, bf16[6,12,256,512]{3,2,1,0:T(8,128)(2,1)}, bf16[3,2,2,2,256,128]{5,4,3,2,1,0:T(8,128)(2,1)S(1)}) custom-call(bf16[6,256,2048]{2,1,0:T(8,128)(2,1)S(1)} %get-tuple-element.94.refs_0_, bf16[6,256,2048]{2,1,0:T(8,128)(2,1)S(1)} %get-tuple-element.95.refs_1_, ...), custom_call_target="tpu_custom_call", output_to_operand_aliasing={{0}: (4, {}), {1}: (5, {})} | custom-call | flops 3221225472 | bytes 2621440 | tf_op jit(solution)/shard_map/pallas_call | solution.py:301
  125.9 4.0 %shard_map.71 = (bf16[6,12,256,512]{3,2,1,0:T(8,128)(2,1)}, bf16[6,12,256,512]{3,2,1,0:T(8,128)(2,1)}, bf16[3,2,2,2,256,128]{5,4,3,2,1,0:T(8,128)(2,1)S(1)}) custom-call(bf16[6,256,2048]{2,1,0:T(8,128)(2,1)S(1)} %get-tuple-element.94.refs_0_, bf16[6,256,2048]{2,1,0:T(8,128)(2,1)S(1)} %get-tuple-element.95.refs_1_, ...), custom_call_target="tpu_custom_call", output_to_operand_aliasing={{0}: (4, {}), {1}: (5, {})} | custom-call | flops 3221225472 | bytes 2621440 | tf_op jit(solution)/shard_map/pallas_call | solution.py:301
  130.0 5.9 %collective-permute-done.8.refs_2_ = bf16[2,128,2048]{2,1,0:T(8,128)(2,1)S(1)} collective-permute-done((bf16[2,128,2048]{2,1,0:T(8,128)(2,1)S(1)}, bf16[2,128,2048]{2,1,0:T(8,128)(2,1)S(1)}, u32[]{:S(2)}, u32[]{:S(2)}) %collective-permute-start.8) | collective-permute-done | bytes 1048608 | tf_op jit(solution)/shard_map/ppermute | solution.py:330
  137.9 3.6 %shard_map.72 = (bf16[6,12,256,512]{3,2,1,0:T(8,128)(2,1)}, bf16[6,12,256,512]{3,2,1,0:T(8,128)(2,1)}, bf16[3,2,2,2,256,128]{5,4,3,2,1,0:T(8,128)(2,1)S(1)}) custom-call(bf16[6,256,2048]{2,1,0:T(8,128)(2,1)S(1)} %get-tuple-element.94.refs_0_, bf16[6,256,2048]{2,1,0:T(8,128)(2,1)S(1)} %get-tuple-element.95.refs_1_, ...), custom_call_target="tpu_custom_call", output_to_operand_aliasing={{0}: (4, {}), {1}: (5, {})} | custom-call | flops 3221225472 | bytes 2621440 | tf_op jit(solution)/shard_map/pallas_call | solution.py:301
  141.5 4.6 %shard_map.73 = (bf16[6,12,256,512]{3,2,1,0:T(8,128)(2,1)}, bf16[6,12,256,512]{3,2,1,0:T(8,128)(2,1)}) custom-call(bf16[6,256,2048]{2,1,0:T(8,128)(2,1)S(1)} %get-tuple-element.94.refs_0_, bf16[6,256,2048]{2,1,0:T(8,128)(2,1)S(1)} %get-tuple-element.95.refs_1_, ...), custom_call_target="tpu_custom_call", output_to_operand_aliasing={{0}: (4, {}), {1}: (5, {})} | custom-call | flops 3221225472 | bytes 2621440 | tf_op jit(solution)/shard_map/pallas_call | solution.py:301
  (29 shorter events, 17.5 us)
Async XLA Ops:
  2.7 32.4 %collective-permute-start.1 = (bf16[6,64,2048]{2,1,0:T(8,128)(2,1)S(1)}, bf16[6,64,2048]{2,1,0:T(8,128)(2,1)S(1)}, u32[]{:S(2)}, u32[]{:S(2)}) collective-permute-start(bf16[6,64,2048]{2,1,0:T(8,128)(2,1)S(1)} %first.1.y_ref.refs_2_), channel_id=1, source_target_pairs={{0,2},{1,7},{2,4},{3,1},{4,6},{5,3},{6,0},{7,5},{8,10},{9,15},{10,... | collective-permute-start | bytes 4718600 | tf_op jit(solution)/shard_map/ppermute | solution.py:330
  17.5 17.6 %collective-permute-start.2 = (bf16[4,64,2048]{2,1,0:T(8,128)(2,1)S(1)}, bf16[4,64,2048]{2,1,0:T(8,128)(2,1)S(1)}, u32[]{:S(2)}, u32[]{:S(2)}) collective-permute-start(bf16[4,64,2048]{2,1,0:T(8,128)(2,1)S(1)} %get-tuple-element.97), channel_id=1, source_target_pairs={{0,2},{1,7},{2,4},{3,1},{4,6},{5,3},{6,0},{7,5},{8,10},{9,15},{10,... | collective-permute-start | bytes 3145736 | tf_op jit(solution)/shard_map/ppermute | solution.py:330
  42.6 17.8 %collective-permute-start.6 = (bf16[2,128,2048]{2,1,0:T(8,128)(2,1)S(1)}, bf16[2,128,2048]{2,1,0:T(8,128)(2,1)S(1)}, u32[]{:S(2)}, u32[]{:S(2)}) collective-permute-start(bf16[2,128,2048]{2,1,0:T(8,128)(2,1)S(1)} %get-tuple-element.134), channel_id=1, source_target_pairs={{0,1},{1,0},{2,3},{3,2},{4,5},{5,4},{6,7},{7,6},{8,9},{9,8},{10,11... | collective-permute-start | bytes 3145736 | tf_op jit(solution)/shard_map/ppermute | solution.py:330
  45.3 15.2 %collective-permute-start.7 = (bf16[2,128,2048]{2,1,0:T(8,128)(2,1)S(1)}, bf16[2,128,2048]{2,1,0:T(8,128)(2,1)S(1)}, u32[]{:S(2)}, u32[]{:S(2)}) collective-permute-start(bf16[2,128,2048]{2,1,0:T(8,128)(2,1)S(1)} %get-tuple-element.133), channel_id=1, source_target_pairs={{0,1},{1,0},{2,3},{3,2},{4,5},{5,4},{6,7},{7,6},{8,9},{9,8},{10,11... | collective-permute-start | bytes 3145736 | tf_op jit(solution)/shard_map/ppermute | solution.py:330
  45.4 8.3 %collective-permute-start.3 = (bf16[2,64,2048]{2,1,0:T(8,128)(2,1)S(1)}, bf16[2,64,2048]{2,1,0:T(8,128)(2,1)S(1)}, u32[]{:S(2)}, u32[]{:S(2)}) collective-permute-start(bf16[2,64,2048]{2,1,0:T(8,128)(2,1)S(1)} %get-tuple-element.99.refs_3_), channel_id=1, source_target_pairs={{0,2},{1,7},{2,4},{3,1},{4,6},{5,3},{6,0},{7,5},{8,10},{9,15},{10,... | collective-permute-start | bytes 1572872 | tf_op jit(solution)/shard_map/ppermute | solution.py:330
  46.5 21.3 %collective-permute-start.5 = (bf16[2,128,2048]{2,1,0:T(8,128)(2,1)S(1)}, bf16[2,128,2048]{2,1,0:T(8,128)(2,1)S(1)}, u32[]{:S(2)}, u32[]{:S(2)}) collective-permute-start(bf16[2,128,2048]{2,1,0:T(8,128)(2,1)S(1)} %get-tuple-element.100.refs_4_), channel_id=1, source_target_pairs={{0,2},{1,7},{2,4},{3,1},{4,6},{5,3},{6,0},{7,5},{8,10},{9,15},{10,... | collective-permute-start | bytes 3145736 | tf_op jit(solution)/shard_map/ppermute | solution.py:330
  46.9 29.3 %collective-permute-start = (bf16[2,128,2048]{2,1,0:T(8,128)(2,1)S(1)}, bf16[2,128,2048]{2,1,0:T(8,128)(2,1)S(1)}, u32[]{:S(2)}, u32[]{:S(2)}) collective-permute-start(bf16[2,128,2048]{2,1,0:T(8,128)(2,1)S(1)} %get-tuple-element.96.refs_2_), channel_id=1, source_target_pairs={{0,2},{1,7},{2,4},{3,1},{4,6},{5,3},{6,0},{7,5},{8,10},{9,15},{10,... | collective-permute-start | bytes 3145736 | tf_op jit(solution)/shard_map/ppermute | solution.py:330
  57.9 10.1 %collective-permute-start.4 = (bf16[2,128,2048]{2,1,0:T(8,128)(2,1)S(1)}, bf16[2,128,2048]{2,1,0:T(8,128)(2,1)S(1)}, u32[]{:S(2)}, u32[]{:S(2)}) collective-permute-start(bf16[2,128,2048]{2,1,0:T(8,128)(2,1)S(1)} %get-tuple-element.132), channel_id=1, source_target_pairs={{0,1},{1,0},{2,3},{3,2},{4,5},{5,4},{6,7},{7,6},{8,9},{9,8},{10,11... | collective-permute-start | bytes 3145736 | tf_op jit(solution)/shard_map/ppermute | solution.py:330
  67.8 10.9 %collective-permute-start.12 = (bf16[2,128,2048]{2,1,0:T(8,128)(2,1)S(1)}, bf16[2,128,2048]{2,1,0:T(8,128)(2,1)S(1)}, u32[]{:S(2)}, u32[]{:S(2)}) collective-permute-start(bf16[2,128,2048]{2,1,0:T(8,128)(2,1)S(1)} %collective-permute-done.5.refs_3_), channel_id=1, source_target_pairs={{0,1},{1,0},{2,3},{3,2},{4,5},{5,4},{6,7},{7,6},{8,9},{9,8},{10,11... | collective-permute-start | bytes 3145736 | tf_op jit(solution)/shard_map/ppermute | solution.py:330
  67.9 19.5 %collective-permute-start.11 = (bf16[2,128,2048]{2,1,0:T(8,128)(2,1)S(1)}, bf16[2,128,2048]{2,1,0:T(8,128)(2,1)S(1)}, u32[]{:S(2)}, u32[]{:S(2)}) collective-permute-start(bf16[2,128,2048]{2,1,0:T(8,128)(2,1)S(1)} %get-tuple-element.98.refs_3_), channel_id=1, source_target_pairs={{0,2},{1,7},{2,4},{3,1},{4,6},{5,3},{6,0},{7,5},{8,10},{9,15},{10,... | collective-permute-start | bytes 3145736 | tf_op jit(solution)/shard_map/ppermute | solution.py:330
  76.2 13.7 %collective-permute-start.14 = (bf16[2,128,2048]{2,1,0:T(8,128)(2,1)S(1)}, bf16[2,128,2048]{2,1,0:T(8,128)(2,1)S(1)}, u32[]{:S(2)}, u32[]{:S(2)}) collective-permute-start(bf16[2,128,2048]{2,1,0:T(8,128)(2,1)S(1)} %collective-permute-done.refs_3_), channel_id=1, source_target_pairs={{0,1},{1,0},{2,3},{3,2},{4,5},{5,4},{6,7},{7,6},{8,9},{9,8},{10,11... | collective-permute-start | bytes 3145736 | tf_op jit(solution)/shard_map/ppermute | solution.py:330
  87.4 9.9 %collective-permute-start.13 = (bf16[2,128,2048]{2,1,0:T(8,128)(2,1)S(1)}, bf16[2,128,2048]{2,1,0:T(8,128)(2,1)S(1)}, u32[]{:S(2)}, u32[]{:S(2)}) collective-permute-start(bf16[2,128,2048]{2,1,0:T(8,128)(2,1)S(1)} %collective-permute-done.11.refs_3_), channel_id=1, source_target_pairs={{0,1},{1,0},{2,3},{3,2},{4,5},{5,4},{6,7},{7,6},{8,9},{9,8},{10,11... | collective-permute-start | bytes 3145736 | tf_op jit(solution)/shard_map/ppermute | solution.py:330
  89.9 13.9 %collective-permute-start.10 = (bf16[2,128,2048]{2,1,0:T(8,128)(2,1)S(1)}, bf16[2,128,2048]{2,1,0:T(8,128)(2,1)S(1)}, u32[]{:S(2)}, u32[]{:S(2)}) collective-permute-start(bf16[2,128,2048]{2,1,0:T(8,128)(2,1)S(1)} %get-tuple-element.134), channel_id=1, source_target_pairs={{0,2},{1,7},{2,4},{3,1},{4,6},{5,3},{6,0},{7,5},{8,10},{9,15},{10,... | collective-permute-start | bytes 3145736 | tf_op jit(solution)/shard_map/ppermute | solution.py:330
  103.8 6.1 %collective-permute-start.15 = (bf16[2,128,2048]{2,1,0:T(8,128)(2,1)S(1)}, bf16[2,128,2048]{2,1,0:T(8,128)(2,1)S(1)}, u32[]{:S(2)}, u32[]{:S(2)}) collective-permute-start(bf16[2,128,2048]{2,1,0:T(8,128)(2,1)S(1)} %collective-permute-done.10.refs_2_), channel_id=1, source_target_pairs={{0,1},{1,0},{2,3},{3,2},{4,5},{5,4},{6,7},{7,6},{8,9},{9,8},{10,11... | collective-permute-start | bytes 3145736 | tf_op jit(solution)/shard_map/ppermute | solution.py:330
  105.9 13.9 %collective-permute-start.9 = (bf16[2,128,2048]{2,1,0:T(8,128)(2,1)S(1)}, bf16[2,128,2048]{2,1,0:T(8,128)(2,1)S(1)}, u32[]{:S(2)}, u32[]{:S(2)}) collective-permute-start(bf16[2,128,2048]{2,1,0:T(8,128)(2,1)S(1)} %get-tuple-element.133), channel_id=1, source_target_pairs={{0,2},{1,7},{2,4},{3,1},{4,6},{5,3},{6,0},{7,5},{8,10},{9,15},{10,... | collective-permute-start | bytes 3145736 | tf_op jit(solution)/shard_map/ppermute | solution.py:330
  119.8 6.1 %collective-permute-start.16 = (bf16[2,128,2048]{2,1,0:T(8,128)(2,1)S(1)}, bf16[2,128,2048]{2,1,0:T(8,128)(2,1)S(1)}, u32[]{:S(2)}, u32[]{:S(2)}) collective-permute-start(bf16[2,128,2048]{2,1,0:T(8,128)(2,1)S(1)} %collective-permute-done.9.refs_2_), channel_id=1, source_target_pairs={{0,1},{1,0},{2,3},{3,2},{4,5},{5,4},{6,7},{7,6},{8,9},{9,8},{10,11... | collective-permute-start | bytes 3145736 | tf_op jit(solution)/shard_map/ppermute | solution.py:330
  121.9 13.9 %collective-permute-start.8 = (bf16[2,128,2048]{2,1,0:T(8,128)(2,1)S(1)}, bf16[2,128,2048]{2,1,0:T(8,128)(2,1)S(1)}, u32[]{:S(2)}, u32[]{:S(2)}) collective-permute-start(bf16[2,128,2048]{2,1,0:T(8,128)(2,1)S(1)} %get-tuple-element.132), channel_id=1, source_target_pairs={{0,2},{1,7},{2,4},{3,1},{4,6},{5,3},{6,0},{7,5},{8,10},{9,15},{10,... | collective-permute-start | bytes 3145736 | tf_op jit(solution)/shard_map/ppermute | solution.py:330
  135.9 5.6 %collective-permute-start.17 = (bf16[2,128,2048]{2,1,0:T(8,128)(2,1)S(1)}, bf16[2,128,2048]{2,1,0:T(8,128)(2,1)S(1)}, u32[]{:S(2)}, u32[]{:S(2)}) collective-permute-start(bf16[2,128,2048]{2,1,0:T(8,128)(2,1)S(1)} %collective-permute-done.8.refs_2_), channel_id=1, source_target_pairs={{0,1},{1,0},{2,3},{3,2},{4,5},{5,4},{6,7},{7,6},{8,9},{9,8},{10,11... | collective-permute-start | bytes 3145736 | tf_op jit(solution)/shard_map/ppermute | solution.py:330

commit v6 on v5

--- a/solution.py
+++ b/solution.py
@@ -57,9 +57,9 @@
                 stage[c, kv, l, s] = res[l * hk:(l + 1) * hk, s * group:(s + 1) * group]
 
 
-def first_kernel(x_ref, scale_ref, y_ref, xbuf, scale_buf, sem, scale_sem):
+def first_kernel(skip, x_ref, scale_ref, y_ref, xbuf, scale_buf, sem, scale_sem):
     n = y_ref.shape[0]
-    start = lax.rem(lax.axis_index("tp"), 2) * n
+    start = lax.rem(lax.axis_index("tp"), 2) * (x_ref.shape[0] // 2) + skip
     load = lambda i: pltpu.make_async_copy(x_ref.at[pl.ds(start + i, 1)], xbuf.at[pl.ds(i, 1)], sem.at[i])
     get_scale = pltpu.make_async_copy(scale_ref, scale_buf, scale_sem)
     get_scale.start()
@@ -72,11 +72,10 @@
         y_ref[i] = rms_norm(xbuf[i], scale)
 
 
-def normalize_first(x, scale):
-    batch, half, d = x.shape
-    n = batch // 2
+def normalize_first(x, scale, skip, n):
+    _, half, d = x.shape
     return pl.pallas_call(
-        first_kernel,
+        functools.partial(first_kernel, skip),
         out_shape=jax.ShapeDtypeStruct((n, half, d), x.dtype),
         in_specs=[ANY, ANY],
         out_specs=VMEM,
@@ -88,7 +87,6 @@
         ],
         compiler_params=pltpu.CompilerParams(vmem_limit_bytes=8 * 2**20),
         cost_estimate=pl.CostEstimate(flops=32 * x.size, bytes_accessed=2 * x.size, transcendentals=0),
-        name="first",
     )(in_hbm(x), in_hbm(scale))
 
 
@@ -100,7 +98,7 @@
         joined[s, pl.ds(pl.multiple_of((1 - core) * half, half), half)] = theirs[at + s]
 
 
-def second_kernel(n_slots, x_ref, scale_ref, wk_ref, wv_ref, y_ref, *refs):
+def second_kernel(n_slots, x_ref, scale_ref, wk_ref, wv_ref, y_first, y_rest, *refs):
     theirs, refs = refs[:2], refs[2:]
     slots, refs = refs[:n_slots], refs[n_slots:]
     wk_out, wv_out, stage, xbuf, block, scale_buf, in_sem, scale_sem, w_sem, send_sem, recv_sem = refs
@@ -140,7 +138,8 @@
         copy.start()
     parts = block.shape[0]
     to_theirs = [send(i, xbuf.at[i], theirs[i // parts].at[pl.ds(i % parts * PIECE, PIECE)]) for i in range(n_slots)]
-    to_slots = [send(n_slots + i, y_ref.at[pl.ds(i * PIECE, PIECE)], slots[i].at[:, rows]) for i in range(n_slots)]
+    made = [y_first] + [y_rest.at[pl.ds(i * PIECE, PIECE)] for i in range(n_slots - 1)]
+    to_slots = [send(n_slots + i, made[i], slots[i].at[:, rows]) for i in range(n_slots)]
     get_scale.wait()
     scale = scale_buf[...].astype(jnp.float32).reshape(1, -1)
     pl.semaphore_wait(barrier, 1)
@@ -156,7 +155,7 @@
     to_theirs[-1].start()
     for i in range(parts):
         to_theirs[i].wait_recv()
-        join(block.at[i], y_ref, theirs[0], i * PIECE, i * PIECE)
+        join(block.at[i], made[i], theirs[0], 0, i * PIECE)
     chunks = stage.shape[0]
 
     @pl.loop(0, chunks)
@@ -182,7 +181,7 @@
     return jax.ShapeDtypeStruct((layers // LAYERS, len(weights), LAYERS, seqs, hk, group), weights[0].dtype)
 
 
-def prepare(x, scale, weights, y):
+def prepare(x, scale, weights, y_first, y_rest):
     batch, half, d = x.shape
     n_slots = batch // PIECE // 2
     parts = 2
@@ -194,7 +193,7 @@
     outs = pl.pallas_call(
         functools.partial(second_kernel, n_slots),
         out_shape=out_shape,
-        in_specs=[ANY] * 4 + [VMEM],
+        in_specs=[ANY] * 4 + [VMEM] * 2,
         out_specs=(VMEM,) * len(out_shape),
         scratch_shapes=[
             pltpu.VMEM((n_slots, PIECE, half, d), x.dtype),
@@ -209,7 +208,7 @@
         compiler_params=pltpu.CompilerParams(vmem_limit_bytes=9 * 2**20, collective_id=0, has_side_effects=True),
         cost_estimate=pl.CostEstimate(flops=64 * x.size, bytes_accessed=4 * x.size, transcendentals=0),
         name="prep2",
-    )(in_hbm(x), in_hbm(scale), *map(in_hbm, weights), y)
+    )(in_hbm(x), in_hbm(scale), *map(in_hbm, weights), y_first, y_rest)
     return outs[:2], outs[2:2 + n_slots], outs[2 + n_slots:-1], outs[-1]
 
 
@@ -348,14 +347,16 @@
             arrays, state["out"] = lax.optimization_barrier((arrays, state["out"]))
             return arrays if len(arrays) > 1 else arrays[0]
 
-        y = normalize_first(enc_out, norm_scale)
-        ny = send(y, ring)
-        other, slots, weights, stage = prepare(enc_out, norm_scale, (wk, wv), y)
+        ya = normalize_first(enc_out, norm_scale, 0, PIECE)
+        na = send(ya, ring)
+        yb = normalize_first(enc_out, norm_scale, PIECE, batch // 2 - PIECE)
+        nb = send(yb, ring)
+        other, slots, weights, stage = prepare(enc_out, norm_scale, (wk, wv), ya, yb)
         own = lambda i: ((0, seq(i)), (0, seq(i + h)))
         state["carry"] = (stage, tuple((PIECE, *own(i)) for i in range(2)), tuple(range(stage.shape[0])))
         nz = [send(v, ring) for v in other]
         n3 = send(slots[0], ring)
-        run([[((y, other[1], 2 * PIECE, 0), *own(2)), (slots[0], *own(3))]], keep_joined=False)
+        run([[((yb, other[1], PIECE, 0), *own(2)), (slots[0], *own(3))]], keep_joined=False)
         run([[(slots[1], *own(4)), (slots[2], *own(5))]])
 
         LEFT, RIGHT = chips - 1, 1
@@ -364,12 +365,12 @@
         mine = lambda p, where: (p, *where)
         theirs = lambda q, where: (q, *where[::-1])
 
-        py, z0 = hold(ny, nz[0])
+        pa, pb, z0 = hold(na, nb, nz[0])
         n4, n5 = send(slots[1], ring), send(slots[2], ring)
-        p0, p1 = run([[mine((py, z0, 0, 0), near(0)), mine((py, z0, PIECE, PIECE), near(1))]])
+        p0, p1 = run([[mine((pa, z0, 0, 0), near(0)), mine((pb, z0, 0, PIECE), near(1))]])
         q0, q1 = send(p0, swap), send(p1, swap)
         z1 = hold(nz[1])
-        p2, = run([[mine((py, z1, 2 * PIECE, 0), near(2))]])
+        p2, = run([[mine((pb, z1, PIECE, 0), near(2))]])
         q2 = send(p2, swap)
         run([[theirs(q0, near(0)), theirs(q1, near(1))]])
         p3 = hold(n3)
@@ -382,11 +383,11 @@
         p5 = hold(n5)
         q5 = send(p5, swap)
         run([[theirs(q4, near(4)), mine(p5, near(5))]])
-        run([[theirs(q5, near(5))]])
+        run([[theirs(q5, near(5))]], unroll=True)
         for i, v in enumerate((f0, f1, f2)):
             p = hold(v)
             q = send(p, swap)
-            run([[mine(p, far(i))]], unroll=i == 2)
+            run([[mine(p, far(i))]], unroll=i != 1)
             q = hold(q)
             run([[theirs(q, far(i))]], keep=i < 2, unroll=i == 2)
         out = state["out"]

time: 146 us -> 146 us (level)
  starting transfers between devices: 24.1 us -> 22.4 us
    ppermute x18 -> x19, starting transfers between devices: 24.1 us -> 22.4 us  [send(): return lax.ppermute(v, 'tp', perm)]
    pallas_call x1 -> x2, Pallas kernels: 2.02 us -> 2.99 us  [normalize_first(): pl.pallas_call(functools.partial(first_kernel, skip), out_shape=jax.Shape...]
    ppermute x18 -> x19, waiting for transfers between devices: 23.7 us -> 23.4 us  [send(): return lax.ppermute(v, 'tp', perm)]
  transfers between devices with their start and end apart: 18 -> 19, of which waited for: 7 -> 6; matrix products, arithmetic and copies ran while one was open for 0% -> 0% of each run, Pallas kernels for 57% -> 59%
where the time goes in v6:
time: 146 us
  Pallas kernels  98.8 us (68%)
  waiting for transfers between devices  23.4 us (16%)
  starting transfers between devices  22.4 us (15%)
    pallas_call x15, Pallas kernels, project(): pl.pallas_call(functools.partial(project_kernel, plan, tuple(sources), le...  83.5 us
    ppermute x19, waiting for transfers between devices, send(): return lax.ppermute(v, 'tp', perm)  23.4 us
    ppermute x19, starting transfers between devices, send(): return lax.ppermute(v, 'tp', perm)  22.4 us
    pallas_call x1, Pallas kernels, prepare(): pl.pallas_call(functools.partial(second_kernel, n_slots), out_shape=out_s...  12.2 us
    pallas_call x2, Pallas kernels, normalize_first(): pl.pallas_call(functools.partial(first_kernel, skip), out_shape=jax.Shape...  2.99 us
  transfers between devices with their start and end apart: 19, of which 6 were waited for; matrix products, arithmetic and copies ran while one was open for 0% of the time, Pallas kernels for 59%

profile of v6, /device:TPU:81, one launch (start us, length us, event | category | flops | bytes accessed | tf_op | source)
XLA Modules:
  0.0 145.6 jit_solution(16296203332152363651)
XLA Ops:
  2.0 3.8 %collective-permute-start.1 = (bf16[2,64,2048]{2,1,0:T(8,128)(2,1)S(1)}, bf16[2,64,2048]{2,1,0:T(8,128)(2,1)S(1)}, u32[]{:S(2)}, u32[]{:S(2)}) collective-permute-start(bf16[2,64,2048]{2,1,0:T(8,128)(2,1)S(1)} %shard_map.59.y_first), channel_id=1, source_target_pairs={{0,2},{1,7},{2,4},{3,1},{4,6},{5,3},{6,0},{7,5},{8,10},{9,15},{10,... | collective-permute-start | bytes 1572872 | tf_op jit(solution)/shard_map/ppermute | solution.py:329
  7.9 12.2 %prep2.1 = (bf16[4,64,2048]{2,1,0:T(8,128)(2,1)S(1)}, bf16[2,64,2048]{2,1,0:T(8,128)(2,1)S(1)}, bf16[2,128,2048]{2,1,0:T(8,128)(2,1)S(1)}, bf16[2,128,2048]{2,1,...) custom-call(bf16[12,64,2048]{2,1,0:T(8,128)(2,1)} %x_ref.5, ...), custom_call_target="tpu_custom_call" | custom-call | flops 100663296 | bytes 6291456 | tf_op jit(solution)/shard_map/prep2/pallas_call | solution.py:193
  21.6 7.5 %shard_map.61 = (bf16[6,12,256,512]{3,2,1,0:T(8,128)(2,1)}, bf16[6,12,256,512]{3,2,1,0:T(8,128)(2,1)}, bf16[3,2,2,4,256,128]{5,4,3,2,1,0:T(8,128)(2,1)S(1)}) custom-call(bf16[6,256,2048]{2,1,0:T(8,128)(2,1)S(1)} %get-tuple-element.95.refs_0_, bf16[6,256,2048]{2,1,0:T(8,128)(2,1)S(1)} %get-tuple-element.96.refs_1_, ...), custom_call_target="tpu_custom_call" | custom-call | flops 6442450944 | bytes 5242880 | tf_op jit(solution)/shard_map/pallas_call | solution.py:300
  29.1 7.4 %shard_map.62 = (bf16[6,12,256,512]{3,2,1,0:T(8,128)(2,1)}, bf16[6,12,256,512]{3,2,1,0:T(8,128)(2,1)}, bf16[3,2,2,4,256,128]{5,4,3,2,1,0:T(8,128)(2,1)S(1)}) custom-call(bf16[6,256,2048]{2,1,0:T(8,128)(2,1)S(1)} %get-tuple-element.95.refs_0_, bf16[6,256,2048]{2,1,0:T(8,128)(2,1)S(1)} %get-tuple-element.96.refs_1_, ...), custom_call_target="tpu_custom_call", output_to_operand_aliasing={{0}: (5, {}), {1}: (6, {})} | custom-call | flops 6442450944 | bytes 5242880 | tf_op jit(solution)/shard_map/pallas_call | solution.py:300
  36.5 7.6 %shard_map.63 = (bf16[6,12,256,512]{3,2,1,0:T(8,128)(2,1)}, bf16[6,12,256,512]{3,2,1,0:T(8,128)(2,1)}, bf16[3,2,2,4,256,128]{5,4,3,2,1,0:T(8,128)(2,1)S(1)}, bf1...) custom-call(bf16[6,256,2048]{2,1,0:T(8,128)(2,1)S(1)} %get-tuple-element.95.r, ...), custom_call_target="tpu_custom_call", output_to_operand_aliasing={{0}: (7, {}), {1}: (8, {})} | custom-call | flops 6442450944 | bytes 5242880 | tf_op jit(solution)/shard_map/pallas_call | solution.py:300
  46.9 6.1 %collective-permute-done.4.refs_3_ = bf16[2,64,2048]{2,1,0:T(8,128)(2,1)S(1)} collective-permute-done((bf16[2,64,2048]{2,1,0:T(8,128)(2,1)S(1)}, bf16[2,64,2048]{2,1,0:T(8,128)(2,1)S(1)}, u32[]{:S(2)}, u32[]{:S(2)}) %collective-permute-start.4) | collective-permute-done | bytes 524320 | tf_op jit(solution)/shard_map/ppermute | solution.py:329
  53.0 4.1 %shard_map.64 = (bf16[6,12,256,512]{3,2,1,0:T(8,128)(2,1)}, bf16[6,12,256,512]{3,2,1,0:T(8,128)(2,1)}, bf16[3,2,2,2,256,128]{5,4,3,2,1,0:T(8,128)(2,1)S(1)}, bf16[2,128,2048]{2,1,0:T(8,128)(2,1)S(1)}) custom-call(bf16[6,256,2048]{2,1,0:T(8,128)(2,1)S(1)} %get-tuple-element.95.refs_0_, ...), custom_call_target="tpu_custom_call", output_to_operand_aliasing={{0}: (5, {}), {1}: (6, {})} | custom-call | flops 3221225472 | bytes 2621440 | tf_op jit(solution)/shard_map/pallas_call | solution.py:300
  57.2 2.5 %collective-permute-start.5 = (bf16[2,128,2048]{2,1,0:T(8,128)(2,1)S(1)}, bf16[2,128,2048]{2,1,0:T(8,128)(2,1)S(1)}, u32[]{:S(2)}, u32[]{:S(2)}) collective-permute-start(bf16[2,128,2048]{2,1,0:T(8,128)(2,1)S(1)} %get-tuple-element.134), channel_id=1, source_target_pairs={{0,1},{1,0},{2,3},{3,2},{4,5},{5,4},{6,7},{7,6},{8,9},{9,8},{10,11... | collective-permute-start | bytes 3145736 | tf_op jit(solution)/shard_map/ppermute | solution.py:329
  59.7 7.3 %shard_map.65 = (bf16[6,12,256,512]{3,2,1,0:T(8,128)(2,1)}, bf16[6,12,256,512]{3,2,1,0:T(8,128)(2,1)}, bf16[3,2,2,4,256,128]{5,4,3,2,1,0:T(8,128)(2,1)S(1)}) custom-call(bf16[6,256,2048]{2,1,0:T(8,128)(2,1)S(1)} %get-tuple-element.95.refs_0_, bf16[6,256,2048]{2,1,0:T(8,128)(2,1)S(1)} %get-tuple-element.96.refs_1_, ...), custom_call_target="tpu_custom_call", output_to_operand_aliasing={{0}: (5, {}), {1}: (6, {})} | custom-call | flops 6442450944 | bytes 5242880 | tf_op jit(solution)/shard_map/pallas_call | solution.py:300
  67.3 7.4 %shard_map.66 = (bf16[6,12,256,512]{3,2,1,0:T(8,128)(2,1)}, bf16[6,12,256,512]{3,2,1,0:T(8,128)(2,1)}, bf16[3,2,2,4,256,128]{5,4,3,2,1,0:T(8,128)(2,1)S(1)}) custom-call(bf16[6,256,2048]{2,1,0:T(8,128)(2,1)S(1)} %get-tuple-element.95.refs_0_, bf16[6,256,2048]{2,1,0:T(8,128)(2,1)S(1)} %get-tuple-element.96.refs_1_, ...), custom_call_target="tpu_custom_call", output_to_operand_aliasing={{0}: (5, {}), {1}: (6, {})} | custom-call | flops 6442450944 | bytes 5242880 | tf_op jit(solution)/shard_map/pallas_call | solution.py:300
  75.5 2.4 %collective-permute-start.15 = (bf16[2,128,2048]{2,1,0:T(8,128)(2,1)S(1)}, bf16[2,128,2048]{2,1,0:T(8,128)(2,1)S(1)}, u32[]{:S(2)}, u32[]{:S(2)}) collective-permute-start(bf16[2,128,2048]{2,1,0:T(8,128)(2,1)S(1)} %collective-permute-done.refs_3_), channel_id=1, source_target_pairs={{0,1},{1,0},{2,3},{3,2},{4,5},{5,4},{6,7},{7,6},{8,9},{9,8},{10,11... | collective-permute-start | bytes 3145736 | tf_op jit(solution)/shard_map/ppermute | solution.py:329
  77.9 7.4 %shard_map.67 = (bf16[6,12,256,512]{3,2,1,0:T(8,128)(2,1)}, bf16[6,12,256,512]{3,2,1,0:T(8,128)(2,1)}, bf16[3,2,2,4,256,128]{5,4,3,2,1,0:T(8,128)(2,1)S(1)}) custom-call(bf16[6,256,2048]{2,1,0:T(8,128)(2,1)S(1)} %get-tuple-element.95.refs_0_, bf16[6,256,2048]{2,1,0:T(8,128)(2,1)S(1)} %get-tuple-element.96.refs_1_, ...), custom_call_target="tpu_custom_call", output_to_operand_aliasing={{0}: (5, {}), {1}: (6, {})} | custom-call | flops 6442450944 | bytes 5242880 | tf_op jit(solution)/shard_map/pallas_call | solution.py:300
  86.7 2.4 %collective-permute-start.14 = (bf16[2,128,2048]{2,1,0:T(8,128)(2,1)S(1)}, bf16[2,128,2048]{2,1,0:T(8,128)(2,1)S(1)}, u32[]{:S(2)}, u32[]{:S(2)}) collective-permute-start(bf16[2,128,2048]{2,1,0:T(8,128)(2,1)S(1)} %collective-permute-done.12.refs_3_), channel_id=1, source_target_pairs={{0,1},{1,0},{2,3},{3,2},{4,5},{5,4},{6,7},{7,6},{8,9},{9,8},{10,11... | collective-permute-start | bytes 3145736 | tf_op jit(solution)/shard_map/ppermute | solution.py:329
  89.2 7.4 %shard_map.68 = (bf16[6,12,256,512]{3,2,1,0:T(8,128)(2,1)}, bf16[6,12,256,512]{3,2,1,0:T(8,128)(2,1)}, bf16[3,2,2,4,256,128]{5,4,3,2,1,0:T(8,128)(2,1)S(1)}) custom-call(bf16[6,256,2048]{2,1,0:T(8,128)(2,1)S(1)} %get-tuple-element.95.refs_0_, bf16[6,256,2048]{2,1,0:T(8,128)(2,1)S(1)} %get-tuple-element.96.refs_1_, ...), custom_call_target="tpu_custom_call", output_to_operand_aliasing={{0}: (5, {}), {1}: (6, {})} | custom-call | flops 6442450944 | bytes 5242880 | tf_op jit(solution)/shard_map/pallas_call | solution.py:300
  96.6 3.7 %shard_map.69 = (bf16[6,12,256,512]{3,2,1,0:T(8,128)(2,1)}, bf16[6,12,256,512]{3,2,1,0:T(8,128)(2,1)}, bf16[3,2,2,2,256,128]{5,4,3,2,1,0:T(8,128)(2,1)S(1)}) custom-call(bf16[6,256,2048]{2,1,0:T(8,128)(2,1)S(1)} %get-tuple-element.95.refs_0_, bf16[6,256,2048]{2,1,0:T(8,128)(2,1)S(1)} %get-tuple-element.96.refs_1_, ...), custom_call_target="tpu_custom_call", output_to_operand_aliasing={{0}: (4, {}), {1}: (5, {})} | custom-call | flops 3221225472 | bytes 2621440 | tf_op jit(solution)/shard_map/pallas_call | solution.py:300
  100.3 2.9 %collective-permute-done.11.refs_2_ = bf16[2,128,2048]{2,1,0:T(8,128)(2,1)S(1)} collective-permute-done((bf16[2,128,2048]{2,1,0:T(8,128)(2,1)S(1)}, bf16[2,128,2048]{2,1,0:T(8,128)(2,1)S(1)}, u32[]{:S(2)}, u32[]{:S(2)}) %collective-permute-start.11) | collective-permute-done | bytes 1048608 | tf_op jit(solution)/shard_map/ppermute | solution.py:329
  105.2 3.6 %shard_map.70 = (bf16[6,12,256,512]{3,2,1,0:T(8,128)(2,1)}, bf16[6,12,256,512]{3,2,1,0:T(8,128)(2,1)}, bf16[3,2,2,2,256,128]{5,4,3,2,1,0:T(8,128)(2,1)S(1)}) custom-call(bf16[6,256,2048]{2,1,0:T(8,128)(2,1)S(1)} %get-tuple-element.95.refs_0_, bf16[6,256,2048]{2,1,0:T(8,128)(2,1)S(1)} %get-tuple-element.96.refs_1_, ...), custom_call_target="tpu_custom_call", output_to_operand_aliasing={{0}: (4, {}), {1}: (5, {})} | custom-call | flops 3221225472 | bytes 2621440 | tf_op jit(solution)/shard_map/pallas_call | solution.py:300
  108.8 4.1 %shard_map.71 = (bf16[6,12,256,512]{3,2,1,0:T(8,128)(2,1)}, bf16[6,12,256,512]{3,2,1,0:T(8,128)(2,1)}, bf16[3,2,2,2,256,128]{5,4,3,2,1,0:T(8,128)(2,1)S(1)}) custom-call(bf16[6,256,2048]{2,1,0:T(8,128)(2,1)S(1)} %get-tuple-element.95.refs_0_, bf16[6,256,2048]{2,1,0:T(8,128)(2,1)S(1)} %get-tuple-element.96.refs_1_, ...), custom_call_target="tpu_custom_call", output_to_operand_aliasing={{0}: (4, {}), {1}: (5, {})} | custom-call | flops 3221225472 | bytes 2621440 | tf_op jit(solution)/shard_map/pallas_call | solution.py:300
  112.8 6.3 %collective-permute-done.10.refs_2_ = bf16[2,128,2048]{2,1,0:T(8,128)(2,1)S(1)} collective-permute-done((bf16[2,128,2048]{2,1,0:T(8,128)(2,1)S(1)}, bf16[2,128,2048]{2,1,0:T(8,128)(2,1)S(1)}, u32[]{:S(2)}, u32[]{:S(2)}) %collective-permute-start.10) | collective-permute-done | bytes 1048608 | tf_op jit(solution)/shard_map/ppermute | solution.py:329
  121.2 4.0 %shard_map.72 = (bf16[6,12,256,512]{3,2,1,0:T(8,128)(2,1)}, bf16[6,12,256,512]{3,2,1,0:T(8,128)(2,1)}, bf16[3,2,2,2,256,128]{5,4,3,2,1,0:T(8,128)(2,1)S(1)}) custom-call(bf16[6,256,2048]{2,1,0:T(8,128)(2,1)S(1)} %get-tuple-element.95.refs_0_, bf16[6,256,2048]{2,1,0:T(8,128)(2,1)S(1)} %get-tuple-element.96.refs_1_, ...), custom_call_target="tpu_custom_call", output_to_operand_aliasing={{0}: (4, {}), {1}: (5, {})} | custom-call | flops 3221225472 | bytes 2621440 | tf_op jit(solution)/shard_map/pallas_call | solution.py:300
  125.2 4.0 %shard_map.73 = (bf16[6,12,256,512]{3,2,1,0:T(8,128)(2,1)}, bf16[6,12,256,512]{3,2,1,0:T(8,128)(2,1)}, bf16[3,2,2,2,256,128]{5,4,3,2,1,0:T(8,128)(2,1)S(1)}) custom-call(bf16[6,256,2048]{2,1,0:T(8,128)(2,1)S(1)} %get-tuple-element.95.refs_0_, bf16[6,256,2048]{2,1,0:T(8,128)(2,1)S(1)} %get-tuple-element.96.refs_1_, ...), custom_call_target="tpu_custom_call", output_to_operand_aliasing={{0}: (4, {}), {1}: (5, {})} | custom-call | flops 3221225472 | bytes 2621440 | tf_op jit(solution)/shard_map/pallas_call | solution.py:300
  129.3 5.9 %collective-permute-done.9.refs_2_ = bf16[2,128,2048]{2,1,0:T(8,128)(2,1)S(1)} collective-permute-done((bf16[2,128,2048]{2,1,0:T(8,128)(2,1)S(1)}, bf16[2,128,2048]{2,1,0:T(8,128)(2,1)S(1)}, u32[]{:S(2)}, u32[]{:S(2)}) %collective-permute-start.9) | collective-permute-done | bytes 1048608 | tf_op jit(solution)/shard_map/ppermute | solution.py:329
  137.2 3.6 %shard_map.74 = (bf16[6,12,256,512]{3,2,1,0:T(8,128)(2,1)}, bf16[6,12,256,512]{3,2,1,0:T(8,128)(2,1)}, bf16[3,2,2,2,256,128]{5,4,3,2,1,0:T(8,128)(2,1)S(1)}) custom-call(bf16[6,256,2048]{2,1,0:T(8,128)(2,1)S(1)} %get-tuple-element.95.refs_0_, bf16[6,256,2048]{2,1,0:T(8,128)(2,1)S(1)} %get-tuple-element.96.refs_1_, ...), custom_call_target="tpu_custom_call", output_to_operand_aliasing={{0}: (4, {}), {1}: (5, {})} | custom-call | flops 3221225472 | bytes 2621440 | tf_op jit(solution)/shard_map/pallas_call | solution.py:300
  140.8 4.6 %shard_map.75 = (bf16[6,12,256,512]{3,2,1,0:T(8,128)(2,1)}, bf16[6,12,256,512]{3,2,1,0:T(8,128)(2,1)}) custom-call(bf16[6,256,2048]{2,1,0:T(8,128)(2,1)S(1)} %get-tuple-element.95.refs_0_, bf16[6,256,2048]{2,1,0:T(8,128)(2,1)S(1)} %get-tuple-element.96.refs_1_, ...), custom_call_target="tpu_custom_call", output_to_operand_aliasing={{0}: (4, {}), {1}: (5, {})} | custom-call | flops 3221225472 | bytes 2621440 | tf_op jit(solution)/shard_map/pallas_call | solution.py:300
  (32 shorter events, 16.4 us)
Async XLA Ops:
  2.0 34.5 %collective-permute-start.1 = (bf16[2,64,2048]{2,1,0:T(8,128)(2,1)S(1)}, bf16[2,64,2048]{2,1,0:T(8,128)(2,1)S(1)}, u32[]{:S(2)}, u32[]{:S(2)}) collective-permute-start(bf16[2,64,2048]{2,1,0:T(8,128)(2,1)S(1)} %shard_map.59.y_first), channel_id=1, source_target_pairs={{0,2},{1,7},{2,4},{3,1},{4,6},{5,3},{6,0},{7,5},{8,10},{9,15},{10,... | collective-permute-start | bytes 1572872 | tf_op jit(solution)/shard_map/ppermute | solution.py:329
  7.4 29.1 %collective-permute-start.2 = (bf16[4,64,2048]{2,1,0:T(8,128)(2,1)S(1)}, bf16[4,64,2048]{2,1,0:T(8,128)(2,1)S(1)}, u32[]{:S(2)}, u32[]{:S(2)}) collective-permute-start(bf16[4,64,2048]{2,1,0:T(8,128)(2,1)S(1)} %shard_map.60.y_rest.refs_2_), channel_id=1, source_target_pairs={{0,2},{1,7},{2,4},{3,1},{4,6},{5,3},{6,0},{7,5},{8,10},{9,15},{10,... | collective-permute-start | bytes 3145736 | tf_op jit(solution)/shard_map/ppermute | solution.py:329
  20.2 16.3 %collective-permute-start.3 = (bf16[4,64,2048]{2,1,0:T(8,128)(2,1)S(1)}, bf16[4,64,2048]{2,1,0:T(8,128)(2,1)S(1)}, u32[]{:S(2)}, u32[]{:S(2)}) collective-permute-start(bf16[4,64,2048]{2,1,0:T(8,128)(2,1)S(1)} %get-tuple-element.98), channel_id=1, source_target_pairs={{0,2},{1,7},{2,4},{3,1},{4,6},{5,3},{6,0},{7,5},{8,10},{9,15},{10,... | collective-permute-start | bytes 3145736 | tf_op jit(solution)/shard_map/ppermute | solution.py:329
  44.1 15.6 %collective-permute-start.7 = (bf16[2,128,2048]{2,1,0:T(8,128)(2,1)S(1)}, bf16[2,128,2048]{2,1,0:T(8,128)(2,1)S(1)}, u32[]{:S(2)}, u32[]{:S(2)}) collective-permute-start(bf16[2,128,2048]{2,1,0:T(8,128)(2,1)S(1)} %get-tuple-element.136), channel_id=1, source_target_pairs={{0,1},{1,0},{2,3},{3,2},{4,5},{5,4},{6,7},{7,6},{8,9},{9,8},{10,11... | collective-permute-start | bytes 3145736 | tf_op jit(solution)/shard_map/ppermute | solution.py:329
  44.6 15.1 %collective-permute-start.8 = (bf16[2,128,2048]{2,1,0:T(8,128)(2,1)S(1)}, bf16[2,128,2048]{2,1,0:T(8,128)(2,1)S(1)}, u32[]{:S(2)}, u32[]{:S(2)}) collective-permute-start(bf16[2,128,2048]{2,1,0:T(8,128)(2,1)S(1)} %get-tuple-element.135), channel_id=1, source_target_pairs={{0,1},{1,0},{2,3},{3,2},{4,5},{5,4},{6,7},{7,6},{8,9},{9,8},{10,11... | collective-permute-start | bytes 3145736 | tf_op jit(solution)/shard_map/ppermute | solution.py:329
  44.7 8.3 %collective-permute-start.4 = (bf16[2,64,2048]{2,1,0:T(8,128)(2,1)S(1)}, bf16[2,64,2048]{2,1,0:T(8,128)(2,1)S(1)}, u32[]{:S(2)}, u32[]{:S(2)}) collective-permute-start(bf16[2,64,2048]{2,1,0:T(8,128)(2,1)S(1)} %get-tuple-element.100.refs_3_), channel_id=1, source_target_pairs={{0,2},{1,7},{2,4},{3,1},{4,6},{5,3},{6,0},{7,5},{8,10},{9,15},{10,... | collective-permute-start | bytes 1572872 | tf_op jit(solution)/shard_map/ppermute | solution.py:329
  45.9 21.2 %collective-permute-start.6 = (bf16[2,128,2048]{2,1,0:T(8,128)(2,1)S(1)}, bf16[2,128,2048]{2,1,0:T(8,128)(2,1)S(1)}, u32[]{:S(2)}, u32[]{:S(2)}) collective-permute-start(bf16[2,128,2048]{2,1,0:T(8,128)(2,1)S(1)} %get-tuple-element.101.refs_4_), channel_id=1, source_target_pairs={{0,2},{1,7},{2,4},{3,1},{4,6},{5,3},{6,0},{7,5},{8,10},{9,15},{10,... | collective-permute-start | bytes 3145736 | tf_op jit(solution)/shard_map/ppermute | solution.py:329
  46.5 29.0 %collective-permute-start = (bf16[2,128,2048]{2,1,0:T(8,128)(2,1)S(1)}, bf16[2,128,2048]{2,1,0:T(8,128)(2,1)S(1)}, u32[]{:S(2)}, u32[]{:S(2)}) collective-permute-start(bf16[2,128,2048]{2,1,0:T(8,128)(2,1)S(1)} %get-tuple-element.97.refs_2_), channel_id=1, source_target_pairs={{0,2},{1,7},{2,4},{3,1},{4,6},{5,3},{6,0},{7,5},{8,10},{9,15},{10,... | collective-permute-start | bytes 3145736 | tf_op jit(solution)/shard_map/ppermute | solution.py:329
  57.2 10.2 %collective-permute-start.5 = (bf16[2,128,2048]{2,1,0:T(8,128)(2,1)S(1)}, bf16[2,128,2048]{2,1,0:T(8,128)(2,1)S(1)}, u32[]{:S(2)}, u32[]{:S(2)}) collective-permute-start(bf16[2,128,2048]{2,1,0:T(8,128)(2,1)S(1)} %get-tuple-element.134), channel_id=1, source_target_pairs={{0,1},{1,0},{2,3},{3,2},{4,5},{5,4},{6,7},{7,6},{8,9},{9,8},{10,11... | collective-permute-start | bytes 3145736 | tf_op jit(solution)/shard_map/ppermute | solution.py:329
  67.1 10.9 %collective-permute-start.13 = (bf16[2,128,2048]{2,1,0:T(8,128)(2,1)S(1)}, bf16[2,128,2048]{2,1,0:T(8,128)(2,1)S(1)}, u32[]{:S(2)}, u32[]{:S(2)}) collective-permute-start(bf16[2,128,2048]{2,1,0:T(8,128)(2,1)S(1)} %collective-permute-done.6.refs_3_), channel_id=1, source_target_pairs={{0,1},{1,0},{2,3},{3,2},{4,5},{5,4},{6,7},{7,6},{8,9},{9,8},{10,11... | collective-permute-start | bytes 3145736 | tf_op jit(solution)/shard_map/ppermute | solution.py:329
  67.2 19.5 %collective-permute-start.12 = (bf16[2,128,2048]{2,1,0:T(8,128)(2,1)S(1)}, bf16[2,128,2048]{2,1,0:T(8,128)(2,1)S(1)}, u32[]{:S(2)}, u32[]{:S(2)}) collective-permute-start(bf16[2,128,2048]{2,1,0:T(8,128)(2,1)S(1)} %get-tuple-element.99.refs_3_), channel_id=1, source_target_pairs={{0,2},{1,7},{2,4},{3,1},{4,6},{5,3},{6,0},{7,5},{8,10},{9,15},{10,... | collective-permute-start | bytes 3145736 | tf_op jit(solution)/shard_map/ppermute | solution.py:329
  75.5 13.7 %collective-permute-start.15 = (bf16[2,128,2048]{2,1,0:T(8,128)(2,1)S(1)}, bf16[2,128,2048]{2,1,0:T(8,128)(2,1)S(1)}, u32[]{:S(2)}, u32[]{:S(2)}) collective-permute-start(bf16[2,128,2048]{2,1,0:T(8,128)(2,1)S(1)} %collective-permute-done.refs_3_), channel_id=1, source_target_pairs={{0,1},{1,0},{2,3},{3,2},{4,5},{5,4},{6,7},{7,6},{8,9},{9,8},{10,11... | collective-permute-start | bytes 3145736 | tf_op jit(solution)/shard_map/ppermute | solution.py:329
  86.7 9.8 %collective-permute-start.14 = (bf16[2,128,2048]{2,1,0:T(8,128)(2,1)S(1)}, bf16[2,128,2048]{2,1,0:T(8,128)(2,1)S(1)}, u32[]{:S(2)}, u32[]{:S(2)}) collective-permute-start(bf16[2,128,2048]{2,1,0:T(8,128)(2,1)S(1)} %collective-permute-done.12.refs_3_), channel_id=1, source_target_pairs={{0,1},{1,0},{2,3},{3,2},{4,5},{5,4},{6,7},{7,6},{8,9},{9,8},{10,11... | collective-permute-start | bytes 3145736 | tf_op jit(solution)/shard_map/ppermute | solution.py:329
  89.2 13.9 %collective-permute-start.11 = (bf16[2,128,2048]{2,1,0:T(8,128)(2,1)S(1)}, bf16[2,128,2048]{2,1,0:T(8,128)(2,1)S(1)}, u32[]{:S(2)}, u32[]{:S(2)}) collective-permute-start(bf16[2,128,2048]{2,1,0:T(8,128)(2,1)S(1)} %get-tuple-element.136), channel_id=1, source_target_pairs={{0,2},{1,7},{2,4},{3,1},{4,6},{5,3},{6,0},{7,5},{8,10},{9,15},{10,... | collective-permute-start | bytes 3145736 | tf_op jit(solution)/shard_map/ppermute | solution.py:329
  103.1 5.7 %collective-permute-start.16 = (bf16[2,128,2048]{2,1,0:T(8,128)(2,1)S(1)}, bf16[2,128,2048]{2,1,0:T(8,128)(2,1)S(1)}, u32[]{:S(2)}, u32[]{:S(2)}) collective-permute-start(bf16[2,128,2048]{2,1,0:T(8,128)(2,1)S(1)} %collective-permute-done.11.refs_2_), channel_id=1, source_target_pairs={{0,1},{1,0},{2,3},{3,2},{4,5},{5,4},{6,7},{7,6},{8,9},{9,8},{10,11... | collective-permute-start | bytes 3145736 | tf_op jit(solution)/shard_map/ppermute | solution.py:329
  105.2 13.9 %collective-permute-start.10 = (bf16[2,128,2048]{2,1,0:T(8,128)(2,1)S(1)}, bf16[2,128,2048]{2,1,0:T(8,128)(2,1)S(1)}, u32[]{:S(2)}, u32[]{:S(2)}) collective-permute-start(bf16[2,128,2048]{2,1,0:T(8,128)(2,1)S(1)} %get-tuple-element.135), channel_id=1, source_target_pairs={{0,2},{1,7},{2,4},{3,1},{4,6},{5,3},{6,0},{7,5},{8,10},{9,15},{10,... | collective-permute-start | bytes 3145736 | tf_op jit(solution)/shard_map/ppermute | solution.py:329
  119.1 6.1 %collective-permute-start.17 = (bf16[2,128,2048]{2,1,0:T(8,128)(2,1)S(1)}, bf16[2,128,2048]{2,1,0:T(8,128)(2,1)S(1)}, u32[]{:S(2)}, u32[]{:S(2)}) collective-permute-start(bf16[2,128,2048]{2,1,0:T(8,128)(2,1)S(1)} %collective-permute-done.10.refs_2_), channel_id=1, source_target_pairs={{0,1},{1,0},{2,3},{3,2},{4,5},{5,4},{6,7},{7,6},{8,9},{9,8},{10,11... | collective-permute-start | bytes 3145736 | tf_op jit(solution)/shard_map/ppermute | solution.py:329
  121.2 13.9 %collective-permute-start.9 = (bf16[2,128,2048]{2,1,0:T(8,128)(2,1)S(1)}, bf16[2,128,2048]{2,1,0:T(8,128)(2,1)S(1)}, u32[]{:S(2)}, u32[]{:S(2)}) collective-permute-start(bf16[2,128,2048]{2,1,0:T(8,128)(2,1)S(1)} %get-tuple-element.134), channel_id=1, source_target_pairs={{0,2},{1,7},{2,4},{3,1},{4,6},{5,3},{6,0},{7,5},{8,10},{9,15},{10,... | collective-permute-start | bytes 3145736 | tf_op jit(solution)/shard_map/ppermute | solution.py:329
  135.1 5.6 %collective-permute-start.18 = (bf16[2,128,2048]{2,1,0:T(8,128)(2,1)S(1)}, bf16[2,128,2048]{2,1,0:T(8,128)(2,1)S(1)}, u32[]{:S(2)}, u32[]{:S(2)}) collective-permute-start(bf16[2,128,2048]{2,1,0:T(8,128)(2,1)S(1)} %collective-permute-done.9.refs_2_), channel_id=1, source_target_pairs={{0,1},{1,0},{2,3},{3,2},{4,5},{5,4},{6,7},{7,6},{8,9},{9,8},{10,11... | collective-permute-start | bytes 3145736 | tf_op jit(solution)/shard_map/ppermute | solution.py:329

commit v7 on v6

--- a/solution.py
+++ b/solution.py
@@ -60,16 +60,16 @@
 def first_kernel(skip, x_ref, scale_ref, y_ref, xbuf, scale_buf, sem, scale_sem):
     n = y_ref.shape[0]
     start = lax.rem(lax.axis_index("tp"), 2) * (x_ref.shape[0] // 2) + skip
-    load = lambda i: pltpu.make_async_copy(x_ref.at[pl.ds(start + i, 1)], xbuf.at[pl.ds(i, 1)], sem.at[i])
+    load = lambda i: pltpu.make_async_copy(x_ref.at[pl.ds(start + i, PIECE)], xbuf.at[pl.ds(i, PIECE)], sem.at[i])
     get_scale = pltpu.make_async_copy(scale_ref, scale_buf, scale_sem)
     get_scale.start()
-    for i in range(n):
+    for i in range(0, n, PIECE):
         load(i).start()
     get_scale.wait()
     scale = scale_buf[...].astype(jnp.float32).reshape(1, -1)
-    for i in range(n):
+    for i in range(0, n, PIECE):
         load(i).wait()
-        y_ref[i] = rms_norm(xbuf[i], scale)
+        y_ref[i:i + PIECE] = rms_norm(xbuf[i:i + PIECE], scale)
 
 
 def normalize_first(x, scale, skip, n):
@@ -356,8 +356,7 @@
         state["carry"] = (stage, tuple((PIECE, *own(i)) for i in range(2)), tuple(range(stage.shape[0])))
         nz = [send(v, ring) for v in other]
         n3 = send(slots[0], ring)
-        run([[((yb, other[1], PIECE, 0), *own(2)), (slots[0], *own(3))]], keep_joined=False)
-        run([[(slots[1], *own(4)), (slots[2], *own(5))]])
+        run([[((yb, other[1], PIECE, 0), *own(2)), (slots[0], *own(3))], [(slots[1], *own(4)), (slots[2], *own(5))]], keep_joined=False)
 
         LEFT, RIGHT = chips - 1, 1
         near = lambda i: ((LEFT, seq(i)), (RIGHT, seq(i + h)))

time: 146 us -> 146 us (level)
    pallas_call x15 -> x14, Pallas kernels: 83.5 us -> 83.3 us  [project(): pl.pallas_call(functools.partial(project_kernel, plan, tuple(sources), le...]
  transfers between devices with their start and end apart: 19 -> 19, of which waited for: 6 -> 6; matrix products, arithmetic and copies ran while one was open for 0% -> 0% of each run, Pallas kernels for 59% -> 58%
where the time goes in v7:
time: 146 us
  Pallas kernels  98.4 us (67%)
  waiting for transfers between devices  23.7 us (16%)
  starting transfers between devices  22.4 us (15%)
    pallas_call x14, Pallas kernels, project(): pl.pallas_call(functools.partial(project_kernel, plan, tuple(sources), le...  83.3 us
    ppermute x19, waiting for transfers between devices, send(): return lax.ppermute(v, 'tp', perm)  23.7 us
    ppermute x19, starting transfers between devices, send(): return lax.ppermute(v, 'tp', perm)  22.4 us
    pallas_call x1, Pallas kernels, prepare(): pl.pallas_call(functools.partial(second_kernel, n_slots), out_shape=out_s...  12.2 us
  transfers between devices with their start and end apart: 19, of which 6 were waited for; matrix products, arithmetic and copies ran while one was open for 0% of the time, Pallas kernels for 58%

profile of v7, /device:TPU:81, one launch (start us, length us, event | category | flops | bytes accessed | tf_op | source)
XLA Modules:
  0.0 145.6 jit_solution(14090503956500135071)
XLA Ops:
  1.9 3.8 %collective-permute-start.1 = (bf16[2,64,2048]{2,1,0:T(8,128)(2,1)S(1)}, bf16[2,64,2048]{2,1,0:T(8,128)(2,1)S(1)}, u32[]{:S(2)}, u32[]{:S(2)}) collective-permute-start(bf16[2,64,2048]{2,1,0:T(8,128)(2,1)S(1)} %shard_map.59.y_first), channel_id=1, source_target_pairs={{0,2},{1,7},{2,4},{3,1},{4,6},{5,3},{6,0},{7,5},{8,10},{9,15},{10,... | collective-permute-start | bytes 1572872 | tf_op jit(solution)/shard_map/ppermute | solution.py:329
  7.8 12.2 %prep2.1 = (bf16[4,64,2048]{2,1,0:T(8,128)(2,1)S(1)}, bf16[2,64,2048]{2,1,0:T(8,128)(2,1)S(1)}, bf16[2,128,2048]{2,1,0:T(8,128)(2,1)S(1)}, bf16[2,128,2048]{2,1,...) custom-call(bf16[12,64,2048]{2,1,0:T(8,128)(2,1)} %x_ref.5, ...), custom_call_target="tpu_custom_call" | custom-call | flops 100663296 | bytes 6291456 | tf_op jit(solution)/shard_map/prep2/pallas_call | solution.py:193
  21.5 14.6 %shard_map.61 = (bf16[6,12,256,512]{3,2,1,0:T(8,128)(2,1)}, bf16[6,12,256,512]{3,2,1,0:T(8,128)(2,1)}, bf16[3,2,2,4,256,128]{5,4,3,2,1,0:T(8,128)(2,1)S(1)}) custom-call(bf16[6,256,2048]{2,1,0:T(8,128)(2,1)S(1)} %get-tuple-element.92.refs_0_, bf16[6,256,2048]{2,1,0:T(8,128)(2,1)S(1)} %get-tuple-element.93.refs_1_, ...), custom_call_target="tpu_custom_call" | custom-call | flops 12884901888 | bytes 10485760 | tf_op jit(solution)/shard_map/pallas_call | solution.py:300
  36.1 7.6 %shard_map.62 = (bf16[6,12,256,512]{3,2,1,0:T(8,128)(2,1)}, bf16[6,12,256,512]{3,2,1,0:T(8,128)(2,1)}, bf16[3,2,2,4,256,128]{5,4,3,2,1,0:T(8,128)(2,1)S(1)}, bf1...) custom-call(bf16[6,256,2048]{2,1,0:T(8,128)(2,1)S(1)} %get-tuple-element.92.r, ...), custom_call_target="tpu_custom_call", output_to_operand_aliasing={{0}: (7, {}), {1}: (8, {})} | custom-call | flops 6442450944 | bytes 5242880 | tf_op jit(solution)/shard_map/pallas_call | solution.py:300
  46.5 6.5 %collective-permute-done.4.refs_3_ = bf16[2,64,2048]{2,1,0:T(8,128)(2,1)S(1)} collective-permute-done((bf16[2,64,2048]{2,1,0:T(8,128)(2,1)S(1)}, bf16[2,64,2048]{2,1,0:T(8,128)(2,1)S(1)}, u32[]{:S(2)}, u32[]{:S(2)}) %collective-permute-start.4) | collective-permute-done | bytes 524320 | tf_op jit(solution)/shard_map/ppermute | solution.py:329
  53.0 4.1 %shard_map.63 = (bf16[6,12,256,512]{3,2,1,0:T(8,128)(2,1)}, bf16[6,12,256,512]{3,2,1,0:T(8,128)(2,1)}, bf16[3,2,2,2,256,128]{5,4,3,2,1,0:T(8,128)(2,1)S(1)}, bf16[2,128,2048]{2,1,0:T(8,128)(2,1)S(1)}) custom-call(bf16[6,256,2048]{2,1,0:T(8,128)(2,1)S(1)} %get-tuple-element.92.refs_0_, ...), custom_call_target="tpu_custom_call", output_to_operand_aliasing={{0}: (5, {}), {1}: (6, {})} | custom-call | flops 3221225472 | bytes 2621440 | tf_op jit(solution)/shard_map/pallas_call | solution.py:300
  57.1 2.6 %collective-permute-start.5 = (bf16[2,128,2048]{2,1,0:T(8,128)(2,1)S(1)}, bf16[2,128,2048]{2,1,0:T(8,128)(2,1)S(1)}, u32[]{:S(2)}, u32[]{:S(2)}) collective-permute-start(bf16[2,128,2048]{2,1,0:T(8,128)(2,1)S(1)} %get-tuple-element.128), channel_id=1, source_target_pairs={{0,1},{1,0},{2,3},{3,2},{4,5},{5,4},{6,7},{7,6},{8,9},{9,8},{10,11... | collective-permute-start | bytes 3145736 | tf_op jit(solution)/shard_map/ppermute | solution.py:329
  59.7 7.3 %shard_map.64 = (bf16[6,12,256,512]{3,2,1,0:T(8,128)(2,1)}, bf16[6,12,256,512]{3,2,1,0:T(8,128)(2,1)}, bf16[3,2,2,4,256,128]{5,4,3,2,1,0:T(8,128)(2,1)S(1)}) custom-call(bf16[6,256,2048]{2,1,0:T(8,128)(2,1)S(1)} %get-tuple-element.92.refs_0_, bf16[6,256,2048]{2,1,0:T(8,128)(2,1)S(1)} %get-tuple-element.93.refs_1_, ...), custom_call_target="tpu_custom_call", output_to_operand_aliasing={{0}: (5, {}), {1}: (6, {})} | custom-call | flops 6442450944 | bytes 5242880 | tf_op jit(solution)/shard_map/pallas_call | solution.py:300
  67.3 7.4 %shard_map.65 = (bf16[6,12,256,512]{3,2,1,0:T(8,128)(2,1)}, bf16[6,12,256,512]{3,2,1,0:T(8,128)(2,1)}, bf16[3,2,2,4,256,128]{5,4,3,2,1,0:T(8,128)(2,1)S(1)}) custom-call(bf16[6,256,2048]{2,1,0:T(8,128)(2,1)S(1)} %get-tuple-element.92.refs_0_, bf16[6,256,2048]{2,1,0:T(8,128)(2,1)S(1)} %get-tuple-element.93.refs_1_, ...), custom_call_target="tpu_custom_call", output_to_operand_aliasing={{0}: (5, {}), {1}: (6, {})} | custom-call | flops 6442450944 | bytes 5242880 | tf_op jit(solution)/shard_map/pallas_call | solution.py:300
  75.5 2.5 %collective-permute-start.15 = (bf16[2,128,2048]{2,1,0:T(8,128)(2,1)S(1)}, bf16[2,128,2048]{2,1,0:T(8,128)(2,1)S(1)}, u32[]{:S(2)}, u32[]{:S(2)}) collective-permute-start(bf16[2,128,2048]{2,1,0:T(8,128)(2,1)S(1)} %collective-permute-done.refs_3_), channel_id=1, source_target_pairs={{0,1},{1,0},{2,3},{3,2},{4,5},{5,4},{6,7},{7,6},{8,9},{9,8},{10,11... | collective-permute-start | bytes 3145736 | tf_op jit(solution)/shard_map/ppermute | solution.py:329
  77.9 7.4 %shard_map.66 = (bf16[6,12,256,512]{3,2,1,0:T(8,128)(2,1)}, bf16[6,12,256,512]{3,2,1,0:T(8,128)(2,1)}, bf16[3,2,2,4,256,128]{5,4,3,2,1,0:T(8,128)(2,1)S(1)}) custom-call(bf16[6,256,2048]{2,1,0:T(8,128)(2,1)S(1)} %get-tuple-element.92.refs_0_, bf16[6,256,2048]{2,1,0:T(8,128)(2,1)S(1)} %get-tuple-element.93.refs_1_, ...), custom_call_target="tpu_custom_call", output_to_operand_aliasing={{0}: (5, {}), {1}: (6, {})} | custom-call | flops 6442450944 | bytes 5242880 | tf_op jit(solution)/shard_map/pallas_call | solution.py:300
  86.7 2.5 %collective-permute-start.14 = (bf16[2,128,2048]{2,1,0:T(8,128)(2,1)S(1)}, bf16[2,128,2048]{2,1,0:T(8,128)(2,1)S(1)}, u32[]{:S(2)}, u32[]{:S(2)}) collective-permute-start(bf16[2,128,2048]{2,1,0:T(8,128)(2,1)S(1)} %collective-permute-done.12.refs_3_), channel_id=1, source_target_pairs={{0,1},{1,0},{2,3},{3,2},{4,5},{5,4},{6,7},{7,6},{8,9},{9,8},{10,11... | collective-permute-start | bytes 3145736 | tf_op jit(solution)/shard_map/ppermute | solution.py:329
  89.2 7.4 %shard_map.67 = (bf16[6,12,256,512]{3,2,1,0:T(8,128)(2,1)}, bf16[6,12,256,512]{3,2,1,0:T(8,128)(2,1)}, bf16[3,2,2,4,256,128]{5,4,3,2,1,0:T(8,128)(2,1)S(1)}) custom-call(bf16[6,256,2048]{2,1,0:T(8,128)(2,1)S(1)} %get-tuple-element.92.refs_0_, bf16[6,256,2048]{2,1,0:T(8,128)(2,1)S(1)} %get-tuple-element.93.refs_1_, ...), custom_call_target="tpu_custom_call", output_to_operand_aliasing={{0}: (5, {}), {1}: (6, {})} | custom-call | flops 6442450944 | bytes 5242880 | tf_op jit(solution)/shard_map/pallas_call | solution.py:300
  96.6 3.7 %shard_map.68 = (bf16[6,12,256,512]{3,2,1,0:T(8,128)(2,1)}, bf16[6,12,256,512]{3,2,1,0:T(8,128)(2,1)}, bf16[3,2,2,2,256,128]{5,4,3,2,1,0:T(8,128)(2,1)S(1)}) custom-call(bf16[6,256,2048]{2,1,0:T(8,128)(2,1)S(1)} %get-tuple-element.92.refs_0_, bf16[6,256,2048]{2,1,0:T(8,128)(2,1)S(1)} %get-tuple-element.93.refs_1_, ...), custom_call_target="tpu_custom_call", output_to_operand_aliasing={{0}: (4, {}), {1}: (5, {})} | custom-call | flops 3221225472 | bytes 2621440 | tf_op jit(solution)/shard_map/pallas_call | solution.py:300
  100.2 2.9 %collective-permute-done.11.refs_2_ = bf16[2,128,2048]{2,1,0:T(8,128)(2,1)S(1)} collective-permute-done((bf16[2,128,2048]{2,1,0:T(8,128)(2,1)S(1)}, bf16[2,128,2048]{2,1,0:T(8,128)(2,1)S(1)}, u32[]{:S(2)}, u32[]{:S(2)}) %collective-permute-start.11) | collective-permute-done | bytes 1048608 | tf_op jit(solution)/shard_map/ppermute | solution.py:329
  103.1 2.1 %collective-permute-start.16 = (bf16[2,128,2048]{2,1,0:T(8,128)(2,1)S(1)}, bf16[2,128,2048]{2,1,0:T(8,128)(2,1)S(1)}, u32[]{:S(2)}, u32[]{:S(2)}) collective-permute-start(bf16[2,128,2048]{2,1,0:T(8,128)(2,1)S(1)} %collective-permute-done.11.refs_2_), channel_id=1, source_target_pairs={{0,1},{1,0},{2,3},{3,2},{4,5},{5,4},{6,7},{7,6},{8,9},{9,8},{10,11... | collective-permute-start | bytes 3145736 | tf_op jit(solution)/shard_map/ppermute | solution.py:329
  105.2 3.6 %shard_map.69 = (bf16[6,12,256,512]{3,2,1,0:T(8,128)(2,1)}, bf16[6,12,256,512]{3,2,1,0:T(8,128)(2,1)}, bf16[3,2,2,2,256,128]{5,4,3,2,1,0:T(8,128)(2,1)S(1)}) custom-call(bf16[6,256,2048]{2,1,0:T(8,128)(2,1)S(1)} %get-tuple-element.92.refs_0_, bf16[6,256,2048]{2,1,0:T(8,128)(2,1)S(1)} %get-tuple-element.93.refs_1_, ...), custom_call_target="tpu_custom_call", output_to_operand_aliasing={{0}: (4, {}), {1}: (5, {})} | custom-call | flops 3221225472 | bytes 2621440 | tf_op jit(solution)/shard_map/pallas_call | solution.py:300
  108.8 4.0 %shard_map.70 = (bf16[6,12,256,512]{3,2,1,0:T(8,128)(2,1)}, bf16[6,12,256,512]{3,2,1,0:T(8,128)(2,1)}, bf16[3,2,2,2,256,128]{5,4,3,2,1,0:T(8,128)(2,1)S(1)}) custom-call(bf16[6,256,2048]{2,1,0:T(8,128)(2,1)S(1)} %get-tuple-element.92.refs_0_, bf16[6,256,2048]{2,1,0:T(8,128)(2,1)S(1)} %get-tuple-element.93.refs_1_, ...), custom_call_target="tpu_custom_call", output_to_operand_aliasing={{0}: (4, {}), {1}: (5, {})} | custom-call | flops 3221225472 | bytes 2621440 | tf_op jit(solution)/shard_map/pallas_call | solution.py:300
  112.8 6.3 %collective-permute-done.10.refs_2_ = bf16[2,128,2048]{2,1,0:T(8,128)(2,1)S(1)} collective-permute-done((bf16[2,128,2048]{2,1,0:T(8,128)(2,1)S(1)}, bf16[2,128,2048]{2,1,0:T(8,128)(2,1)S(1)}, u32[]{:S(2)}, u32[]{:S(2)}) %collective-permute-start.10) | collective-permute-done | bytes 1048608 | tf_op jit(solution)/shard_map/ppermute | solution.py:329
  121.2 4.0 %shard_map.71 = (bf16[6,12,256,512]{3,2,1,0:T(8,128)(2,1)}, bf16[6,12,256,512]{3,2,1,0:T(8,128)(2,1)}, bf16[3,2,2,2,256,128]{5,4,3,2,1,0:T(8,128)(2,1)S(1)}) custom-call(bf16[6,256,2048]{2,1,0:T(8,128)(2,1)S(1)} %get-tuple-element.92.refs_0_, bf16[6,256,2048]{2,1,0:T(8,128)(2,1)S(1)} %get-tuple-element.93.refs_1_, ...), custom_call_target="tpu_custom_call", output_to_operand_aliasing={{0}: (4, {}), {1}: (5, {})} | custom-call | flops 3221225472 | bytes 2621440 | tf_op jit(solution)/shard_map/pallas_call | solution.py:300
  125.2 4.0 %shard_map.72 = (bf16[6,12,256,512]{3,2,1,0:T(8,128)(2,1)}, bf16[6,12,256,512]{3,2,1,0:T(8,128)(2,1)}, bf16[3,2,2,2,256,128]{5,4,3,2,1,0:T(8,128)(2,1)S(1)}) custom-call(bf16[6,256,2048]{2,1,0:T(8,128)(2,1)S(1)} %get-tuple-element.92.refs_0_, bf16[6,256,2048]{2,1,0:T(8,128)(2,1)S(1)} %get-tuple-element.93.refs_1_, ...), custom_call_target="tpu_custom_call", output_to_operand_aliasing={{0}: (4, {}), {1}: (5, {})} | custom-call | flops 3221225472 | bytes 2621440 | tf_op jit(solution)/shard_map/pallas_call | solution.py:300
  129.2 5.9 %collective-permute-done.9.refs_2_ = bf16[2,128,2048]{2,1,0:T(8,128)(2,1)S(1)} collective-permute-done((bf16[2,128,2048]{2,1,0:T(8,128)(2,1)S(1)}, bf16[2,128,2048]{2,1,0:T(8,128)(2,1)S(1)}, u32[]{:S(2)}, u32[]{:S(2)}) %collective-permute-start.9) | collective-permute-done | bytes 1048608 | tf_op jit(solution)/shard_map/ppermute | solution.py:329
  137.2 3.6 %shard_map.73 = (bf16[6,12,256,512]{3,2,1,0:T(8,128)(2,1)}, bf16[6,12,256,512]{3,2,1,0:T(8,128)(2,1)}, bf16[3,2,2,2,256,128]{5,4,3,2,1,0:T(8,128)(2,1)S(1)}) custom-call(bf16[6,256,2048]{2,1,0:T(8,128)(2,1)S(1)} %get-tuple-element.92.refs_0_, bf16[6,256,2048]{2,1,0:T(8,128)(2,1)S(1)} %get-tuple-element.93.refs_1_, ...), custom_call_target="tpu_custom_call", output_to_operand_aliasing={{0}: (4, {}), {1}: (5, {})} | custom-call | flops 3221225472 | bytes 2621440 | tf_op jit(solution)/shard_map/pallas_call | solution.py:300
  140.8 4.6 %shard_map.74 = (bf16[6,12,256,512]{3,2,1,0:T(8,128)(2,1)}, bf16[6,12,256,512]{3,2,1,0:T(8,128)(2,1)}) custom-call(bf16[6,256,2048]{2,1,0:T(8,128)(2,1)S(1)} %get-tuple-element.92.refs_0_, bf16[6,256,2048]{2,1,0:T(8,128)(2,1)S(1)} %get-tuple-element.93.refs_1_, ...), custom_call_target="tpu_custom_call", output_to_operand_aliasing={{0}: (4, {}), {1}: (5, {})} | custom-call | flops 3221225472 | bytes 2621440 | tf_op jit(solution)/shard_map/pallas_call | solution.py:300
  (31 shorter events, 14.1 us)
Async XLA Ops:
  1.9 34.1 %collective-permute-start.1 = (bf16[2,64,2048]{2,1,0:T(8,128)(2,1)S(1)}, bf16[2,64,2048]{2,1,0:T(8,128)(2,1)S(1)}, u32[]{:S(2)}, u32[]{:S(2)}) collective-permute-start(bf16[2,64,2048]{2,1,0:T(8,128)(2,1)S(1)} %shard_map.59.y_first), channel_id=1, source_target_pairs={{0,2},{1,7},{2,4},{3,1},{4,6},{5,3},{6,0},{7,5},{8,10},{9,15},{10,... | collective-permute-start | bytes 1572872 | tf_op jit(solution)/shard_map/ppermute | solution.py:329
  7.3 28.8 %collective-permute-start.2 = (bf16[4,64,2048]{2,1,0:T(8,128)(2,1)S(1)}, bf16[4,64,2048]{2,1,0:T(8,128)(2,1)S(1)}, u32[]{:S(2)}, u32[]{:S(2)}) collective-permute-start(bf16[4,64,2048]{2,1,0:T(8,128)(2,1)S(1)} %shard_map.60.y_rest.refs_2_), channel_id=1, source_target_pairs={{0,2},{1,7},{2,4},{3,1},{4,6},{5,3},{6,0},{7,5},{8,10},{9,15},{10,... | collective-permute-start | bytes 3145736 | tf_op jit(solution)/shard_map/ppermute | solution.py:329
  20.0 16.1 %collective-permute-start.3 = (bf16[4,64,2048]{2,1,0:T(8,128)(2,1)S(1)}, bf16[4,64,2048]{2,1,0:T(8,128)(2,1)S(1)}, u32[]{:S(2)}, u32[]{:S(2)}) collective-permute-start(bf16[4,64,2048]{2,1,0:T(8,128)(2,1)S(1)} %get-tuple-element.95), channel_id=1, source_target_pairs={{0,2},{1,7},{2,4},{3,1},{4,6},{5,3},{6,0},{7,5},{8,10},{9,15},{10,... | collective-permute-start | bytes 3145736 | tf_op jit(solution)/shard_map/ppermute | solution.py:329
  43.7 16.0 %collective-permute-start.7 = (bf16[2,128,2048]{2,1,0:T(8,128)(2,1)S(1)}, bf16[2,128,2048]{2,1,0:T(8,128)(2,1)S(1)}, u32[]{:S(2)}, u32[]{:S(2)}) collective-permute-start(bf16[2,128,2048]{2,1,0:T(8,128)(2,1)S(1)} %get-tuple-element.130), channel_id=1, source_target_pairs={{0,1},{1,0},{2,3},{3,2},{4,5},{5,4},{6,7},{7,6},{8,9},{9,8},{10,11... | collective-permute-start | bytes 3145736 | tf_op jit(solution)/shard_map/ppermute | solution.py:329
  44.5 15.2 %collective-permute-start.8 = (bf16[2,128,2048]{2,1,0:T(8,128)(2,1)S(1)}, bf16[2,128,2048]{2,1,0:T(8,128)(2,1)S(1)}, u32[]{:S(2)}, u32[]{:S(2)}) collective-permute-start(bf16[2,128,2048]{2,1,0:T(8,128)(2,1)S(1)} %get-tuple-element.129), channel_id=1, source_target_pairs={{0,1},{1,0},{2,3},{3,2},{4,5},{5,4},{6,7},{7,6},{8,9},{9,8},{10,11... | collective-permute-start | bytes 3145736 | tf_op jit(solution)/shard_map/ppermute | solution.py:329
  44.7 8.3 %collective-permute-start.4 = (bf16[2,64,2048]{2,1,0:T(8,128)(2,1)S(1)}, bf16[2,64,2048]{2,1,0:T(8,128)(2,1)S(1)}, u32[]{:S(2)}, u32[]{:S(2)}) collective-permute-start(bf16[2,64,2048]{2,1,0:T(8,128)(2,1)S(1)} %get-tuple-element.96.refs_3_), channel_id=1, source_target_pairs={{0,2},{1,7},{2,4},{3,1},{4,6},{5,3},{6,0},{7,5},{8,10},{9,15},{10,... | collective-permute-start | bytes 1572872 | tf_op jit(solution)/shard_map/ppermute | solution.py:329
  45.7 21.3 %collective-permute-start.6 = (bf16[2,128,2048]{2,1,0:T(8,128)(2,1)S(1)}, bf16[2,128,2048]{2,1,0:T(8,128)(2,1)S(1)}, u32[]{:S(2)}, u32[]{:S(2)}) collective-permute-start(bf16[2,128,2048]{2,1,0:T(8,128)(2,1)S(1)} %get-tuple-element.97.refs_4_), channel_id=1, source_target_pairs={{0,2},{1,7},{2,4},{3,1},{4,6},{5,3},{6,0},{7,5},{8,10},{9,15},{10,... | collective-permute-start | bytes 3145736 | tf_op jit(solution)/shard_map/ppermute | solution.py:329
  46.2 29.3 %collective-permute-start = (bf16[2,128,2048]{2,1,0:T(8,128)(2,1)S(1)}, bf16[2,128,2048]{2,1,0:T(8,128)(2,1)S(1)}, u32[]{:S(2)}, u32[]{:S(2)}) collective-permute-start(bf16[2,128,2048]{2,1,0:T(8,128)(2,1)S(1)} %get-tuple-element.94.refs_5_), channel_id=1, source_target_pairs={{0,2},{1,7},{2,4},{3,1},{4,6},{5,3},{6,0},{7,5},{8,10},{9,15},{10,... | collective-permute-start | bytes 3145736 | tf_op jit(solution)/shard_map/ppermute | solution.py:329
  57.1 10.2 %collective-permute-start.5 = (bf16[2,128,2048]{2,1,0:T(8,128)(2,1)S(1)}, bf16[2,128,2048]{2,1,0:T(8,128)(2,1)S(1)}, u32[]{:S(2)}, u32[]{:S(2)}) collective-permute-start(bf16[2,128,2048]{2,1,0:T(8,128)(2,1)S(1)} %get-tuple-element.128), channel_id=1, source_target_pairs={{0,1},{1,0},{2,3},{3,2},{4,5},{5,4},{6,7},{7,6},{8,9},{9,8},{10,11... | collective-permute-start | bytes 3145736 | tf_op jit(solution)/shard_map/ppermute | solution.py:329
  67.1 10.9 %collective-permute-start.13 = (bf16[2,128,2048]{2,1,0:T(8,128)(2,1)S(1)}, bf16[2,128,2048]{2,1,0:T(8,128)(2,1)S(1)}, u32[]{:S(2)}, u32[]{:S(2)}) collective-permute-start(bf16[2,128,2048]{2,1,0:T(8,128)(2,1)S(1)} %collective-permute-done.6.refs_3_), channel_id=1, source_target_pairs={{0,1},{1,0},{2,3},{3,2},{4,5},{5,4},{6,7},{7,6},{8,9},{9,8},{10,11... | collective-permute-start | bytes 3145736 | tf_op jit(solution)/shard_map/ppermute | solution.py:329
  67.2 19.5 %collective-permute-start.12 = (bf16[2,128,2048]{2,1,0:T(8,128)(2,1)S(1)}, bf16[2,128,2048]{2,1,0:T(8,128)(2,1)S(1)}, u32[]{:S(2)}, u32[]{:S(2)}) collective-permute-start(bf16[2,128,2048]{2,1,0:T(8,128)(2,1)S(1)} %get-tuple-element.98.refs_6_), channel_id=1, source_target_pairs={{0,2},{1,7},{2,4},{3,1},{4,6},{5,3},{6,0},{7,5},{8,10},{9,15},{10,... | collective-permute-start | bytes 3145736 | tf_op jit(solution)/shard_map/ppermute | solution.py:329
  75.5 13.7 %collective-permute-start.15 = (bf16[2,128,2048]{2,1,0:T(8,128)(2,1)S(1)}, bf16[2,128,2048]{2,1,0:T(8,128)(2,1)S(1)}, u32[]{:S(2)}, u32[]{:S(2)}) collective-permute-start(bf16[2,128,2048]{2,1,0:T(8,128)(2,1)S(1)} %collective-permute-done.refs_3_), channel_id=1, source_target_pairs={{0,1},{1,0},{2,3},{3,2},{4,5},{5,4},{6,7},{7,6},{8,9},{9,8},{10,11... | collective-permute-start | bytes 3145736 | tf_op jit(solution)/shard_map/ppermute | solution.py:329
  86.7 9.8 %collective-permute-start.14 = (bf16[2,128,2048]{2,1,0:T(8,128)(2,1)S(1)}, bf16[2,128,2048]{2,1,0:T(8,128)(2,1)S(1)}, u32[]{:S(2)}, u32[]{:S(2)}) collective-permute-start(bf16[2,128,2048]{2,1,0:T(8,128)(2,1)S(1)} %collective-permute-done.12.refs_3_), channel_id=1, source_target_pairs={{0,1},{1,0},{2,3},{3,2},{4,5},{5,4},{6,7},{7,6},{8,9},{9,8},{10,11... | collective-permute-start | bytes 3145736 | tf_op jit(solution)/shard_map/ppermute | solution.py:329
  89.2 13.9 %collective-permute-start.11 = (bf16[2,128,2048]{2,1,0:T(8,128)(2,1)S(1)}, bf16[2,128,2048]{2,1,0:T(8,128)(2,1)S(1)}, u32[]{:S(2)}, u32[]{:S(2)}) collective-permute-start(bf16[2,128,2048]{2,1,0:T(8,128)(2,1)S(1)} %get-tuple-element.130), channel_id=1, source_target_pairs={{0,2},{1,7},{2,4},{3,1},{4,6},{5,3},{6,0},{7,5},{8,10},{9,15},{10,... | collective-permute-start | bytes 3145736 | tf_op jit(solution)/shard_map/ppermute | solution.py:329
  103.1 5.7 %collective-permute-start.16 = (bf16[2,128,2048]{2,1,0:T(8,128)(2,1)S(1)}, bf16[2,128,2048]{2,1,0:T(8,128)(2,1)S(1)}, u32[]{:S(2)}, u32[]{:S(2)}) collective-permute-start(bf16[2,128,2048]{2,1,0:T(8,128)(2,1)S(1)} %collective-permute-done.11.refs_2_), channel_id=1, source_target_pairs={{0,1},{1,0},{2,3},{3,2},{4,5},{5,4},{6,7},{7,6},{8,9},{9,8},{10,11... | collective-permute-start | bytes 3145736 | tf_op jit(solution)/shard_map/ppermute | solution.py:329
  105.2 13.9 %collective-permute-start.10 = (bf16[2,128,2048]{2,1,0:T(8,128)(2,1)S(1)}, bf16[2,128,2048]{2,1,0:T(8,128)(2,1)S(1)}, u32[]{:S(2)}, u32[]{:S(2)}) collective-permute-start(bf16[2,128,2048]{2,1,0:T(8,128)(2,1)S(1)} %get-tuple-element.129), channel_id=1, source_target_pairs={{0,2},{1,7},{2,4},{3,1},{4,6},{5,3},{6,0},{7,5},{8,10},{9,15},{10,... | collective-permute-start | bytes 3145736 | tf_op jit(solution)/shard_map/ppermute | solution.py:329
  119.1 6.1 %collective-permute-start.17 = (bf16[2,128,2048]{2,1,0:T(8,128)(2,1)S(1)}, bf16[2,128,2048]{2,1,0:T(8,128)(2,1)S(1)}, u32[]{:S(2)}, u32[]{:S(2)}) collective-permute-start(bf16[2,128,2048]{2,1,0:T(8,128)(2,1)S(1)} %collective-permute-done.10.refs_2_), channel_id=1, source_target_pairs={{0,1},{1,0},{2,3},{3,2},{4,5},{5,4},{6,7},{7,6},{8,9},{9,8},{10,11... | collective-permute-start | bytes 3145736 | tf_op jit(solution)/shard_map/ppermute | solution.py:329
  121.2 13.9 %collective-permute-start.9 = (bf16[2,128,2048]{2,1,0:T(8,128)(2,1)S(1)}, bf16[2,128,2048]{2,1,0:T(8,128)(2,1)S(1)}, u32[]{:S(2)}, u32[]{:S(2)}) collective-permute-start(bf16[2,128,2048]{2,1,0:T(8,128)(2,1)S(1)} %get-tuple-element.128), channel_id=1, source_target_pairs={{0,2},{1,7},{2,4},{3,1},{4,6},{5,3},{6,0},{7,5},{8,10},{9,15},{10,... | collective-permute-start | bytes 3145736 | tf_op jit(solution)/shard_map/ppermute | solution.py:329
  135.1 5.7 %collective-permute-start.18 = (bf16[2,128,2048]{2,1,0:T(8,128)(2,1)S(1)}, bf16[2,128,2048]{2,1,0:T(8,128)(2,1)S(1)}, u32[]{:S(2)}, u32[]{:S(2)}) collective-permute-start(bf16[2,128,2048]{2,1,0:T(8,128)(2,1)S(1)} %collective-permute-done.9.refs_2_), channel_id=1, source_target_pairs={{0,1},{1,0},{2,3},{3,2},{4,5},{5,4},{6,7},{7,6},{8,9},{9,8},{10,11... | collective-permute-start | bytes 3145736 | tf_op jit(solution)/shard_map/ppermute | solution.py:329
